TPU v7x, 8 devices: a whole 2x2x1 slice. The times are simulated.
8 devices in a mesh: dp: 1 (over z), fsdp: 8 (over y, x, core).
Axes of the slice: x: 2, y: 2, z: 1, core: 2. Of those that a mesh axis runs over, the one named last changes fastest.
Arguments:
- tok_ids: int32 [48, 384], P(('dp', 'fsdp'))
- grad_out: bfloat16 [48, 384, 2048], P(('dp', 'fsdp'))
- emb_table: bfloat16 [163840, 2048], P('fsdp')
- norm_gain: bfloat16 [2048], P('fsdp')
- w_query: bfloat16 [2048, 3072], P('fsdp')
- w_kv_down: bfloat16 [2048, 576], P('fsdp')
- kv_gain: bfloat16 [512], P('fsdp')
- w_kv_up: bfloat16 [512, 4096], P('fsdp')
- w_out: bfloat16 [2048, 2048], P('fsdp')
Outputs:
- output 1: bfloat16 [48, 384, 2048], P(('dp', 'fsdp'))
- output 2: bfloat16 [163840, 2048], P(('dp', 'fsdp'))
- output 3: float32 [2048], P(('dp', 'fsdp'))
- output 4: float32 [2048, 3072], P(('dp', 'fsdp'))
- output 5: float32 [2048, 576], P(('dp', 'fsdp'))
- output 6: float32 [512], P(('dp', 'fsdp'))
- output 7: float32 [512, 4096], P(('dp', 'fsdp'))
- output 8: float32 [2048, 2048], P(('dp', 'fsdp'))
All inputs are finite; a program needn't handle non-finite values.
Results may differ from a plain program's by a relative error of at most 0.011954.
Values are sent between devices in bfloat16 or wider.
A program may use at most 1 GiB of HBM per device.

v0:
```python
import math
import jax
import jax.numpy as jnp
from jax import lax
from jax.sharding import PartitionSpec as P

NOPE_DIM = 128
ROPE_DIM = 64
VALUE_DIM = 128
ROPE_THETA = 50000.0
RMS_EPS = 1e-6
ATTN_SCALE = (NOPE_DIM + ROPE_DIM) ** -0.5 * (0.1 * math.log(32.0) + 1.0) ** 2
ROW_DIMS = (((0,), (0,)), ((), ()))
COL_DIMS = (((1,), (1,)), ((), ()))


def rms_scale(in_vals, gain_vec):
    vals_f32 = in_vals.astype(jnp.float32)
    inv_rms = lax.rsqrt(jnp.mean(vals_f32 * vals_f32, axis=-1, keepdims=True) + RMS_EPS)
    return (vals_f32 * inv_rms * gain_vec).astype(jnp.bfloat16)


def rope_tables(seq_len):
    positions = jnp.arange(seq_len, dtype=jnp.float32)
    inv_freq = ROPE_THETA ** (-2.0 * jnp.arange(ROPE_DIM // 2, dtype=jnp.float32) / ROPE_DIM)
    rot_angle = positions[:, None] * inv_freq[None, :]
    rot_angle = jnp.concatenate([rot_angle, rot_angle], axis=-1)
    return jnp.cos(rot_angle), jnp.sin(rot_angle)


def apply_rope(in_vals, cos_tab, sin_tab):
    half_dim = ROPE_DIM // 2
    vals_f32 = in_vals.astype(jnp.float32)
    turned = jnp.concatenate([-vals_f32[..., half_dim:], vals_f32[..., :half_dim]], axis=-1)
    return (vals_f32 * cos_tab + turned * sin_tab).astype(jnp.bfloat16)


def attend_local(q_proj, pe_raw, kv_up):
    seq_len = q_proj.shape[1]
    cos_tab, sin_tab = rope_tables(seq_len)
    q_rot = apply_rope(q_proj[..., NOPE_DIM:], cos_tab[:, None, :], sin_tab[:, None, :])
    k_rot = apply_rope(pe_raw, cos_tab, sin_tab)
    scores = jnp.einsum('bshd,bthd->bhst', q_proj[..., :NOPE_DIM], kv_up[..., :NOPE_DIM], preferred_element_type=jnp.float32)
    scores = scores + jnp.einsum('bshd,btd->bhst', q_rot, k_rot, preferred_element_type=jnp.float32)
    positions = jnp.arange(seq_len)
    causal = positions[:, None] >= positions[None, :]
    scores = jnp.where(causal, scores * ATTN_SCALE, -1e30)
    attn_probs = jax.nn.softmax(scores, axis=-1).astype(jnp.bfloat16)
    attn_mix = jnp.einsum('bhst,bthd->bshd', attn_probs, kv_up[..., NOPE_DIM:], preferred_element_type=jnp.float32)
    return attn_mix.astype(jnp.bfloat16)


def block_step(tok_rows, grad_rows, full_weights, seq_count):
    gain_vec, w_query, w_kv_down, kv_gain, w_kv_up, w_out = full_weights
    kv_rank = kv_gain.shape[0]
    tok_count = tok_rows.shape[0]
    seq_len = tok_count // seq_count
    rows_f32 = tok_rows.astype(jnp.float32)
    normed, norm_pull = jax.vjp(rms_scale, rows_f32, gain_vec.astype(jnp.float32))
    q_proj = jnp.dot(normed, w_query, preferred_element_type=jnp.float32).astype(jnp.bfloat16)
    kv_down = jnp.dot(normed, w_kv_down, preferred_element_type=jnp.float32).astype(jnp.bfloat16)
    latent, latent_pull = jax.vjp(rms_scale, kv_down[:, :kv_rank], kv_gain.astype(jnp.float32))
    kv_up = jnp.dot(latent, w_kv_up, preferred_element_type=jnp.float32).astype(jnp.bfloat16)
    attn_mix, attn_pull = jax.vjp(attend_local, q_proj.reshape(seq_count, seq_len, -1, NOPE_DIM + ROPE_DIM), kv_down[:, kv_rank:].reshape(seq_count, seq_len, ROPE_DIM), kv_up.reshape(seq_count, seq_len, -1, NOPE_DIM + VALUE_DIM))
    mix_rows = attn_mix.reshape(tok_count, -1)
    out_f32 = rows_f32 + jnp.dot(mix_rows, w_out, preferred_element_type=jnp.float32)
    d_w_out = lax.dot_general(mix_rows, grad_rows, ROW_DIMS, preferred_element_type=jnp.float32)
    d_mix = lax.dot_general(grad_rows, w_out, COL_DIMS, preferred_element_type=jnp.float32).astype(jnp.bfloat16)
    d_query, d_pe, d_up = attn_pull(d_mix.reshape(attn_mix.shape))
    d_query = d_query.reshape(tok_count, -1)
    d_up = d_up.reshape(tok_count, -1)
    d_w_kv_up = lax.dot_general(latent, d_up, ROW_DIMS, preferred_element_type=jnp.float32)
    d_latent = lax.dot_general(d_up, w_kv_up, COL_DIMS, preferred_element_type=jnp.float32).astype(jnp.bfloat16)
    d_ckv, d_kv_gain = latent_pull(d_latent)
    d_down = jnp.concatenate([d_ckv, d_pe.reshape(tok_count, ROPE_DIM)], axis=1)
    d_w_kv_down = lax.dot_general(normed, d_down, ROW_DIMS, preferred_element_type=jnp.float32)
    d_w_query = lax.dot_general(normed, d_query, ROW_DIMS, preferred_element_type=jnp.float32)
    d_normed = lax.dot_general(d_query, w_query, COL_DIMS, preferred_element_type=jnp.float32)
    d_normed = d_normed + lax.dot_general(d_down, w_kv_down, COL_DIMS, preferred_element_type=jnp.float32)
    d_rows, d_gain = norm_pull(d_normed.astype(jnp.bfloat16))
    d_rows = d_rows + grad_rows.astype(jnp.float32)
    return out_f32.astype(jnp.bfloat16), d_rows, (d_gain, d_w_query, d_w_kv_down, d_kv_gain, d_w_kv_up, d_w_out)


def solution(mesh):
    tok_spec = P(('dp', 'fsdp'), None)
    seq_spec = P(('dp', 'fsdp'), None, None)
    part_vec = P(('dp', 'fsdp'))
    vec_spec = P('fsdp')
    mat_spec = P('fsdp', None)

    def device_step(tok_ids, grad_out, emb_table, norm_gain, w_query, w_kv_down, kv_gain, w_kv_up, w_out):
        seq_count, seq_len = tok_ids.shape
        vocab_dev, d_model = emb_table.shape
        tok_count = seq_count * seq_len
        all_ids = lax.all_gather(tok_ids.reshape(tok_count), 'fsdp', tiled=True)
        local_ids = all_ids - lax.axis_index('fsdp') * vocab_dev
        is_owned = (local_ids >= 0) & (local_ids < vocab_dev)
        picked = jnp.take(emb_table, jnp.where(is_owned, local_ids, 0), axis=0)
        picked = jnp.where(is_owned[:, None], picked, jnp.zeros((), picked.dtype))
        tok_rows = lax.psum_scatter(picked, 'fsdp', scatter_dimension=0, tiled=True)
        full_weights = tuple(lax.all_gather(shard_piece, 'fsdp', tiled=True) for shard_piece in (norm_gain, w_query, w_kv_down, kv_gain, w_kv_up, w_out))
        block_out, d_rows, weight_grads = block_step(tok_rows, grad_out.reshape(tok_count, d_model), full_weights, seq_count)
        all_grads = lax.all_gather(d_rows, 'fsdp', tiled=True)
        seg_ids = jnp.where(is_owned, local_ids, vocab_dev)
        grad_table = jax.ops.segment_sum(all_grads, seg_ids, num_segments=vocab_dev).astype(jnp.bfloat16)
        grad_shards = tuple(lax.psum_scatter(full_grad, 'fsdp', scatter_dimension=0, tiled=True) for full_grad in weight_grads)
        return (block_out.reshape(seq_count, seq_len, d_model), grad_table) + grad_shards

    return jax.shard_map(device_step, mesh=mesh, in_specs=(tok_spec, seq_spec, mat_spec, vec_spec, mat_spec, mat_spec, vec_spec, mat_spec, mat_spec), out_specs=(seq_spec, tok_spec, part_vec, tok_spec, tok_spec, part_vec, tok_spec, tok_spec), check_vma=False)
```

profile of v0, /device:TPU:0, one launch (start us, length us, event | category | flops | bytes accessed | tf_op | source)
XLA Modules:
  0.0 3533.8 jit_solution(13022343637823868345)
XLA Ops:
  24.2 654.2 %gather_fusion = bf16[18432,2048]{1,0:T(8,128)(2,1)} fusion(bf16[20480,2048]{1,0:T(8,128)(2,1)} %param.11, s32[18432]{0:T(1024)S(1)} %get-tuple-element.31), kind=kCustom, calls=%fused_computation | custom fusion | bytes 151068672 | tf_op jit(solution)/shard_map/jit(_take)/gather | solution.py:99
  678.5 50.1 %select_select_fusion = bf16[18432,2048]{1,0:T(8,128)(2,1)} fusion(bf16[18432,2048]{1,0:T(8,128)(2,1)} %gather_fusion, pred[18432]{0:T(1024)(128)(4,1)S(1)} %get-tuple-element.33, pred[18432]{0:T(1024)(128)(4,1)S(1)} %get-tuple-element.32), kind=kLoop, calls=%fused_computation.9 | loop fusion | flops 75497472 | bytes 151031808 | tf_op jit(solution)/shard_map/jit(_where)/select_n | solution.py:100
  732.2 326.6 %all-reduce.8 = bf16[512]{0:T(512)(128)(2,1)S(1)} all-reduce(bf16[512]{0:T(512)(128)(2,1)S(1)} %dynamic-update-slice), channel_id=1, replica_groups=mesh['dp'=1,'fsdp'=8] {'fsdp'}, use_global_device_ids=true, to_apply=%add.8 | all-reduce | flops 512 | bytes 2048
  1073.9 25.8 fusion.60
  1123.1 325.3 %reduce-scatter.6.cloned.1.call-done = bf16[2304,2048]{1,0:T(8,128)(2,1)} async-done(((bf16[18432,2048]{1,0:T(8,128)(2,1)}), bf16[2304,2048]{1,0:T(8,128)(2,1)}) %reduce-scatter.6.cloned.1.call-update) | async-done | bytes 9437200 | tf_op jit(solution)/shard_map/reduce_scatter | solution.py:101
  1454.6 61.9 %all-gather.12.cloned.1.call-done = bf16[2048,3072]{1,0:T(8,128)(2,1)} async-done(((bf16[256,3072]{1,0:T(8,128)(2,1)}), bf16[2048,3072]{1,0:T(8,128)(2,1)}) %all-gather.12.cloned.1.call-update) | async-done | bytes 12582928 | tf_op jit(solution)/shard_map/all_gather | solution.py:102
  1516.5 37.9 %convolution_convert_fusion.2 = bf16[2304,3072]{1,0:T(8,128)(2,1)} fusion(bf16[2048,3072]{1,0:T(8,128)(2,1)} %all-gather.12.cloned.1.call-done, bf16[2304,2048]{1,0:T(8,128)(2,1)} %reduce-scatter.6.cloned.1.call-done, f32[2048]{0:T(1024)S(1)} %bitcast.146, f32[2304]{0:T(1024)S(1)} %fusion.80), kind=kOutput, calls=%fused_computation.52 | convolution fusion | flops 29016981504 | bytes 36193280 | tf_op jit(solution)/shard_map/dot_general | solution.py:60
  1554.4 31.0 reshape.193
  1693.7 21.8 fusion.97
  1715.5 61.0 %fusion.91 = (f32[6,16,384]{2,1,0:T(8,128)S(1)}, f32[6,16,384,384]{2,3,1,0:T(8,128)}, f32[6,16,384,384]{2,3,1,0:T(8,128)}) fusion(f32[6,384,384,16]{2,1,3,0:T(8,128)} %fusion.97, pred[384,384]{0,1:T(8,128)(4,1)S(1)} %copy-done.9, bf16[6,384,16,128]{3,2,1,0:T(8,128)(2,1)} %get-tuple-element.20, bf16[6,384,16,128]{3,2,1,0:T(8,128)(2,1)} %slice.46), kind=kOutput, calls=%fused_computation.145 | convolution fusion | flops 3680464896 | bytes 189038592 | tf_op jit(solution)/shard_map/jvp(bshd,bthd->bhst)/dot_general | solution.py:43
  1776.5 18.3 fusion.23
  1794.9 43.0 %fusion.11 = (f32[6,16,384]{2,1,0:T(8,128)S(1)}, bf16[6,16,384,384]{2,3,1,0:T(8,128)(2,1)}, bf16[6,16,384,384]{2,3,1,0:T(8,128)(2,1)}) fusion(f32[6,16,384,384]{2,3,1,0:T(8,128)} %get-tuple-element.17, f32[6,16,384]{2,1,0:T(8,128)S(1)} %multiply_divide_fusion, f32[6,16,384]{2,1,0:T(8,128)S(1)} %get-tuple-element.16, f32[6,16,384]{2,1,0:T(8,128)S(1)} %fusion.23, ...), kind=kOutput, calls=%fused_computation.15 | convolution fusion | flops 3737088000 | bytes 132710400 | tf_op jit(solution)/shard_map/transpose(jvp(bhst,bthd->bshd))/dot_general | solution.py:49
  1838.0 56.8 %fusion.16 = bf16[6,384,384,16]{2,1,3,0:T(8,128)(2,1)} fusion(bf16[6,16,384,384]{2,3,1,0:T(8,128)(2,1)} %get-tuple-element.37, f32[6,384,384,16]{2,1,3,0:T(8,128)} %fusion.97, f32[6,16,384,384]{2,3,1,0:T(8,128)} %get-tuple-element.36, f32[6,384,16]{1,2,0:T(8,128)S(1)} %bitcast.139, f32[6,384,16]{1,2,0:T(8,128)S(1)} %get-tuple-element.29, ...), kind=kLoop, calls=%fused_computation.20 | loop fusion | flops 155713536 | bytes 170459136 | tf_op jit(solution)/shard_map/transpose(jvp())/mul | solution.py:47
  1909.5 16.7 convert_multiply_fusion.7
  1926.2 36.2 %convert_bitcast_fusion.1 = bf16[6,384,16,128]{1,3,2,0:T(8,128)(2,1)} fusion(bf16[6,384,16,128]{3,2,1,0:T(8,128)(2,1)} %slice.46, bf16[6,16,384,384]{2,3,1,0:T(8,128)(2,1)} %get-tuple-element.37, f32[6,16,384,384]{2,3,1,0:T(8,128)} %get-tuple-element.17, f32[6,16,384]{2,1,0:T(8,128)S(1)} %get-tuple-element.28, f32[6,16,384]{2,1,0:T(8,128)S(1)} %fusion.23, ...), kind=kOutput, calls=%fused_computation.69 | convolution fusion | flops 3727687680 | bytes 104398848 | tf_op jit(solution)/shard_map/transpose(jvp(bshd,bthd->bhst))/dot_general | solution.py:43
  1962.5 41.2 %convert_bitcast_fusion.3 = bf16[6,384,16,128]{1,3,2,0:T(8,128)(2,1)} fusion(bf16[6,384,16,128]{3,2,1,0:T(8,128)(2,1)} %get-tuple-element.20, bf16[6,16,384,384]{2,3,1,0:T(8,128)(2,1)} %get-tuple-element.37, f32[6,16,384,384]{2,3,1,0:T(8,128)} %get-tuple-element.17, f32[6,16,384]{2,1,0:T(8,128)S(1)} %get-tuple-element.28, f32[6,16,384]{2,1,0:T(8,128)S(1)} %fusion.23, ...), kind=kOutput, calls=%fused_computation.71 | convolution fusion | flops 3727687680 | bytes 104398848 | tf_op jit(solution)/shard_map/transpose(jvp(bshd,bthd->bhst))/dot_general | solution.py:43
  2003.7 19.6 convert_bitcast_fusion.2
  2039.9 24.4 copy.66
  2064.3 19.4 copy.85
  2083.8 17.6 fusion.62
  2128.2 25.2 copy.63
  2153.4 29.8 reshape.198
  2199.8 45.6 %fusion.27 = (f32[2048]{0:T(1024)S(1)}, f32[2304]{0:T(1024)S(1)}, bf16[2304,2048]{1,0:T(8,128)(2,1)}) fusion(bf16[2304,2048]{1,0:T(8,128)(2,1)} %reduce-scatter.6.cloned.1.call-done, f32[2304]{0:T(1024)S(1)} %copy-done.28, f32[2048]{0:T(1024)S(1)} %bitcast.148, f32[2304,2048]{1,0:T(8,128)} %fusion.67, bf16[2304,3072]{1,0:T(8,128)(2,1)} %reshape.198, ...), kind=kOutput, calls=%fused_computation.44 | convolution fusion | flops 29038211072 | bytes 64522240 | tf_op jit(solution)/shard_map/dot_general | solution.py:78
  2245.4 19.2 fusion.28
  2293.8 19.1 convert_bitcast_fusion.4
  2325.6 27.8 fusion.35
  2353.7 40.4 %fusion.85 = f32[2048,3072]{1,0:T(8,128)} fusion(bf16[2304,3072]{1,0:T(8,128)(2,1)} %reshape.198, bf16[2304,2048]{1,0:T(8,128)(2,1)} %reduce-scatter.6.cloned.1.call-done, f32[2048]{0:T(1024)S(1)} %bitcast.151, f32[2304]{0:T(1024)S(1)} %copy-done.28), kind=kOutput, calls=%fused_computation.144 | convolution fusion | flops 29009903616 | bytes 48776192 | tf_op jit(solution)/shard_map/dot_general | solution.py:77
  2405.7 23.5 all-reduce.11
  2430.4 27.0 fusion.30
  2457.4 461.4 %all-gather.16.cloned.1.call-done = f32[18432,2048]{1,0:T(8,128)} async-done(((f32[2304,2048]{1,0:T(8,128)}), f32[18432,2048]{1,0:T(8,128)}) %all-gather.16.cloned.1.call-update) | async-done | bytes 150994960 | tf_op jit(solution)/shard_map/all_gather | solution.py:104
  2918.8 528.6 %scatter_custom_fusion = f32[20480,2048]{1,0:T(8,128)} fusion(s32[18432]{0:T(1024)S(1)} %get-tuple-element.8, f32[18432,2048]{1,0:T(8,128)} %all-gather.16.cloned.1.call-done, s32[18432]{0:T(1024)S(1)} %broadcast_clamp_fusion, f32[]{:T(128)} %constant.23.clone.1), kind=kCustom, calls=%fused_computation.3 | custom fusion | flops 37748736 | bytes 167772672 | tf_op jit(solution)/shard_map/scatter-add | solution.py:106
  3447.4 79.2 %convert_element_type.170 = bf16[20480,2048]{1,0:T(8,128)(2,1)} convert(f32[20480,2048]{1,0:T(8,128)} %scatter_custom_fusion) | non-fusion elementwise | flops 41943040 | bytes 251658240 | tf_op jit(solution)/shard_map/convert_element_type | solution.py:106
  (176 shorter events, 303.1 us)
Async XLA Ops:
  7.2 1066.7 %all-gather.14.cloned.1.call-start = ((), (), s32[]{:S(2)}) async-start(), calls=%async_computation.9 | async-start | bytes 9437184 | tf_op jit(solution)/shard_map/all_gather | solution.py:102
  7.9 1440.5 %reduce-scatter.6.cloned.1.call-start = ((), (), s32[]{:S(2)}) async-start(), calls=%async_computation.5 | async-start | bytes 84934656 | tf_op jit(solution)/shard_map/reduce_scatter | solution.py:101
  24.2 654.2 %copy-start.20 = (s32[1,8,2304]{2,1,0:T(8,128)S(1)}, s32[1,8,2304]{2,1,0:T(8,128)}, u32[]{:S(2)}) copy-start(s32[1,8,2304]{2,1,0:T(8,128)} %copy-done.19) | copy-start | bytes 221188
  728.6 787.9 %all-gather.12.cloned.1.call-start = ((), (), s32[]{:S(2)}) async-start(), calls=%async_computation.8 | async-start | bytes 14155776 | tf_op jit(solution)/shard_map/all_gather | solution.py:102
  729.3 895.4 %all-gather.8.cloned.1.call-start = ((), (), s32[]{:S(2)}) async-start(), calls=%async_computation.6 | async-start | bytes 2654208 | tf_op jit(solution)/shard_map/all_gather | solution.py:102
  729.9 910.1 %all-gather.10.cloned.1.call-start = ((), (), s32[]{:S(2)}) async-start(), calls=%async_computation.7 | async-start | bytes 4718592 | tf_op jit(solution)/shard_map/all_gather | solution.py:102
  730.5 2188.3 %all-gather.16.cloned.1.call-start = ((), (), s32[]{:S(2)}) async-start(), calls=%async_computation.10 | async-start | bytes 169869312 | tf_op jit(solution)/shard_map/all_gather | solution.py:104
  1072.9 551.8 %copy-start.32 = (f32[8,1,256]{2,1,0:T(1,128)}, f32[8,1,256]{2,1,0:T(1,128)S(1)}, u32[]{:S(2)}) copy-start(f32[8,1,256]{2,1,0:T(1,128)S(1)} %convert_element_type.173) | copy-start | bytes 24580
  1454.6 170.1 %copy-start.27 = (f32[2304]{0:T(1024)}, f32[2304]{0:T(1024)S(1)}, u32[]{:S(2)}) copy-start(f32[2304]{0:T(1024)S(1)} %fusion.80) | copy-start | bytes 27652
  1635.0 20.7 copy-start.6
  1636.4 19.2 copy-start.29
  1693.7 21.8 copy-start.1
  1693.7 21.8 copy-start.9
  1794.9 43.1 %copy-start.21 = (pred[384,384]{1,0:T(8,128)(4,1)S(1)}, pred[384,384]{1,0:T(8,128)(4,1)}, u32[]{:S(2)}) copy-start(pred[384,384]{1,0:T(8,128)(4,1)} %iota_compare_fusion) | copy-start | bytes 442372
  1838.0 56.8 %copy-start.2 = (bf16[6,384,16,64]{1,3,2,0:T(8,128)(2,1)S(1)}, bf16[6,384,16,64]{1,3,2,0:T(8,128)(2,1)}, u32[]{:S(2)}) copy-start(bf16[6,384,16,64]{1,3,2,0:T(8,128)(2,1)} %copy-done.1) | copy-start | bytes 14155780
  1838.0 56.8 %copy-start.4 = (f32[384,64]{0,1:T(8,128)S(1)}, f32[384,64]{0,1:T(8,128)}, u32[]{:S(2)}) copy-start(f32[384,64]{0,1:T(8,128)} %get-tuple-element.35) | copy-start | bytes 294916
  2064.3 19.4 copy-start.7
  2064.3 19.4 copy-start.30
  2064.3 19.4 copy-start.35
  2064.3 19.4 copy-start.38
  2083.7 17.9 slice-start
  2083.7 17.7 copy-start.26
  2083.8 17.7 copy-start.17
  2083.8 17.7 copy-start.14
  2083.8 17.7 copy-start.16
  2083.8 17.9 slice-start.1
  2083.8 17.9 slice-start.2
  2199.8 45.6 %copy-start.24 = (f32[2304]{0:T(1024)S(1)}, f32[2304]{0:T(1024)}, u32[]{:S(2)}) copy-start(f32[2304]{0:T(1024)} %copy-done.23) | copy-start | bytes 27652
  2264.6 1262.0 %reduce-scatter.10.cloned.1.call-start = ((), (), s32[]{:S(2)}) async-start(), calls=%async_computation.12 | async-start | bytes 5308416 | tf_op jit(solution)/shard_map/reduce_scatter | solution.py:107
  2277.4 1249.2 %reduce-scatter.12.cloned.1.call-start = ((), (), s32[]{:S(2)}) async-start(), calls=%async_computation.13 | async-start | bytes 9437184 | tf_op jit(solution)/shard_map/reduce_scatter | solution.py:107
  2293.4 1233.3 %reduce-scatter.14.cloned.1.call-start = ((), (), s32[]{:S(2)}) async-start(), calls=%async_computation.14 | async-start | bytes 18874368 | tf_op jit(solution)/shard_map/reduce_scatter | solution.py:107
  2353.5 1173.2 %reduce-scatter.8.cloned.1.call-start = ((), (), s32[]{:S(2)}) async-start(), calls=%async_computation.11 | async-start | bytes 28311552 | tf_op jit(solution)/shard_map/reduce_scatter | solution.py:107
  (22 other events, 183.8 us)
Sparse Core Ops, SparseCore 0:
  9.8 51.3 all-gather.13
  728.7 719.6 reduce-scatter.5
  1450.2 66.2 all-gather.11
  1518.2 23.4 all-gather.7
  1543.3 30.7 all-gather.9
  2264.7 653.9 all-gather.15
  2922.7 45.0 reduce-scatter.9
  2971.7 62.2 reduce-scatter.11
  3038.1 106.9 reduce-scatter.13
  3149.0 146.4 reduce-scatter.7
where the time goes:
time: 3560 us; the launch traced here: 3530 us
  local copies, waits for them, and re-layouts  892 us (25%)
  waiting for transfers between devices  851 us (24%)
  other arithmetic  834 us (23%)
  matrix products  562 us (16%)
  blocking collectives  378 us (11%)
    gather x1, local copies, waits for them, and re-layouts, device_step(): picked = jnp.take(emb_table, jnp.where(is_owned, local_ids, 0), axis=0)  654 us
    scatter-add x3, other arithmetic, device_step(): jax.ops.segment_sum(all_grads, seg_ids, num_segments=vocab_dev)  539 us
    all_gather x1, waiting for transfers between devices, device_step(): all_grads = lax.all_gather(d_rows, 'fsdp', tiled=True)  461 us
    unnamed x2, blocking collectives  350 us
    reduce_scatter x1, waiting for transfers between devices, device_step(): tok_rows = lax.psum_scatter(picked, 'fsdp', scatter_dimension=0, tiled=True)  325 us
    dot_general x3, matrix products, attend_local(): jnp.einsum('bshd,bthd->bhst', q_proj[..., :NOPE_DIM], kv_up[..., :NOPE_DI...  138 us
    dot_general x3, matrix products, attend_local(): jnp.einsum('bhst,bthd->bshd', attn_probs, kv_up[..., NOPE_DIM:], preferre...  81.7 us
    convert_element_type x1, other arithmetic, device_step(): jax.ops.segment_sum(all_grads, seg_ids, num_segments=vocab_dev)  79.2 us
  transfers between devices with their start and end apart: 10, of which 3 were waited for; matrix products, arithmetic and copies ran while one was open for 47% of the time, Pallas kernels for 0%

commit v1 on v0

v1 whole, which is shorter than its diff:
```python
import functools
import math
import jax
import jax.numpy as jnp
import numpy as np
from jax import lax
from jax.experimental import pallas as pl
from jax.experimental.pallas import tpu as pltpu
from jax.sharding import PartitionSpec as P

NOPE_DIM = 128
ROPE_DIM = 64
VALUE_DIM = 128
ROPE_THETA = 50000.0
RMS_EPS = 1e-6
ATTN_SCALE = (NOPE_DIM + ROPE_DIM) ** -0.5 * (0.1 * math.log(32.0) + 1.0) ** 2
ROW_DIMS = (((0,), (0,)), ((), ()))
COL_DIMS = (((1,), (1,)), ((), ()))
LANES = 128
TABLE_BLOCK = 256
PICK_CHUNK = 32
PICK_RING = 4
ADD_CHUNK = 16
ADD_RING = 3
NO_ROW = 1 << 30
F32 = jnp.float32
BF16 = jnp.bfloat16
SMEM = pltpu.SMEM
ANY = pl.ANY


def params(vmem_mib, **kw):
    return pltpu.CompilerParams(vmem_limit_bytes=vmem_mib << 20, **kw)


def unique_body(shift, keys_ref, uniq_ref, rank_ref, count_ref):
    n = keys_ref.shape[0]
    unroll = 8

    def step(i, carry):
        k, prev = carry
        for j in range(unroll):
            key = keys_ref[i * unroll + j]
            row = lax.shift_right_logical(key, shift)
            k = k + (row != prev).astype(jnp.int32)
            uniq_ref[k] = row
            rank_ref[key & ((1 << shift) - 1)] = k
            prev = row
        return k, prev

    k, _ = lax.fori_loop(0, n // unroll, step, (jnp.int32(-1), jnp.int32(-1)))
    count_ref[0] = k + 1


def unique_rows(ids):
    n = ids.shape[0]
    shift = max(1, (n - 1).bit_length())
    keys = lax.sort(ids * (1 << shift) + jnp.arange(n, dtype=jnp.int32))
    smem = pl.BlockSpec(memory_space=SMEM)
    uniq, rank, count = pl.pallas_call(
        functools.partial(unique_body, shift),
        out_shape=[jax.ShapeDtypeStruct((n,), jnp.int32), jax.ShapeDtypeStruct((n,), jnp.int32), jax.ShapeDtypeStruct((1,), jnp.int32)],
        in_specs=[smem], out_specs=[smem] * 3, name="unique_rows")(keys)
    return jnp.where(jnp.arange(n, dtype=jnp.int32) < count[0], uniq, NO_ROW), rank


def pick_body(n_dev, n_tok, rows_ref, edge_ref, table_ref, out_ref, lin_ref, stage_ref, sems):
    b = pl.program_id(0)
    n_blk = pl.num_programs(0)
    rows_blk, d_model = table_ref.shape
    cols = d_model // LANES
    n_edge = edge_ref.shape[0] // n_dev

    def chunk_copy(d, k):
        slot = lax.rem(k, PICK_RING)
        return pltpu.make_async_copy(
            stage_ref.at[d, pl.ds(slot * PICK_CHUNK, PICK_CHUNK)],
            out_ref.at[pl.ds(d * n_tok + k * PICK_CHUNK, PICK_CHUNK)],
            sems.at[d, slot])

    @pl.loop(0, rows_blk // 16)
    def _(g):
        for j in range(cols):
            lin_ref[pl.ds(g * 16 * cols + j, 16, stride=cols), :] = table_ref[pl.ds(g * 16, 16), j * LANES:(j + 1) * LANES].astype(F32)

    @pl.loop(0, n_dev)
    def _(d):
        first = edge_ref[d * n_edge]
        lo = edge_ref[d * n_edge + b] - first
        hi = edge_ref[d * n_edge + b + 1] - first

        @pl.when(hi > lo)
        def _():
            @pl.loop(lo // PICK_CHUNK, (hi - 1) // PICK_CHUNK + 1)
            def _(k):
                start = jnp.maximum(lo, k * PICK_CHUNK)
                stop = jnp.minimum(hi, (k + 1) * PICK_CHUNK)

                @pl.when((start == k * PICK_CHUNK) & (k >= PICK_RING))
                def _():
                    chunk_copy(d, k - PICK_RING).wait()

                @pl.loop(start, stop)
                def _(p):
                    row = rows_ref[d * n_tok + first + p] - b * rows_blk
                    vals = lin_ref[pl.ds(pl.multiple_of(row * cols, cols), cols), :]
                    stage_ref[d, lax.rem(p, PICK_RING * PICK_CHUNK)] = vals.astype(BF16)

                @pl.when(stop == (k + 1) * PICK_CHUNK)
                def _():
                    chunk_copy(d, k).start()

    @pl.when(b == n_blk - 1)
    def _():
        @pl.loop(0, n_dev)
        def _(d):
            total = edge_ref[d * n_edge + n_blk] - edge_ref[d * n_edge]
            chunks = (total + PICK_CHUNK - 1) // PICK_CHUNK

            @pl.when(lax.rem(total, PICK_CHUNK) != 0)
            def _():
                chunk_copy(d, chunks - 1).start()

            @pl.loop(jnp.maximum(chunks - PICK_RING, 0), chunks)
            def _(k):
                chunk_copy(d, k).wait()


def pick_rows(table, rows, edges):
    n_dev, n_tok = rows.shape
    n_rows, d_model = table.shape
    cols = d_model // LANES
    return pl.pallas_call(
        functools.partial(pick_body, n_dev, n_tok),
        grid_spec=pltpu.PrefetchScalarGridSpec(
            num_scalar_prefetch=2, grid=(n_rows // TABLE_BLOCK,),
            in_specs=[pl.BlockSpec((TABLE_BLOCK, d_model), lambda b, *_: (b, 0))],
            out_specs=pl.BlockSpec(memory_space=ANY),
            scratch_shapes=[
                pltpu.VMEM((TABLE_BLOCK * cols, LANES), F32),
                pltpu.VMEM((n_dev, PICK_RING * PICK_CHUNK, cols, LANES), BF16),
                pltpu.SemaphoreType.DMA((n_dev, PICK_RING))]),
        out_shape=jax.ShapeDtypeStruct((n_dev * n_tok, cols, LANES), BF16),
        compiler_params=params(32), name="pick_rows",
        cost_estimate=pl.CostEstimate(flops=60_000_000, bytes_accessed=table.size * 2, transcendentals=0),
    )(rows.reshape(-1), edges.reshape(-1), table)


def spread_body(rank_ref, slot_ref, recv_ref, gain_ref, h0_ref, x_ref, lin_ref):
    i = pl.program_id(0)
    rows_blk, d_model = h0_ref.shape
    cols = d_model // LANES
    unroll = 8

    @pl.loop(0, rows_blk // unroll)
    def _(t0):
        for u in range(unroll):
            t = t0 * unroll + u
            lin_ref[pl.ds(pl.multiple_of(t * cols, cols), cols), :] = recv_ref[slot_ref[rank_ref[i * rows_blk + t]]].astype(F32)

    @pl.loop(0, rows_blk // 16)
    def _(g):
        tiles = [lin_ref[pl.ds(g * 16 * cols + j, 16, stride=cols), :] for j in range(cols)]
        square = tiles[0] * tiles[0]
        for v in tiles[1:]:
            square = square + v * v
        inv = lax.rsqrt(jnp.sum(square, axis=-1, keepdims=True) * (1.0 / d_model) + RMS_EPS)
        for j, v in enumerate(tiles):
            at = (pl.ds(g * 16, 16), slice(j * LANES, (j + 1) * LANES))
            h0_ref[at] = v.astype(BF16)
            x_ref[at] = (v * inv * gain_ref[:, j * LANES:(j + 1) * LANES]).astype(BF16)


def spread_rows(recv, rank, slot, gain):
    n_tok, cols, _ = recv.shape
    d_model = cols * LANES
    blk = 128
    out = jax.ShapeDtypeStruct((n_tok, d_model), BF16)
    row_spec = pl.BlockSpec((blk, d_model), lambda i, *_: (i, 0))
    return pl.pallas_call(
        spread_body,
        grid_spec=pltpu.PrefetchScalarGridSpec(
            num_scalar_prefetch=2, grid=(n_tok // blk,),
            in_specs=[pl.BlockSpec((n_tok, cols, LANES), lambda i, *_: (0, 0, 0), pipeline_mode=pl.Buffered(1)),
                      pl.BlockSpec((1, d_model), lambda i, *_: (0, 0))],
            out_specs=[row_spec, row_spec],
            scratch_shapes=[pltpu.VMEM((blk * cols, LANES), F32)]),
        out_shape=[out, out], compiler_params=params(32), name="spread_rows",
        cost_estimate=pl.CostEstimate(flops=60_000_000, bytes_accessed=n_tok * d_model * 6, transcendentals=0),
    )(rank, slot, recv, gain.reshape(1, d_model))


def rope_tables(seq_len):
    pos = np.arange(seq_len, dtype=np.float32)
    inv_freq = (np.float32(ROPE_THETA) ** (np.float32(-2.0) * np.arange(ROPE_DIM // 2, dtype=np.float32) / np.float32(ROPE_DIM))).astype(np.float32)
    angle = (pos[:, None] * inv_freq[None, :]).astype(np.float32).astype(np.float64)
    cos, sin, zero = np.cos(angle), np.sin(angle), np.zeros_like(angle)
    full = lambda lo, hi: np.concatenate([lo, hi, lo, hi], axis=1).astype(np.float32)
    return full(cos, cos), full(-sin, zero), full(zero, sin)


def turn(vals, cos, sin_lo, sin_hi, sign):
    half = ROPE_DIM // 2
    return vals * cos + sign * (pltpu.roll(vals, LANES - half, 1) * sin_lo + pltpu.roll(vals, half, 1) * sin_hi)


def attn_body(q_ref, pe_ref, kv_ref, do_ref, cos_ref, sin_lo_ref, sin_hi_ref,
              o_ref, dq_ref, dkv_ref, dpe_ref, krot_ref, dk_ref, dv_ref, dkrot_ref):
    pair = pl.program_id(1)
    seq_len = q_ref.shape[0]
    blk = 128
    low = lax.broadcasted_iota(jnp.int32, (1, LANES), 1) < ROPE_DIM

    @pl.when(pair == 0)
    def _():
        pe = pe_ref[...].astype(F32)
        pe = jnp.where(low, pe, pltpu.roll(pe, ROPE_DIM, 1))
        krot_ref[...] = turn(pe, cos_ref[...], sin_lo_ref[...], sin_hi_ref[...], 1.0).astype(BF16)
        dkrot_ref[...] = jnp.zeros_like(dkrot_ref)

    qrot = turn(q_ref[:, 2 * LANES:].astype(F32), cos_ref[...], sin_lo_ref[...], sin_hi_ref[...], 1.0)
    krot = krot_ref[...]
    causal = lax.broadcasted_iota(jnp.int32, (blk, blk), 0) >= lax.broadcasted_iota(jnp.int32, (blk, blk), 1)
    dqrots = []
    for h in range(2):
        mine = low if h == 0 else ~low
        qcat = jnp.concatenate([q_ref[:, h * LANES:(h + 1) * LANES], jnp.where(mine, qrot, 0.0).astype(BF16)], axis=1)
        kcat = jnp.concatenate([kv_ref[:, 2 * h * LANES:(2 * h + 1) * LANES], krot], axis=1)
        val = kv_ref[:, (2 * h + 1) * LANES:(2 * h + 2) * LANES]
        dout = do_ref[:, h * LANES:(h + 1) * LANES]
        dqrot = []
        for i in reversed(range(seq_len // blk)):
            here, seen = slice(i * blk, (i + 1) * blk), (i + 1) * blk
            s = lax.dot_general(qcat[here], kcat[:seen], COL_DIMS, preferred_element_type=F32) * ATTN_SCALE
            diag = jnp.where(causal, s[:, i * blk:], -1e30)
            s = diag if i == 0 else jnp.concatenate([s[:, :i * blk], diag], axis=1)
            e = jnp.exp(s - jnp.max(s, axis=-1, keepdims=True))
            p = e * (1.0 / jnp.sum(e, axis=-1, keepdims=True))
            pb = p.astype(BF16)
            o_ref[here, h * LANES:(h + 1) * LANES] = jnp.dot(pb, val[:seen], preferred_element_type=F32).astype(BF16)
            dp = lax.dot_general(dout[here], val[:seen], COL_DIMS, preferred_element_type=F32)
            ds = (p * (dp - jnp.sum(dp * p, axis=-1, keepdims=True)) * ATTN_SCALE).astype(BF16)
            dqi = jnp.dot(ds, kcat[:seen], preferred_element_type=F32)
            dq_ref[here, h * LANES:(h + 1) * LANES] = dqi[:, :LANES].astype(BF16)
            dqrot.append(dqi[:, LANES:])
            dvi = lax.dot_general(pb, dout[here], ROW_DIMS, preferred_element_type=F32)
            dki = lax.dot_general(ds, qcat[here], ROW_DIMS, preferred_element_type=F32)
            if seen == seq_len:
                dv_ref[...] = dvi
                dk_ref[...] = dki
            else:
                dv_ref[:seen] += dvi
                dk_ref[:seen] += dki
        dqrots.append(jnp.concatenate(dqrot[::-1], axis=0))
        dkv_ref[:, 2 * h * LANES:(2 * h + 1) * LANES] = dk_ref[:, :LANES].astype(BF16)
        dkv_ref[:, (2 * h + 1) * LANES:(2 * h + 2) * LANES] = dv_ref[...].astype(BF16)
        dkrot_ref[...] += dk_ref[:, LANES:]
    dqr = jnp.where(low, dqrots[0], dqrots[1]).astype(BF16).astype(F32)
    dq_ref[:, 2 * LANES:] = turn(dqr, cos_ref[...], sin_lo_ref[...], sin_hi_ref[...], -1.0).astype(BF16)

    @pl.when(pair == pl.num_programs(1) - 1)
    def _():
        both = dkrot_ref[...]
        both = (both + pltpu.roll(both, ROPE_DIM, 1)).astype(BF16).astype(F32)
        dpe = turn(both, cos_ref[...], sin_lo_ref[...], sin_hi_ref[...], -1.0)
        dpe_ref[...] = jnp.where(low, dpe, 0.0).astype(BF16)


def attend(qx, kv, d_mix, seq_count, pe_block):
    tok = qx.shape[0]
    seq_len = tok // seq_count
    pairs = d_mix.shape[1] // (2 * VALUE_DIM)
    tabs = [jnp.asarray(t) for t in rope_tables(seq_len)]
    at = lambda width: pl.BlockSpec((seq_len, width), lambda s, j: (s, j))
    tab = pl.BlockSpec((seq_len, LANES), lambda s, j: (0, 0))
    shape = lambda w: jax.ShapeDtypeStruct((tok, w), BF16)
    return pl.pallas_call(
        attn_body, grid=(seq_count, pairs),
        in_specs=[at(3 * LANES), pl.BlockSpec((seq_len, LANES), lambda s, j: (s, pe_block)), at(4 * LANES), at(2 * LANES), tab, tab, tab],
        out_specs=[at(2 * LANES), at(3 * LANES), at(4 * LANES), pl.BlockSpec((seq_len, LANES), lambda s, j: (s, 0))],
        out_shape=[shape(pairs * 2 * LANES), shape(pairs * 3 * LANES), shape(pairs * 4 * LANES), shape(LANES)],
        scratch_shapes=[pltpu.VMEM((seq_len, LANES), BF16), pltpu.VMEM((seq_len, 2 * LANES), F32),
                        pltpu.VMEM((seq_len, LANES), F32), pltpu.VMEM((seq_len, LANES), F32)],
        compiler_params=params(40), name="attention",
        cost_estimate=pl.CostEstimate(flops=tok * seq_len * pairs * 2 * 7 * 256, bytes_accessed=tok * pairs * 128 * 2 * 18, transcendentals=0),
    )(qx, qx, kv, d_mix, *tabs)


def merge_body(rank_ref, slot_ref, dx_ref, h0_ref, dy_ref, gain_ref, out_ref, dgain_ref, lin_ref, acc_ref, gacc_ref, sem):
    i = pl.program_id(0)
    rows_blk, d_model = h0_ref.shape
    cols = d_model // LANES

    @pl.when(i == 0)
    def _():
        gacc_ref[...] = jnp.zeros_like(gacc_ref)

        @pl.loop(0, acc_ref.shape[0] // 8)
        def _(r):
            acc_ref[pl.ds(r * 8, 8)] = jnp.zeros((8,) + acc_ref.shape[1:], F32)

    @pl.loop(0, rows_blk // 16)
    def _(g):
        rows = pl.ds(g * 16, 16)
        lanes = [slice(j * LANES, (j + 1) * LANES) for j in range(cols)]
        square, cross = jnp.zeros((16, LANES), F32), jnp.zeros((16, LANES), F32)
        for at in lanes:
            v = h0_ref[rows, at].astype(F32)
            square = square + v * v
            cross = cross + v * (dx_ref[rows, at].astype(F32) * gain_ref[:, at])
        inv = lax.rsqrt(jnp.sum(square, axis=-1, keepdims=True) * (1.0 / d_model) + RMS_EPS)
        mean = jnp.sum(cross, axis=-1, keepdims=True) * inv * (1.0 / d_model)
        for j, at in enumerate(lanes):
            hat = h0_ref[rows, at].astype(F32) * inv
            w = dx_ref[rows, at].astype(F32)
            gacc_ref[:, at] += w * hat
            lin_ref[pl.ds(j, 16, stride=cols), :] = inv * (w * gain_ref[:, at] - hat * mean) + dy_ref[rows, at].astype(F32)
        for t in range(16):
            r = slot_ref[rank_ref[i * rows_blk + g * 16 + t]]
            acc_ref[r] = acc_ref[r] + lin_ref[pl.ds(t * cols, cols), :]

    @pl.when(i == pl.num_programs(0) - 1)
    def _():
        dgain_ref[...] = jnp.sum(gacc_ref[...], axis=0, keepdims=True)
        copy = pltpu.make_async_copy(acc_ref, out_ref, sem)
        copy.start()
        copy.wait()


def merge_rows(dx, h0, dy, gain, rank, slot):
    n_tok, d_model = h0.shape
    cols = d_model // LANES
    blk = 128
    row_spec = pl.BlockSpec((blk, d_model), lambda i, *_: (i, 0))
    return pl.pallas_call(
        merge_body,
        grid_spec=pltpu.PrefetchScalarGridSpec(
            num_scalar_prefetch=2, grid=(n_tok // blk,),
            in_specs=[row_spec, row_spec, row_spec, pl.BlockSpec((1, d_model), lambda i, *_: (0, 0))],
            out_specs=[pl.BlockSpec(memory_space=ANY), pl.BlockSpec((1, d_model), lambda i, *_: (0, 0))],
            scratch_shapes=[pltpu.VMEM((16 * cols, LANES), F32), pltpu.VMEM((n_tok, cols, LANES), F32),
                            pltpu.VMEM((16, d_model), F32), pltpu.SemaphoreType.DMA]),
        out_shape=[jax.ShapeDtypeStruct((n_tok, cols, LANES), F32), jax.ShapeDtypeStruct((1, d_model), F32)],
        compiler_params=params(40), name="merge_rows",
        cost_estimate=pl.CostEstimate(flops=100_000_000, bytes_accessed=n_tok * d_model * 10, transcendentals=0),
    )(rank, slot, dx, h0, dy, gain.reshape(1, d_model))


def add_body(n_dev, n_tok, rows_ref, edge_ref, recv_ref, out_ref, acc_ref, ring_ref, sems):
    b = pl.program_id(0)
    n_blk = pl.num_programs(0)
    rows_blk, d_model = out_ref.shape
    cols = d_model // LANES
    n_edge = edge_ref.shape[0] // n_dev

    def chunk_copy(s, k):
        slot = lax.rem(k, ADD_RING)
        return pltpu.make_async_copy(recv_ref.at[pl.ds(s * n_tok + k * ADD_CHUNK, ADD_CHUNK)],
                                     ring_ref.at[s, pl.ds(slot * ADD_CHUNK, ADD_CHUNK)], sems.at[s, slot])

    def chunks_of(s):
        return (edge_ref[s * n_edge + n_blk] - edge_ref[s * n_edge] + ADD_CHUNK - 1) // ADD_CHUNK

    @pl.when(b == 0)
    def _():
        @pl.loop(0, n_dev)
        def _(s):
            @pl.loop(0, jnp.minimum(chunks_of(s), ADD_RING))
            def _(k):
                chunk_copy(s, k).start()

    @pl.loop(0, rows_blk * cols // 64)
    def _(r):
        acc_ref[pl.ds(r * 64, 64), :] = jnp.zeros((64, LANES), F32)

    @pl.loop(0, n_dev)
    def _(s):
        first = edge_ref[s * n_edge]
        lo = edge_ref[s * n_edge + b] - first
        hi = edge_ref[s * n_edge + b + 1] - first

        @pl.when(hi > lo)
        def _():
            @pl.loop(lo // ADD_CHUNK, (hi - 1) // ADD_CHUNK + 1)
            def _(k):
                start = jnp.maximum(lo, k * ADD_CHUNK)
                stop = jnp.minimum(hi, (k + 1) * ADD_CHUNK)

                @pl.when(start == k * ADD_CHUNK)
                def _():
                    chunk_copy(s, k).wait()

                @pl.loop(start, stop)
                def _(p):
                    row = rows_ref[s * n_tok + first + p] - b * rows_blk
                    at = pl.ds(pl.multiple_of(row * cols, cols), cols)
                    acc_ref[at, :] += ring_ref[s, lax.rem(p, ADD_RING * ADD_CHUNK)]

                @pl.when((stop == (k + 1) * ADD_CHUNK) & (k + ADD_RING < chunks_of(s)))
                def _():
                    chunk_copy(s, k + ADD_RING).start()

    @pl.loop(0, rows_blk // 16)
    def _(g):
        for j in range(cols):
            out_ref[pl.ds(g * 16, 16), j * LANES:(j + 1) * LANES] = acc_ref[pl.ds(g * 16 * cols + j, 16, stride=cols), :].astype(BF16)


def add_rows(recv, rows, edges, n_rows):
    n_dev, n_tok = rows.shape
    cols = recv.shape[1]
    d_model = cols * LANES
    return pl.pallas_call(
        functools.partial(add_body, n_dev, n_tok),
        grid_spec=pltpu.PrefetchScalarGridSpec(
            num_scalar_prefetch=2, grid=(n_rows // TABLE_BLOCK,),
            in_specs=[pl.BlockSpec(memory_space=ANY)],
            out_specs=pl.BlockSpec((TABLE_BLOCK, d_model), lambda b, *_: (b, 0)),
            scratch_shapes=[pltpu.VMEM((TABLE_BLOCK * cols, LANES), F32),
                            pltpu.VMEM((n_dev, ADD_RING * ADD_CHUNK, cols, LANES), F32),
                            pltpu.SemaphoreType.DMA((n_dev, ADD_RING))]),
        out_shape=jax.ShapeDtypeStruct((n_rows, d_model), BF16),
        compiler_params=params(32), name="add_rows",
        cost_estimate=pl.CostEstimate(flops=60_000_000, bytes_accessed=n_rows * d_model * 2, transcendentals=0),
    )(rows.reshape(-1), edges.reshape(-1), recv)


def exchange_body(caps, tok, fetch, x_ref, out_ref, via_ref, send_sems, recv_sems, hop_send, hop_recv, end_send, end_recv, own_sem):
    n_dev = len(caps)
    offs = [sum(caps[:o]) for o in range(n_dev)]
    place = lax.axis_index('fsdp')
    far, side = 6, 4
    across = lambda m: [((m ^ far) & ~1) | c for c in range(2)]

    def rows(src, dst):
        if fetch:
            return dst * tok, offs[src], caps[src]
        return offs[dst], src * tok, caps[dst]

    def remote(src, dst, sems, to):
        return pltpu.make_async_remote_copy(src, dst, sems[0], sems[1], device_id={'fsdp': to}, device_id_type=pl.DeviceIdType.MESH)

    def direct(src, dst):
        at, to, n = rows(src, dst)
        n = n // 2 if (src ^ dst) & far == far else n
        return remote(x_ref.at[pl.ds(at, n)], out_ref.at[pl.ds(to, n)], (send_sems.at[dst], recv_sems.at[src]), dst)

    def hop(src, dst):
        at, _, n = rows(src, dst)
        c = dst & 1
        return remote(x_ref.at[pl.ds(at + n // 2, n - n // 2)], via_ref.at[c, pl.ds(0, n - n // 2)], (hop_send.at[c], hop_recv.at[c]), src ^ side)

    def end(src, dst):
        _, to, n = rows(src, dst)
        return remote(via_ref.at[dst & 1, pl.ds(0, n - n // 2)], out_ref.at[pl.ds(to + n // 2, n - n // 2)], (end_send.at[dst & 1], end_recv.at[src & 1]), dst)

    for m in range(n_dev):
        @pl.when(place == m)
        def _():
            for dst in across(m):
                hop(m, dst).start()
            for k in (6, 7, 4, 5, 2, 3, 1):
                direct(m, m ^ k).start()
            at, to, n = rows(m, m)
            own = pltpu.make_async_copy(x_ref.at[pl.ds(at, n)], out_ref.at[pl.ds(to, n)], own_sem)
            own.start()
            for dst in across(m ^ side):
                hop(m ^ side, dst).wait_recv()
                end(m ^ side, dst).start()
            own.wait()
            for dst in across(m):
                hop(m, dst).wait_send()
            for k in range(1, n_dev):
                direct(m, m ^ k).wait_send()
                direct(m ^ k, m).wait_recv()
            for dst in across(m ^ side):
                end(m ^ side, dst).wait_send()
            for src in across(m):
                end(src, m).wait_recv()


def exchange(x, caps, tok, fetch):
    n_dev = len(caps)
    cols = x.shape[1:]
    n_out = tok if fetch and sum(caps) <= tok else n_dev * tok
    hbm = pl.BlockSpec(memory_space=ANY)
    pair = pltpu.SemaphoreType.DMA((2,))
    wide = pltpu.SemaphoreType.DMA((n_dev,))
    return pl.pallas_call(
        functools.partial(exchange_body, tuple(caps), tok, fetch),
        out_shape=[jax.ShapeDtypeStruct((n_out,) + cols, x.dtype), jax.ShapeDtypeStruct((2, (max(caps) + 1) // 2) + cols, x.dtype)],
        in_specs=[hbm], out_specs=[hbm, hbm],
        scratch_shapes=[wide, wide, pair, pair, pair, pair, pltpu.SemaphoreType.DMA],
        compiler_params=pltpu.CompilerParams(has_side_effects=True), name="exchange",
        cost_estimate=pl.CostEstimate(flops=200_000_000_000, bytes_accessed=x.size * 2, transcendentals=0),
    )(x)[0]


def move_body(tok, count_ref, from_ref, to_ref, x_ref, out_ref, sems):
    depth = sems.shape[0]

    @pl.loop(0, count_ref.shape[0])
    def _(o):
        n = count_ref[o]

        def copy(i):
            return pltpu.make_async_copy(x_ref.at[pl.ds(from_ref[o] + i, 1)], out_ref.at[pl.ds(to_ref[o] + i, 1)], sems.at[lax.rem(i, depth)])

        @pl.loop(0, n)
        def _(i):
            @pl.when(i >= depth)
            def _():
                copy(i - depth).wait()
            copy(i).start()

        @pl.loop(jnp.maximum(n - depth, 0), n)
        def _(i):
            copy(i).wait()


def move_rows(x, count, start_from, start_to, n_out):
    smem, hbm = pl.BlockSpec(memory_space=SMEM), pl.BlockSpec(memory_space=ANY)
    return pl.pallas_call(
        functools.partial(move_body, n_out), out_shape=jax.ShapeDtypeStruct((n_out,) + x.shape[1:], x.dtype),
        in_specs=[smem, smem, smem, hbm], out_specs=hbm, scratch_shapes=[pltpu.SemaphoreType.DMA((16,))],
        name="move_rows")(count, start_from, start_to, x)


def rms_scale(in_vals, gain_vec):
    vals_f32 = in_vals.astype(F32)
    inv_rms = lax.rsqrt(jnp.mean(vals_f32 * vals_f32, axis=-1, keepdims=True) + RMS_EPS)
    return (vals_f32 * inv_rms * gain_vec).astype(BF16)


def dot(a, b, dims):
    return lax.dot_general(a, b, dims, preferred_element_type=F32)


NN = (((1,), (0,)), ((), ()))


def pair_heads(w):
    r = w.shape[0]
    w = w.reshape(r, -1, 2, NOPE_DIM + ROPE_DIM)
    plain = w[..., :NOPE_DIM].reshape(r, -1, 2 * NOPE_DIM)
    rot = w[..., NOPE_DIM:].reshape(r, -1, 2 * ROPE_DIM)
    return jnp.concatenate([plain, rot], axis=-1).reshape(r, -1)


def unpair_heads(w):
    r = w.shape[0]
    w = w.reshape(r, -1, 2 * (NOPE_DIM + ROPE_DIM))
    plain = w[..., :2 * NOPE_DIM].reshape(r, -1, 2, NOPE_DIM)
    rot = w[..., 2 * NOPE_DIM:].reshape(r, -1, 2, ROPE_DIM)
    return jnp.concatenate([plain, rot], axis=-1).reshape(r, -1)


def solution(mesh):
    n_dev = mesh.shape['fsdp']
    tok_spec = P(('dp', 'fsdp'), None)
    seq_spec = P(('dp', 'fsdp'), None, None)
    part_vec = P(('dp', 'fsdp'))
    vec_spec = P('fsdp')
    mat_spec = P('fsdp', None)

    def device_step(tok_ids, grad_out, emb_table, norm_gain, w_query, w_kv_down, kv_gain, w_kv_up, w_out):
        seq_count, seq_len = tok_ids.shape
        vocab_dev, d_model = emb_table.shape
        tok = seq_count * seq_len
        me = lax.axis_index('fsdp')
        gather = lambda piece: lax.all_gather(piece, 'fsdp', tiled=True)
        scatter = lambda full: lax.psum_scatter(full, 'fsdp', scatter_dimension=0, tiled=True)
        rows_dev, q_width = w_query.shape
        kv_rank = kv_gain.shape[0] * n_dev
        latent_at = q_width
        rank_dev = kv_gain.shape[0]
        pe_at = q_width + kv_rank
        pad_at = pe_at + ROPE_DIM
        width = -(-(pad_at + 2) // LANES) * LANES
        cols = d_model // LANES
        dy = grad_out.reshape(tok, d_model)

        uniq, rank = unique_rows(tok_ids.reshape(tok))
        all_uniq = gather(uniq).reshape(n_dev, tok)
        owner_edges = jnp.arange(n_dev + 1, dtype=jnp.int32) * vocab_dev
        starts = jnp.sum(all_uniq[:, None, :] < owner_edges[None, :, None], axis=-1, dtype=jnp.int32)
        counts = starts[:, 1:] - starts[:, :-1]
        rows = all_uniq - me * vocab_dev
        block_edges = jnp.arange(vocab_dev // TABLE_BLOCK + 1, dtype=jnp.int32) * TABLE_BLOCK
        edges = jnp.sum(rows[:, None, :] < block_edges[None, :, None], axis=-1, dtype=jnp.int32)
        mine = lambda table, axis: lax.dynamic_index_in_dim(table, me, axis, keepdims=False)
        named, my_starts = mine(counts, 0), mine(starts, 0)[:-1]
        caps = [3 * tok // 8] + [tok // 12] * (n_dev - 1)
        offs = jnp.asarray(np.cumsum([0] + caps[:-1]), jnp.int32)
        fits = jnp.all(counts <= jnp.asarray(caps, jnp.int32)[None, :])
        shift = jnp.where(fits, offs - my_starts, 0)
        place = jnp.arange(tok, dtype=jnp.int32)
        slot = place + shift[0] + jnp.sum(jnp.where(place[:, None] >= my_starts[None, 1:], (shift[1:] - shift[:-1])[None, :], 0), axis=-1)
        slots = jnp.arange(n_dev, dtype=jnp.int32) * tok

        gains = jnp.zeros((rows_dev, width - pad_at), BF16)
        gains = gains.at[:, 0].set(norm_gain).at[:rank_dev, 1].set(kv_gain)
        w_x = gather(jnp.concatenate([pair_heads(w_query), w_kv_down, gains], axis=1))
        w_o, w_up = gather(w_out), gather(w_kv_up)
        gain_vec = w_x[:, pad_at].astype(F32)
        kv_gain_vec = w_x.reshape(n_dev, rows_dev, width)[:, :rank_dev, pad_at + 1].reshape(kv_rank).astype(F32)

        sent = pick_rows(emb_table, rows, edges)
        recv = lax.cond(fits, lambda v: exchange(v, caps, tok, True),
                        lambda v: move_rows(exchange(v, [tok] * n_dev, tok, True), named, slots, my_starts, tok), sent)
        h0, x = spread_rows(recv, rank, slot, gain_vec)

        d_mix = dot(dy, w_o, COL_DIMS).astype(BF16)
        qx = dot(x, w_x, NN).astype(BF16)
        down = qx[:, latent_at:pe_at]
        latent, latent_pull = jax.vjp(rms_scale, down, kv_gain_vec)
        kv = dot(latent, w_up, NN).astype(BF16)
        mix, d_q, d_kv, d_pe = attend(qx, kv, d_mix, seq_count, pe_at // LANES)
        d_w_out = dot(mix, dy, ROW_DIMS)
        d_w_up = dot(latent, d_kv, ROW_DIMS)
        d_latent = dot(d_kv, w_up, COL_DIMS).astype(BF16)
        d_down, d_kv_gain = latent_pull(d_latent)
        d_qx = jnp.concatenate([d_q, d_down, d_pe], axis=1)
        d_x = dot(d_qx, w_x, COL_DIMS).astype(BF16)
        merged, d_gain = merge_rows(d_x, h0, dy, gain_vec, rank, slot)
        out = (h0.astype(F32) + dot(mix, w_o, NN)).astype(BF16)

        back = lax.cond(fits, lambda v: exchange(v, caps, tok, False),
                        lambda v: exchange(move_rows(v, named, my_starts, slots, n_dev * tok), [tok] * n_dev, tok, False), merged)
        grad_table = add_rows(back, rows, edges, vocab_dev)
        d_w_x = dot(x, d_qx, ROW_DIMS)
        d_gains = jnp.stack([d_gain.reshape(n_dev, rows_dev), jnp.pad(d_kv_gain.reshape(n_dev, rank_dev), ((0, 0), (0, rows_dev - rank_dev)))], axis=-1)
        d_w_x = lax.dynamic_update_slice(d_w_x, d_gains.reshape(d_model, 2), (0, pad_at))
        g_out, g_up, g_x = scatter(d_w_out), scatter(d_w_up), scatter(d_w_x)
        return (out.reshape(seq_count, seq_len, d_model), grad_table, g_x[:, pad_at], unpair_heads(g_x[:, :q_width]),
                g_x[:, q_width:pad_at], g_x[:rank_dev, pad_at + 1], g_up, g_out)

    return jax.shard_map(device_step, mesh=mesh, in_specs=(tok_spec, seq_spec, mat_spec, vec_spec, mat_spec, mat_spec, vec_spec, mat_spec, mat_spec), out_specs=(seq_spec, tok_spec, part_vec, tok_spec, tok_spec, part_vec, tok_spec, tok_spec), check_vma=False)
```

time: 3560 us -> 1660 us (0.47)
  Pallas kernels: 0 us -> 1280 us
  waiting for transfers between devices: 851 us -> 1.48 us
  local copies, waits for them, and re-layouts: 892 us -> 46.9 us
  other arithmetic: 834 us -> 22.6 us
  blocking collectives: 378 us -> 14.7 us
  matrix products: 562 us -> 264 us
    pallas_call x0 -> x8, Pallas kernels: none -> 1280 us  [the longest x2 621 us: exchange(): pl.pallas_call(functools.partial(exchange_body, tuple(caps), tok, fetch),...]
    gather x1 -> x0, local copies, waits for them, and re-layouts: 654 us -> none  [device_step(): picked = jnp.take(emb_table, jnp.where(is_owned, local_ids, 0), axis=0)]
    scatter-add x3 -> x0, other arithmetic: 539 us -> none  [device_step(): jax.ops.segment_sum(all_grads, seg_ids, num_segments=vocab_dev)]
    all_gather x5 -> x3, waiting for transfers between devices: 523 us -> 0.04 us  [device_step(): gather = lambda piece: lax.all_gather(piece, 'fsdp', tiled=True)]
    unnamed x2 -> x0, blocking collectives: 350 us -> none
    reduce_scatter x5 -> x3, waiting for transfers between devices: 325 us -> 0.01 us  [device_step(): lax.psum_scatter(full, 'fsdp', scatter_dimension=0, tiled=True)]
    dot_general x21 -> x9, matrix products: 562 us -> 264 us  [dot(): return lax.dot_general(a, b, dims, preferred_element_type=F32)]
    convert_element_type x9 -> x3, other arithmetic: 103 us -> 3.45 us  [the longest x1 2.68 us: rms_scale(): vals_f32 = in_vals.astype(F32)]
  transfers between devices with their start and end apart: 10 -> 6, of which waited for: 3 -> 0; matrix products, arithmetic and copies ran while one was open for 47% -> 12% of each run, Pallas kernels for 0% -> 64%
where the time goes in v1:
time: 1660 us; the launch traced here: 1650 us
  Pallas kernels  1280 us (77%)
  matrix products  264 us (16%)
  local copies, waits for them, and re-layouts  46.9 us (3%)
  other arithmetic  22.6 us (1%)
    pallas_call x2, Pallas kernels, exchange(): pl.pallas_call(functools.partial(exchange_body, tuple(caps), tok, fetch),...  621 us
    dot_general x9, matrix products, dot(): return lax.dot_general(a, b, dims, preferred_element_type=F32)  264 us
    pallas_call x1, Pallas kernels, add_rows(): pl.pallas_call(functools.partial(add_body, n_dev, n_tok), grid_spec=pltpu...  239 us
    pallas_call x1, Pallas kernels, attend(): pl.pallas_call(attn_body, grid=(seq_count, pairs), in_specs=[at(3 * LANES...  187 us
    pallas_call x1, Pallas kernels, pick_rows(): pl.pallas_call(functools.partial(pick_body, n_dev, n_tok), grid_spec=pltp...  157 us
    pallas_call x1, Pallas kernels, merge_rows(): pl.pallas_call(merge_body, grid_spec=pltpu.PrefetchScalarGridSpec(num_sca...  41.5 us
  transfers between devices with their start and end apart: 6, of which 0 were waited for; matrix products, arithmetic and copies ran while one was open for 12% of the time, Pallas kernels for 64%

profile of v1, /device:TPU:0, one launch (start us, length us, event | category | flops | bytes accessed | tf_op | source)
XLA Modules:
  0.0 1650.1 jit_solution(3917051013085451293)
XLA Ops:
  12.4 2.1 scatter.9
  17.4 5.8 sort.10
  23.2 10.1 unique_rows.1
  34.7 14.7 all-gather
  54.7 157.3 %pick_rows.1 = bf16[18432,16,128]{2,1,0:T(8,128)(2,1)} custom-call(s32[18432]{0:T(1024)S(1)} %bitcast.56, s32[648]{0:T(1024)S(1)} %reshape.184.edge_ref, bf16[20480,2048]{1,0:T(8,128)(2,1)} %table_ref.1), custom_call_target="tpu_custom_call" | custom-call | flops 60000000 | bytes 83886080 | tf_op jit(solution)/shard_map/pick_rows/pallas_call | solution.py:133
  212.0 157.4 %conditional.2 = (bf16[2304,16,128]{2,1,0:T(8,128)(2,1)}) conditional(s32[]{:T(128)} %convert_element_type.69, (bf16[18432,16,128]{2,1,0:T(8,128)(2,1)}, s32[8]{0:T(128)}, s32[8]{0:T(128)}, s32[8]{0:T(128)}) %tuple.57, bf16[18432,16,128]{2,1,0:T(8,128)(2,1)} %pick_rows.1), branch_computations={%region_5.6_spmd, %region_6.7_spmd} | conditional | flops 199999995904 | bytes 75497944 | solution.py:609
  212.0 157.1 %exchange.5 = (bf16[2304,16,128]{2,1,0:T(8,128)(2,1)}, bf16[2,432,16,128]{3,2,1,0:T(8,128)(2,1)}) custom-call(bf16[18432,16,128]{2,1,0:T(8,128)(2,1)} %x_ref), custom_call_target="tpu_custom_call" | custom-call | flops 199999995904 | bytes 75497472 | tf_op jit(solution)/shard_map/cond/branch_1_fun/exchange/pallas_call | solution.py:489
  369.4 25.9 %convolution_convert_fusion.2.do_ref = bf16[2304,2048]{1,0:T(8,128)(2,1)} fusion(bf16[2304,2048]{1,0:T(8,128)(2,1)} %bitcast.65, bf16[2048,2048]{1,0:T(8,128)(2,1)} %all-gather.9.cloned.1.call-done), kind=kOutput, calls=%fused_computation.4 | convolution fusion | flops 19332071424 | bytes 27262976 | tf_op jit(solution)/shard_map/dot_general | solution.py:536
  395.3 11.2 copy.61
  407.3 29.4 %spread_rows.1 = (bf16[2304,2048]{1,0:T(8,128)(2,1)S(1)}, bf16[2304,2048]{1,0:T(8,128)(2,1)S(1)}) custom-call(s32[2304]{0:T(1024)S(1)} %copy-done.4, s32[2304]{0:T(1024)S(1)} %add_add_fusion.1.slot_ref, bf16[2304,16,128]{2,1,0:T(8,128)(2,1)} %get-tuple-element.142.recv_ref, f32[1,2048]{1,0:T(1,128)S(1)} %fusion.13.gain_ref), custom_call_target="tpu_custom_call" | custom-call | flops 60000000 | bytes 28311552 | tf_op jit(solution)/shard_map/spread_rows/pallas_call | solution.py:180
  436.8 3.7 copy-done
  440.5 45.4 %convolution_convert_fusion.1.q_ref.pe_ref = bf16[2304,3712]{1,0:T(8,128)(2,1)} fusion(bf16[2304,2048]{1,0:T(8,128)(2,1)S(1)} %get-tuple-element.86, bf16[2048,3712]{0,1:T(8,128)(2,1)} %all-gather.5.cloned.1.call-done), kind=kOutput, calls=%fused_computation.1 | convolution fusion | flops 35039379456 | bytes 41746432 | tf_op jit(solution)/shard_map/dot_general | solution.py:536
  485.9 2.2 fusion.6
  488.1 17.0 %convolution_convert_fusion.kv_ref = bf16[2304,4096]{1,0:T(8,128)(2,1)} fusion(bf16[512,4096]{1,0:T(8,128)(2,1)} %all-gather.7.cloned.1.call-done, f32[512]{0:T(512)S(1)} %reshape.202, f32[2304]{0:T(1024)S(1)} %fusion.12, bf16[2304,3712]{1,0:T(8,128)(2,1)} %convolution_convert_fusion.1.q_ref.pe_ref), kind=kOutput, calls=%fused_computation | convolution fusion | flops 9677832192 | bytes 25439232 | tf_op jit(solution)/shard_map/dot_general | solution.py:536
  505.2 186.5 %attention.1 = (bf16[2304,2048]{1,0:T(8,128)(2,1)S(1)}, bf16[2304,3072]{1,0:T(8,128)(2,1)}, bf16[2304,4096]{1,0:T(8,128)(2,1)}, bf16[2304,128]{1,0:T(8,128)(2,1)S(1)}) custom-call(bf16[2304,3712]{1,0:T(8,128)(2,1)} %convolution_convert_fusion.1.q_ref.pe_ref, bf16[2304,3712]{1,0:T(8,128)(2,1)} %convolution_convert_fusion.1.q_ref.pe_ref, ...), custom_call_target="tpu_custom_call" | custom-call | flops 25367150592 | bytes 84934656 | tf_op jit(solution)/shard_map/attention/pallas_call | solution.py:277
  691.7 3.6 copy-done.11
  695.3 15.6 fusion.4
  711.0 2.7 fusion.5
  713.7 47.3 %fusion = f32[2048,3712]{1,0:T(8,128)} fusion(bf16[2304,2048]{1,0:T(8,128)(2,1)} %copy-done.7, bf16[2304,128]{1,0:T(8,128)(2,1)S(1)} %get-tuple-element.90, bf16[2304,512]{1,0:T(8,128)(2,1)S(1)} %fusion.5, bf16[2304,3072]{1,0:T(8,128)(2,1)} %get-tuple-element.88), kind=kOutput, calls=%fused_computation.11 | convolution fusion | flops 35082141696 | bytes 56950784 | tf_op jit(solution)/shard_map/dot_general | solution.py:536
  761.0 42.4 %convolution_convert_fusion.3.dx_ref = bf16[2304,2048]{1,0:T(8,128)(2,1)S(1)} fusion(bf16[2048,3712]{0,1:T(8,128)(2,1)} %all-gather.5.cloned.1.call-done, bf16[2304,128]{1,0:T(8,128)(2,1)S(1)} %get-tuple-element.90, bf16[2304,512]{1,0:T(8,128)(2,1)S(1)} %fusion.5, bf16[2304,3072]{1,0:T(8,128)(2,1)} %get-tuple-element.88), kind=kOutput, calls=%fused_computation.5 | convolution fusion | flops 35086860288 | bytes 41746432 | tf_op jit(solution)/shard_map/dot_general | solution.py:536
  803.4 41.5 %merge_rows.1 = (f32[2304,16,128]{2,1,0:T(8,128)}, f32[1,2048]{1,0:T(1,128)S(1)}) custom-call(s32[2304]{0:T(1024)S(1)} %copy-done.4, s32[2304]{0:T(1024)S(1)} %add_add_fusion.1.slot_ref, bf16[2304,2048]{1,0:T(8,128)(2,1)S(1)} %convolution_convert_fusion.3.dx_ref, bf16[2304,2048]{1,0:T(8,128)(2,1)} %copy-done, bf16[2304,2048]{1,0:T(8,128)(2,1)} %bitcast.66, ...), custom_call_target="tpu_custom_call" | custom-call | flops 100000000 | bytes 47185920 | tf_op jit(solution)/shard_map/merge_rows/pallas_call | solution.py:335
  845.3 5.9 dynamic_update_slice.3
  851.3 17.0 %fusion.8 = f32[512,4096]{1,0:T(8,128)} fusion(bf16[2304,4096]{1,0:T(8,128)(2,1)} %get-tuple-element.89, f32[512]{0:T(512)S(1)} %reshape.202, f32[2304]{0:T(1024)S(1)} %fusion.12, bf16[2304,3712]{1,0:T(8,128)(2,1)} %convolution_convert_fusion.1.q_ref.pe_ref), kind=kOutput, calls=%fused_computation.27 | convolution fusion | flops 9668395008 | bytes 29633536 | tf_op jit(solution)/shard_map/dot_general | solution.py:536
  868.4 27.1 %fusion.17 = f32[2048,2048]{1,0:T(8,128)} fusion(bf16[2304,2048]{1,0:T(8,128)(2,1)} %copy-done.11, bf16[2304,2048]{1,0:T(8,128)(2,1)} %bitcast.67), kind=kOutput, calls=%fused_computation.63 | convolution fusion | flops 19327352832 | bytes 35651584 | tf_op jit(solution)/shard_map/dot_general | solution.py:536
  896.3 463.7 %conditional.3 = (f32[18432,16,128]{2,1,0:T(8,128)}) conditional(s32[]{:T(128)} %convert_element_type.69, (s32[8]{0:T(128)S(1)}, s32[8]{0:T(128)S(1)}, s32[8]{0:T(128)S(1)}, f32[2304,16,128]{2,1,0:T(8,128)}) %tuple.60, f32[2304,16,128]{2,1,0:T(8,128)} %get-tuple-element.91), branch_computations={%region_10.11_spmd, %region_11.12_spmd} | conditional | flops 199999995904 | bytes 75497480 | solution.py:628
  896.3 463.7 %exchange.7 = (f32[18432,16,128]{2,1,0:T(8,128)}, f32[2,432,16,128]{3,2,1,0:T(8,128)}) custom-call(f32[2304,16,128]{2,1,0:T(8,128)} %x_ref.1), custom_call_target="tpu_custom_call" | custom-call | flops 199999995904 | bytes 9437184 | tf_op jit(solution)/shard_map/cond/branch_1_fun/exchange/pallas_call | solution.py:489
  1360.0 238.9 %add_rows.1 = bf16[20480,2048]{1,0:T(8,128)(2,1)} custom-call(s32[18432]{0:T(1024)S(1)} %bitcast.57, s32[648]{0:T(1024)S(1)} %copy-done.6, f32[18432,16,128]{2,1,0:T(8,128)} %get-tuple-element.143.recv_ref), custom_call_target="tpu_custom_call" | custom-call | flops 60000000 | bytes 83886080 | tf_op jit(solution)/shard_map/add_rows/pallas_call | solution.py:413
  1599.0 25.8 %add_convert_fusion = bf16[2304,2048]{1,0:T(8,128)(2,1)} fusion(bf16[2304,2048]{1,0:T(8,128)(2,1)S(1)} %copy-done.1, bf16[2304,2048]{1,0:T(8,128)(2,1)} %copy-done.11, bf16[2048,2048]{1,0:T(8,128)(2,1)} %all-gather.9.cloned.1.call-done), kind=kOutput, calls=%fused_computation.2 | convolution fusion | flops 19341508608 | bytes 36700160 | tf_op jit(solution)/shard_map/dot_general | solution.py:536
  1624.8 2.1 slice.123
  1629.7 2.1 copy.57
  1635.0 2.2 pad_maximum_fusion.3
  1637.2 2.4 copy.56
  (110 shorter events, 25.3 us)
Async XLA Ops:
  7.2 44.4 %copy-start.22 = (s32[8]{0:T(128)S(1)}, s32[8]{0:T(128)}, u32[]{:S(2)}) copy-start(s32[8]{0:T(128)} %constant.103.clone) | copy-start | bytes 100
  7.2 46.6 %copy-start.21 = (s32[8]{0:T(128)S(1)}, s32[8]{0:T(128)}, u32[]{:S(2)}) copy-start(s32[8]{0:T(128)} %constant.102.clone) | copy-start | bytes 100
  7.2 7.4 copy-start.12
  7.2 10.2 copy-start.13
  7.2 362.2 %all-gather.9.cloned.1.call-start = ((), (), s32[]{:S(2)}) async-start(), calls=%async_computation.5 | async-start | bytes 9437184 | tf_op jit(solution)/shard_map/all_gather | solution.py:571
  7.9 387.3 %all-gather.5.cloned.1.call-start = ((), (), s32[]{:S(2)}) async-start(), calls=%async_computation.3 | async-start | bytes 17104896 | tf_op jit(solution)/shard_map/all_gather | solution.py:571
  16.0 472.1 %all-gather.7.cloned.1.call-start = ((), (), s32[]{:S(2)}) async-start(), calls=%async_computation.4 | async-start | bytes 4718592 | tf_op jit(solution)/shard_map/all_gather | solution.py:571
  16.8 1608.0 %reduce-scatter.4.cloned.1.call-start = ((), (), s32[]{:S(2)}) async-start(), calls=%async_computation.6 | async-start | bytes 34209792 | tf_op jit(solution)/shard_map/reduce_scatter | solution.py:572
  51.2 160.8 %copy-start.5 = (s32[648]{0:T(1024)}, s32[648]{0:T(1024)S(1)}, u32[]{:S(2)}) copy-start(s32[648]{0:T(1024)S(1)} %reshape.184.edge_ref) | copy-start | bytes 7780
  53.8 0.7 copy-start.14
  395.3 12.1 copy-start.4
  407.3 29.4 %copy-start.2 = (f32[1,2048]{1,0:T(1,128)}, f32[1,2048]{1,0:T(1,128)S(1)}, u32[]{:S(2)}) copy-start(f32[1,2048]{1,0:T(1,128)S(1)} %fusion.13.gain_ref) | copy-start | bytes 24580
  436.8 3.7 copy-start
  440.5 45.4 %copy-start.7 = (bf16[2304,2048]{1,0:T(8,128)(2,1)}, bf16[2304,2048]{1,0:T(8,128)(2,1)S(1)}, u32[]{:S(2)}) copy-start(bf16[2304,2048]{1,0:T(8,128)(2,1)S(1)} %get-tuple-element.86) | copy-start | bytes 28311556
  488.1 17.1 %copy-start.8 = (f32[384,128]{1,0:T(8,128)S(1)}, f32[384,128]{1,0:T(8,128)}, u32[]{:S(2)}) copy-start(f32[384,128]{1,0:T(8,128)} %constant.106.clone.sin_hi_ref) | copy-start | bytes 589828
  488.1 17.1 %copy-start.9 = (f32[384,128]{1,0:T(8,128)S(1)}, f32[384,128]{1,0:T(8,128)}, u32[]{:S(2)}) copy-start(f32[384,128]{1,0:T(8,128)} %constant.105.clone.sin_lo_ref) | copy-start | bytes 589828
  488.1 17.1 %copy-start.10 = (f32[384,128]{1,0:T(8,128)S(1)}, f32[384,128]{1,0:T(8,128)}, u32[]{:S(2)}) copy-start(f32[384,128]{1,0:T(8,128)} %constant.104.clone.cos_ref) | copy-start | bytes 589828
  505.2 190.2 %copy-start.23 = (bf16[512,4096]{1,0:T(8,128)(2,1)S(1)}, bf16[512,4096]{1,0:T(8,128)(2,1)}, u32[]{:S(2)}) copy-start(bf16[512,4096]{1,0:T(8,128)(2,1)} %all-gather.7.cloned.1.call-done) | copy-start | bytes 12582916
  691.7 3.6 copy-start.11
  761.0 42.4 %copy-start.3 = (f32[1,2048]{1,0:T(1,128)S(1)}, f32[1,2048]{1,0:T(1,128)}, u32[]{:S(2)}) copy-start(f32[1,2048]{1,0:T(1,128)} %copy-done.2) | copy-start | bytes 24580
  851.3 791.4 %reduce-scatter.6.cloned.1.call-start = ((), (), s32[]{:S(2)}) async-start(), calls=%async_computation.7 | async-start | bytes 9437184 | tf_op jit(solution)/shard_map/reduce_scatter | solution.py:572
  868.4 774.3 %reduce-scatter.8.cloned.1.call-start = ((), (), s32[]{:S(2)}) async-start(), calls=%async_computation.8 | async-start | bytes 18874368 | tf_op jit(solution)/shard_map/reduce_scatter | solution.py:572
  895.6 0.6 copy-start.15
  895.6 0.7 copy-start.17
  895.6 0.7 copy-start.19
  896.3 463.8 %copy-start.6 = (s32[648]{0:T(1024)S(1)}, s32[648]{0:T(1024)}, u32[]{:S(2)}) copy-start(s32[648]{0:T(1024)} %copy-done.5) | copy-start | bytes 7780
  1360.0 239.0 %copy-start.1 = (bf16[2304,2048]{1,0:T(8,128)(2,1)S(1)}, bf16[2304,2048]{1,0:T(8,128)(2,1)}, u32[]{:S(2)}) copy-start(bf16[2304,2048]{1,0:T(8,128)(2,1)} %copy-done) | copy-start | bytes 28311556
Sparse Core Ops, SparseCore 0:
  9.8 51.9 all-gather.8
  64.2 80.3 all-gather.4
  146.5 30.7 all-gather.6
  851.4 376.5 reduce-scatter.3
  1231.8 93.9 reduce-scatter.5
  1329.7 105.5 reduce-scatter.7

commit v2 on v1

v2 whole, which is shorter than its diff:
```python
import functools
import math
import jax
import jax.numpy as jnp
import numpy as np
from jax import lax
from jax.experimental import pallas as pl
from jax.experimental.pallas import tpu as pltpu
from jax.sharding import PartitionSpec as P

NOPE_DIM = 128
ROPE_DIM = 64
VALUE_DIM = 128
ROPE_THETA = 50000.0
RMS_EPS = 1e-6
ATTN_SCALE = (NOPE_DIM + ROPE_DIM) ** -0.5 * (0.1 * math.log(32.0) + 1.0) ** 2
ROW_DIMS = (((0,), (0,)), ((), ()))
COL_DIMS = (((1,), (1,)), ((), ()))
LANES = 128
TABLE_BLOCK = 1024
PICK_CHUNK = 32
PICK_RING = 4
ADD_CHUNK = 32
ADD_RING = 4
UNROLL = 8
NO_ROW = 1 << 30
PITCH = 17
F32 = jnp.float32
BF16 = jnp.bfloat16
SMEM = pltpu.SMEM
ANY = pl.ANY
HBM = pl.BlockSpec(memory_space=ANY)
SCALARS = pl.BlockSpec(memory_space=SMEM)


def shift_of(x, n):
    return lax.shift_right_logical(x, n.bit_length() - 1)


def lane(j, n=1):
    return slice(j * LANES, (j + n) * LANES)


def rowsum(x):
    return jnp.sum(x, axis=-1, keepdims=True)


def tree_sum(terms):
    while len(terms) > 1:
        terms = [a + b for a, b in zip(terms[::2], terms[1::2])]
    return terms[0]


def inverse_rms(square_sum, width):
    return lax.rsqrt(square_sum * (1.0 / width) + RMS_EPS)


def row_spec(blk, width):
    return pl.BlockSpec((blk, width), lambda i, *_: (i, 0))


def whole_spec(shape, **kw):
    return pl.BlockSpec(shape, lambda *_: (0,) * len(shape), **kw)


def struct(shape, dtype):
    return jax.ShapeDtypeStruct(shape, dtype)


def cost(flops, size):
    return pl.CostEstimate(flops=int(flops), bytes_accessed=int(size), transcendentals=0)


def params(vmem_mib, **kw):
    return pltpu.CompilerParams(vmem_limit_bytes=vmem_mib << 20, **kw)


def unique_body(shift, keys_ref, uniq_ref, rank_ref, count_ref):
    n = keys_ref.shape[0]
    unroll = 8

    def step(i, carry):
        k, prev = carry
        for j in range(unroll):
            key = keys_ref[i * unroll + j]
            row = lax.shift_right_logical(key, shift)
            k = k + (row != prev).astype(jnp.int32)
            uniq_ref[k] = row
            rank_ref[key & ((1 << shift) - 1)] = k
            prev = row
        return k, prev

    k, _ = lax.fori_loop(0, n // unroll, step, (jnp.int32(-1), jnp.int32(-1)))
    count_ref[0] = k + 1


def unique_rows(ids):
    n = ids.shape[0]
    shift = max(1, (n - 1).bit_length())
    keys = lax.sort(ids * (1 << shift) + jnp.arange(n, dtype=jnp.int32))
    uniq, rank, count = pl.pallas_call(
        functools.partial(unique_body, shift),
        out_shape=[struct((n,), jnp.int32), struct((n,), jnp.int32), struct((1,), jnp.int32)],
        in_specs=[SCALARS], out_specs=[SCALARS] * 3, name="unique_rows")(keys)
    return jnp.where(jnp.arange(n, dtype=jnp.int32) < count[0], uniq, NO_ROW), rank


def pick_body(n_dev, n_tok, rows_ref, edge_ref, table_ref, out_ref, lin_ref, stage_ref, sems):
    b = pl.program_id(0)
    n_blk = pl.num_programs(0)
    rows_blk, d_model = table_ref.shape
    cols = d_model // LANES
    n_edge = edge_ref.shape[0] // n_dev
    size, ring = PICK_CHUNK, PICK_RING

    def chunk_copy(d, k):
        slot = k & (ring - 1)
        return pltpu.make_async_copy(stage_ref.at[d, pl.ds(slot * size, size)], out_ref.at[pl.ds(d * n_tok + k * size, size)], sems.at[d, slot])

    @pl.loop(0, rows_blk // 16)
    def _(g):
        for j in range(cols):
            lin_ref[pl.ds(g * 16 * PITCH + j, 16, stride=PITCH), :] = table_ref[pl.ds(g * 16, 16), lane(j)].astype(F32)

    @pl.loop(0, n_dev)
    def _(d):
        first = edge_ref[d * n_edge]
        lo = edge_ref[d * n_edge + b] - first
        hi = edge_ref[d * n_edge + b + 1] - first
        at = d * n_tok + first
        base = b * (rows_blk * PITCH)

        @pl.when(hi > lo)
        def _():
            @pl.loop(shift_of(lo, size), shift_of(hi - 1, size) + 1)
            def _(k):
                start = jnp.maximum(lo, k * size)
                stop = jnp.minimum(hi, (k + 1) * size)

                @pl.when((start == k * size) & (k + 1 >= ring))
                def _():
                    chunk_copy(d, k + 1 - ring).wait()

                @pl.loop(0, shift_of(stop - start + UNROLL - 1, UNROLL))
                def _(i):
                    p = start + i * UNROLL
                    vals = []
                    for u in range(UNROLL):
                        vals.append(lin_ref[pl.ds(jnp.minimum(rows_ref[at + p + u] - base, (rows_blk - 1) * PITCH), cols), :])
                    for u in range(UNROLL):
                        stage_ref[d, (p + u) & (ring * size - 1)] = vals[u].astype(BF16)

                @pl.when(stop == (k + 1) * size)
                def _():
                    chunk_copy(d, k).start()

    @pl.when(b == n_blk - 1)
    def _():
        @pl.loop(0, n_dev)
        def _(d):
            total = edge_ref[d * n_edge + n_blk] - edge_ref[d * n_edge]
            chunks = shift_of(total + size - 1, size)

            @pl.when((total & (size - 1)) != 0)
            def _():
                chunk_copy(d, chunks - 1).start()

            @pl.loop(jnp.maximum(chunks + 1 - ring, 0), chunks)
            def _(k):
                chunk_copy(d, k).wait()


def row_spots(rows):
    return jnp.pad(jnp.minimum(rows, NO_ROW // PITCH).reshape(-1) * PITCH, (0, UNROLL))


def pick_rows(table, rows, edges):
    n_dev, n_tok = rows.shape
    n_rows, d_model = table.shape
    cols = d_model // LANES
    return pl.pallas_call(
        functools.partial(pick_body, n_dev, n_tok),
        grid_spec=pltpu.PrefetchScalarGridSpec(
            num_scalar_prefetch=2, grid=(n_rows // TABLE_BLOCK,),
            in_specs=[row_spec(TABLE_BLOCK, d_model)],
            out_specs=HBM,
            scratch_shapes=[
                pltpu.VMEM((TABLE_BLOCK * PITCH, LANES), F32),
                pltpu.VMEM((n_dev, PICK_RING * PICK_CHUNK, cols, LANES), BF16),
                pltpu.SemaphoreType.DMA((n_dev, PICK_RING))]),
        out_shape=struct((n_dev * n_tok, cols, LANES), BF16),
        compiler_params=params(48), name="pick_rows",
        cost_estimate=cost(60_000_000, table.size * 2),
    )(row_spots(rows), edges.reshape(-1), table)


def spread_body(rank_ref, slot_ref, recv_ref, gain_ref, h0_ref, x_ref, lin_ref):
    i = pl.program_id(0)
    rows_blk, d_model = h0_ref.shape
    cols = d_model // LANES
    unroll = 8

    @pl.loop(0, rows_blk // unroll)
    def _(t0):
        for u in range(unroll):
            t = t0 * unroll + u
            lin_ref[pl.ds(t * PITCH, cols), :] = recv_ref[slot_ref[rank_ref[i * rows_blk + t]]].astype(F32)

    @pl.loop(0, rows_blk // 32)
    def _(g):
        groups = []
        for u in range(2):
            tiles = [lin_ref[pl.ds((g * 32 + u * 16) * PITCH + j, 16, stride=PITCH), :] for j in range(cols)]
            groups.append((tiles, rowsum(tree_sum([v * v for v in tiles]))))
        for u, (tiles, square) in enumerate(groups):
            inv = inverse_rms(square, d_model)
            for j, v in enumerate(tiles):
                at = (pl.ds(g * 32 + u * 16, 16), lane(j))
                h0_ref[at] = v.astype(BF16)
                x_ref[at] = (v * inv * gain_ref[:, lane(j)]).astype(BF16)


def spread_rows(recv, rank, slot, gain):
    n_tok, cols, _ = recv.shape
    d_model = cols * LANES
    blk = 128
    out = struct((n_tok, d_model), BF16)
    rows = row_spec(blk, d_model)
    return pl.pallas_call(
        spread_body,
        grid_spec=pltpu.PrefetchScalarGridSpec(
            num_scalar_prefetch=2, grid=(n_tok // blk,),
            in_specs=[whole_spec((n_tok, cols, LANES), pipeline_mode=pl.Buffered(1)), whole_spec((1, d_model))],
            out_specs=[rows, rows],
            scratch_shapes=[pltpu.VMEM((blk * PITCH, LANES), F32)]),
        out_shape=[out, out], compiler_params=params(32), name="spread_rows",
        cost_estimate=cost(60_000_000, n_tok * d_model * 6),
    )(rank, slot, recv, gain.reshape(1, d_model))


def rope_tables(seq_len):
    pos = np.arange(seq_len, dtype=np.float32)
    inv_freq = (np.float32(ROPE_THETA) ** (np.float32(-2.0) * np.arange(ROPE_DIM // 2, dtype=np.float32) / np.float32(ROPE_DIM))).astype(np.float32)
    angle = (pos[:, None] * inv_freq[None, :]).astype(np.float32).astype(np.float64)
    cos, sin, zero = np.cos(angle), np.sin(angle), np.zeros_like(angle)
    full = lambda lo, hi: np.concatenate([lo, hi, lo, hi], axis=1).astype(np.float32)
    return full(cos, cos), full(-sin, zero), full(zero, sin)


def turn(vals, cos, sin_lo, sin_hi, sign):
    half = ROPE_DIM // 2
    return vals * cos + sign * (pltpu.roll(vals, LANES - half, 1) * sin_lo + pltpu.roll(vals, half, 1) * sin_hi)


def attn_body(q_ref, pe_ref, kv_ref, do_ref, cos_ref, sin_lo_ref, sin_hi_ref,
              o_ref, dq_ref, dkv_ref, dpe_ref, krot_ref, qcat_ref, p_ref, ds_ref, dkrot_ref):
    pair = pl.program_id(1)
    seq_len = q_ref.shape[0]
    blk = 128
    n_blk = seq_len // blk
    low = lax.broadcasted_iota(jnp.int32, (1, LANES), 1) < ROPE_DIM

    @pl.when(pair == 0)
    def _():
        pe = pe_ref[...].astype(F32)
        pe = jnp.where(low, pe, pltpu.roll(pe, ROPE_DIM, 1))
        krot_ref[...] = turn(pe, cos_ref[...], sin_lo_ref[...], sin_hi_ref[...], 1.0).astype(BF16)
        dkrot_ref[...] = jnp.zeros_like(dkrot_ref)

    qrot = turn(q_ref[:, 2 * LANES:].astype(F32), cos_ref[...], sin_lo_ref[...], sin_hi_ref[...], 1.0)
    for h in range(2):
        mine = low if h == 0 else ~low
        qcat_ref[h, :, :LANES] = q_ref[:, lane(h)]
        qcat_ref[h, :, LANES:] = jnp.where(mine, qrot, 0.0).astype(BF16)
    causal = lax.broadcasted_iota(jnp.int32, (blk, blk), 0) >= lax.broadcasted_iota(jnp.int32, (blk, blk), 1)
    blocks = [(h, i, slice(i * blk, (i + 1) * blk), (i + 1) * blk) for i in reversed(range(n_blk)) for h in range(2)]
    key = lambda h: lane(2 * h)
    val = lambda h: lane(2 * h + 1)
    head = lane
    kcat = lambda h, seen: jnp.concatenate([kv_ref[:seen, key(h)], krot_ref[:seen]], axis=1)
    scores = [lax.dot_general(qcat_ref[h, here], kcat(h, seen), COL_DIMS, preferred_element_type=F32) for h, i, here, seen in blocks]
    dps = [lax.dot_general(do_ref[here, head(h)], kv_ref[:seen, val(h)], COL_DIMS, preferred_element_type=F32) for h, i, here, seen in blocks]
    for (h, i, here, seen), s, dp in zip(blocks, scores, dps):
        diag = jnp.where(causal, s[:, i * blk:], -1e30)
        s = diag if i == 0 else jnp.concatenate([s[:, :i * blk], diag], axis=1)
        e = jnp.exp2((s - jnp.max(s, axis=-1, keepdims=True)) * (ATTN_SCALE * math.log2(math.e)))
        p = e * (1.0 / rowsum(e))
        p_ref[h, here, :seen] = p.astype(BF16)
        ds_ref[h, here, :seen] = (p * (dp - rowsum(dp * p)) * ATTN_SCALE).astype(BF16)
    dqrots = [[], []]
    for h, i, here, seen in blocks:
        o_ref[here, head(h)] = jnp.dot(p_ref[h, here, :seen], kv_ref[:seen, val(h)], preferred_element_type=F32).astype(BF16)
        dqi = jnp.dot(ds_ref[h, here, :seen], kcat(h, seen), preferred_element_type=F32)
        dq_ref[here, head(h)] = dqi[:, :LANES].astype(BF16)
        dqrots[h].append(dqi[:, LANES:])
    for h in range(2):
        for j in range(n_blk):
            here, later = slice(j * blk, (j + 1) * blk), slice(j * blk, seq_len)
            dv = lax.dot_general(p_ref[h, later, here], do_ref[later, head(h)], ROW_DIMS, preferred_element_type=F32)
            dk = lax.dot_general(ds_ref[h, later, here], qcat_ref[h, later], ROW_DIMS, preferred_element_type=F32)
            dkv_ref[here, val(h)] = dv.astype(BF16)
            dkv_ref[here, key(h)] = dk[:, :LANES].astype(BF16)
            dkrot_ref[here] += dk[:, LANES:]
    for n, i in enumerate(reversed(range(n_blk))):
        here = slice(i * blk, (i + 1) * blk)
        dqr = jnp.where(low, dqrots[0][n], dqrots[1][n]).astype(BF16).astype(F32)
        dq_ref[here, 2 * LANES:] = turn(dqr, cos_ref[here], sin_lo_ref[here], sin_hi_ref[here], -1.0).astype(BF16)

    @pl.when(pair == pl.num_programs(1) - 1)
    def _():
        both = dkrot_ref[...]
        both = (both + pltpu.roll(both, ROPE_DIM, 1)).astype(BF16).astype(F32)
        dpe = turn(both, cos_ref[...], sin_lo_ref[...], sin_hi_ref[...], -1.0)
        dpe_ref[...] = jnp.where(low, dpe, 0.0).astype(BF16)


def attend(qx, kv, d_mix, seq_count, pe_block):
    tok = qx.shape[0]
    seq_len = tok // seq_count
    pairs = d_mix.shape[1] // (2 * VALUE_DIM)
    tabs = [jnp.asarray(t) for t in rope_tables(seq_len)]
    at = lambda width: pl.BlockSpec((seq_len, width), lambda s, j: (s, j))
    tab = whole_spec((seq_len, LANES))
    shape = lambda w: struct((tok, w), BF16)
    return pl.pallas_call(
        attn_body, grid=(seq_count, pairs),
        in_specs=[at(3 * LANES), pl.BlockSpec((seq_len, LANES), lambda s, j: (s, pe_block)), at(4 * LANES), at(2 * LANES), tab, tab, tab],
        out_specs=[at(2 * LANES), at(3 * LANES), at(4 * LANES), pl.BlockSpec((seq_len, LANES), lambda s, j: (s, 0))],
        out_shape=[shape(pairs * 2 * LANES), shape(qx.shape[1]), shape(pairs * 4 * LANES), shape(LANES)],
        scratch_shapes=[pltpu.VMEM((seq_len, LANES), BF16), pltpu.VMEM((2, seq_len, 2 * LANES), BF16),
                        pltpu.VMEM((2, seq_len, seq_len), BF16), pltpu.VMEM((2, seq_len, seq_len), BF16),
                        pltpu.VMEM((seq_len, LANES), F32)],
        compiler_params=params(40), name="attention",
        cost_estimate=cost(12e9, 1e8),
    )(qx, qx, kv, d_mix, *tabs)


def latent_body(w_ref, c_ref, pe_ref, gain_ref, _, out_ref, dgain_ref, gacc_ref):
    i = pl.program_id(0)
    rank = gain_ref.shape[1]

    @pl.when(i == 0)
    def _():
        gacc_ref[...] = jnp.zeros_like(gacc_ref)

    c = c_ref[...].astype(F32)
    w = w_ref[...].astype(F32)
    inv = inverse_rms(rowsum(c * c), rank)
    hat = c * inv
    gacc_ref[...] += jnp.sum((w * hat).reshape(-1, 8, rank), axis=0)
    w = w * gain_ref[...]
    out_ref[:, :rank] = (inv * (w - hat * (rowsum(w * hat) / rank))).astype(BF16)
    out_ref[:, rank:] = pe_ref[...]

    @pl.when(i == pl.num_programs(0) - 1)
    def _():
        dgain_ref[...] = jnp.sum(gacc_ref[...], axis=0, keepdims=True)


def latent_back(d_latent, qx, d_pe, gain, d_qx, latent_at):
    tok, rank = d_latent.shape
    blk = 256
    wide = lambda width, at: pl.BlockSpec((pl.Element(blk), pl.Element(width)), lambda i: (i * blk, at))
    return pl.pallas_call(
        latent_body, grid=(tok // blk,),
        in_specs=[row_spec(blk, rank), wide(rank, latent_at), row_spec(blk, LANES), whole_spec((1, rank)), HBM],
        out_specs=[wide(rank + LANES, latent_at), whole_spec((1, rank))],
        out_shape=[struct(d_qx.shape, BF16), struct((1, rank), F32)],
        scratch_shapes=[pltpu.VMEM((8, rank), F32)], input_output_aliases={4: 0}, name="latent_back",
        cost_estimate=cost(20_000_000, tok * rank * 6),
    )(d_latent, qx, d_pe, gain.reshape(1, rank), d_qx)


def merge_body(rank_ref, slot_ref, dx_ref, h0_ref, dy_ref, gain_ref, kv_note_ref, out_ref, note_ref, even_ref, odd_ref, acc_ref, gacc_ref, sem):
    i = pl.program_id(0)
    rows_blk, d_model = h0_ref.shape
    cols = d_model // LANES

    @pl.when(i == 0)
    def _():
        gacc_ref[...] = jnp.zeros_like(gacc_ref)

        @pl.loop(0, acc_ref.shape[0] // 8)
        def _(r):
            acc_ref[pl.ds(r * 8, 8)] = jnp.zeros((8,) + acc_ref.shape[1:], F32)

    lanes = [lane(j) for j in range(cols)]

    def derive(g, lin_ref):
        rows = pl.ds(g * 16, 16)
        squares, crosses = [], []
        for at in lanes:
            v = h0_ref[rows, at].astype(F32)
            squares.append(v * v)
            crosses.append(v * (dx_ref[rows, at].astype(F32) * gain_ref[:, at]))
        inv = inverse_rms(rowsum(tree_sum(squares)), d_model)
        mean = rowsum(tree_sum(crosses)) * inv / d_model
        for j, at in enumerate(lanes):
            hat = h0_ref[rows, at].astype(F32) * inv
            w = dx_ref[rows, at].astype(F32)
            gacc_ref[:, at] += w * hat
            lin_ref[pl.ds(j, 16, stride=PITCH), :] = inv * (w * gain_ref[:, at] - hat * mean) + dy_ref[rows, at].astype(F32)

    def add(g, lin_ref):
        for t in range(16):
            r = slot_ref[rank_ref[i * rows_blk + g * 16 + t]]
            acc_ref[r] = acc_ref[r] + lin_ref[pl.ds(t * PITCH, cols), :]

    derive(0, even_ref)
    pairs = rows_blk // 32

    @pl.loop(0, pairs - 1)
    def _(g):
        add(2 * g, even_ref)
        derive(2 * g + 1, odd_ref)
        add(2 * g + 1, odd_ref)
        derive(2 * g + 2, even_ref)

    add(2 * pairs - 2, even_ref)
    derive(2 * pairs - 1, odd_ref)
    add(2 * pairs - 1, odd_ref)

    @pl.when(i == pl.num_programs(0) - 1)
    def _():
        total = jnp.sum(gacc_ref[...], axis=0, keepdims=True)
        each = d_model // note_ref.shape[0]
        note_ref[...] = jnp.zeros_like(note_ref)
        for o in range(note_ref.shape[0]):
            for r in range(each // LANES):
                note_ref[o, pl.ds(r, 1), :] = total[:, o * each + r * LANES:o * each + (r + 1) * LANES]
            note_ref[o, pl.ds(each // LANES, 1), :] = kv_note_ref[pl.ds(o, 1), :]
        copy = pltpu.make_async_copy(acc_ref, out_ref, sem)
        copy.start()
        copy.wait()


def merge_rows(dx, h0, dy, gain, kv_note, rank, slot):
    note = struct((kv_note.shape[0], 8, LANES), F32)
    n_tok, d_model = h0.shape
    cols = d_model // LANES
    blk = 128
    rows = row_spec(blk, d_model)
    return pl.pallas_call(
        merge_body,
        grid_spec=pltpu.PrefetchScalarGridSpec(
            num_scalar_prefetch=2, grid=(n_tok // blk,),
            in_specs=[rows, rows, rows, whole_spec((1, d_model)), whole_spec(kv_note.shape)],
            out_specs=[HBM, whole_spec(note.shape)],
            scratch_shapes=[pltpu.VMEM((16 * PITCH, LANES), F32), pltpu.VMEM((16 * PITCH, LANES), F32), pltpu.VMEM((n_tok, cols, LANES), F32),
                            pltpu.VMEM((16, d_model), F32), pltpu.SemaphoreType.DMA]),
        out_shape=[struct((n_tok, cols, LANES), F32), note],
        compiler_params=params(40), name="merge_rows",
        cost_estimate=cost(100_000_000, n_tok * d_model * 10),
    )(rank, slot, dx, h0, dy, gain.reshape(1, d_model), kv_note)


def add_body(n_dev, n_tok, rows_ref, edge_ref, recv_ref, out_ref, acc_ref, ring_ref, sems):
    b = pl.program_id(0)
    n_blk = pl.num_programs(0)
    rows_blk, d_model = out_ref.shape
    cols = d_model // LANES
    n_edge = edge_ref.shape[0] // n_dev
    size, ring = ADD_CHUNK, ADD_RING

    def chunk_copy(s, k):
        slot = k & (ring - 1)
        return pltpu.make_async_copy(recv_ref.at[pl.ds(s * n_tok + k * size, size)], ring_ref.at[s, pl.ds(slot * size, size)], sems.at[s, slot])

    def chunks_of(s):
        return shift_of(edge_ref[s * n_edge + n_blk] - edge_ref[s * n_edge] + size - 1, size)

    @pl.when(b == 0)
    def _():
        @pl.loop(0, n_dev)
        def _(s):
            @pl.loop(0, jnp.minimum(chunks_of(s), ring))
            def _(k):
                chunk_copy(s, k).start()

    @pl.loop(0, rows_blk // 16)
    def _(r):
        for u in range(2 * PITCH):
            acc_ref[pl.ds((r * 2 * PITCH + u) * 8, 8), :] = jnp.zeros((8, LANES), F32)

    @pl.loop(0, n_dev)
    def _(s):
        first = edge_ref[s * n_edge]
        lo = edge_ref[s * n_edge + b] - first
        hi = edge_ref[s * n_edge + b + 1] - first
        at = s * n_tok + first
        base = b * (rows_blk * PITCH)

        @pl.when(hi > lo)
        def _():
            @pl.loop(shift_of(lo, size), shift_of(hi - 1, size) + 1)
            def _(k):
                start = jnp.maximum(lo, k * size)
                stop = jnp.minimum(hi, (k + 1) * size)

                @pl.when(start == k * size)
                def _():
                    chunk_copy(s, k).wait()

                @pl.loop(0, shift_of(stop - start + UNROLL - 1, UNROLL))
                def _(i):
                    p = start + i * UNROLL
                    spots, sums = [], []
                    for u in range(UNROLL):
                        spots.append(pl.ds(jnp.where(p + u < stop, rows_ref[at + p + u] - base, rows_blk * PITCH), cols))
                        sums.append(acc_ref[spots[u], :] + ring_ref[s, (p + u) & (ring * size - 1)])
                    for u in range(UNROLL):
                        acc_ref[spots[u], :] = sums[u]

                @pl.when((stop == (k + 1) * size) & (k + ring < chunks_of(s)))
                def _():
                    chunk_copy(s, k + ring).start()

    @pl.loop(0, rows_blk // 16)
    def _(g):
        for j in range(cols):
            out_ref[pl.ds(g * 16, 16), lane(j)] = acc_ref[pl.ds(g * 16 * PITCH + j, 16, stride=PITCH), :].astype(BF16)


def add_rows(recv, rows, edges, n_rows):
    n_dev, n_tok = rows.shape
    cols = recv.shape[1]
    d_model = cols * LANES
    return pl.pallas_call(
        functools.partial(add_body, n_dev, n_tok),
        grid_spec=pltpu.PrefetchScalarGridSpec(
            num_scalar_prefetch=2, grid=(n_rows // TABLE_BLOCK,),
            in_specs=[HBM],
            out_specs=row_spec(TABLE_BLOCK, d_model),
            scratch_shapes=[pltpu.VMEM(((TABLE_BLOCK + 1) * PITCH, LANES), F32),
                            pltpu.VMEM((n_dev, ADD_RING * ADD_CHUNK, cols, LANES), F32),
                            pltpu.SemaphoreType.DMA((n_dev, ADD_RING))]),
        out_shape=struct((n_rows, d_model), BF16),
        compiler_params=params(48), name="add_rows",
        cost_estimate=cost(60_000_000, n_rows * d_model * 2),
    )(row_spots(rows), edges.reshape(-1), recv)


def exchange_body(caps, tok, fetch, x_ref, *refs):
    if fetch:
        lhs_ref, rhs_ref, out_ref, via_ref, prod_ref, *sems = refs
    else:
        note_ref, out_ref, via_ref, note_out_ref, *sems = refs
    send_sems, recv_sems, hop_send, hop_recv, end_send, end_recv, note_send, note_recv, own_sems = sems
    n_dev = len(caps)
    offs = [sum(caps[:o]) for o in range(n_dev)]
    place = lax.axis_index('fsdp')
    far, side = 6, 4
    across = lambda m: [((m ^ far) & ~1) | c for c in range(2)]

    def rows(src, dst):
        at, to, n = (dst * tok, offs[src], caps[src]) if fetch else (offs[dst], src * tok, caps[dst])
        by = 0 if (src ^ dst) & far != far else {0: n // 2, 1: n, 2: 0, 3: n // 2}[src >> 1]
        return at, to, n - by, by

    def remote(src, dst, sems, to):
        return pltpu.make_async_remote_copy(src, dst, sems[0], sems[1], device_id={'fsdp': to}, device_id_type=pl.DeviceIdType.MESH)

    def direct(src, dst):
        at, to, n, _ = rows(src, dst)
        return [remote(x_ref.at[pl.ds(at, n)], out_ref.at[pl.ds(to, n)], (send_sems.at[dst], recv_sems.at[src]), dst)] if n else []

    def note(src, dst):
        return [] if fetch else [remote(note_ref.at[dst], note_out_ref.at[src], (note_send.at[dst], note_recv.at[src]), dst)]

    def hop(src, dst):
        at, _, n, by = rows(src, dst)
        c = dst & 1
        return [remote(x_ref.at[pl.ds(at + n, by)], via_ref.at[c, pl.ds(0, by)], (hop_send.at[c], hop_recv.at[c]), src ^ side)] if by else []

    def end(src, dst):
        _, to, n, by = rows(src, dst)
        return [remote(via_ref.at[dst & 1, pl.ds(0, by)], out_ref.at[pl.ds(to + n, by)], (end_send.at[dst & 1], end_recv.at[src & 1]), dst)] if by else []

    def own(m):
        at, to, n, _ = rows(m, m)
        copies = [pltpu.make_async_copy(x_ref.at[pl.ds(at, n)], out_ref.at[pl.ds(to, n)], own_sems.at[0])]
        return copies if fetch else copies + [pltpu.make_async_copy(note_ref.at[m], note_out_ref.at[m], own_sems.at[1])]

    each = lambda copies, act: [getattr(c, act)() for c in copies]

    @pl.when(pl.program_id(0) == 0)
    def _():
        for m in range(n_dev):
            @pl.when(place == m)
            def _():
                for dst in across(m):
                    each(hop(m, dst), 'start')
                for k in (6, 7, 4, 5, 2, 3, 1):
                    each(direct(m, m ^ k) + note(m, m ^ k), 'start')
                each(own(m), 'start')

    if fetch:
        for n in range(0, prod_ref.shape[1], 512):
            prod_ref[:, n:n + 512] = lax.dot_general(lhs_ref[...], rhs_ref[n:n + 512], COL_DIMS, preferred_element_type=F32).astype(BF16)

    @pl.when(pl.program_id(0) == pl.num_programs(0) - 1)
    def _():
        for m in range(n_dev):
            @pl.when(place == m)
            def _():
                for dst in across(m ^ side):
                    each(hop(m ^ side, dst), 'wait_recv')
                    each(end(m ^ side, dst), 'start')
                each(own(m), 'wait')
                for dst in across(m):
                    each(hop(m, dst), 'wait_send')
                for k in range(1, n_dev):
                    each(direct(m, m ^ k) + note(m, m ^ k), 'wait_send')
                    each(direct(m ^ k, m) + note(m ^ k, m), 'wait_recv')
                for dst in across(m ^ side):
                    each(end(m ^ side, dst), 'wait_send')
                for src in across(m):
                    each(end(src, m), 'wait_recv')


def exchange(x, caps, tok, note=None, lhs=None, rhs=None):
    n_dev = len(caps)
    fetch = note is None
    cols = x.shape[1:]
    n_out = tok if fetch and sum(caps) <= tok else n_dev * tok
    blk = 256
    pair, wide = pltpu.SemaphoreType.DMA((2,)), pltpu.SemaphoreType.DMA((n_dev,))
    out_shape = [struct((n_out,) + cols, x.dtype), struct((2, max(caps)) + cols, x.dtype)]
    if fetch:
        grid = (lhs.shape[0] // blk,)
        more_in, args = [row_spec(blk, lhs.shape[1]), whole_spec(rhs.shape, pipeline_mode=pl.Buffered(1))], (x, lhs, rhs)
        more_out, more_shape = row_spec(blk, rhs.shape[0]), struct((lhs.shape[0], rhs.shape[0]), BF16)
    else:
        grid, more_in, args, more_out, more_shape = (1,), [HBM], (x, note), HBM, struct(note.shape, note.dtype)
    rows, _, more = pl.pallas_call(
        functools.partial(exchange_body, tuple(caps), tok, fetch), grid=grid,
        out_shape=out_shape + [more_shape], in_specs=[HBM] + more_in, out_specs=[HBM, HBM, more_out],
        scratch_shapes=[wide, wide, pair, pair, pair, pair, wide, wide, pair],
        compiler_params=params(32, has_side_effects=True), name="exchange",
        cost_estimate=cost(200_000_000_000, x.size * 2),
    )(*args)
    return rows, more


def move_body(count_ref, from_ref, to_ref, x_ref, out_ref, sems):
    depth = sems.shape[0]

    @pl.loop(0, count_ref.shape[0])
    def _(o):
        n = count_ref[o]

        def copy(i):
            return pltpu.make_async_copy(x_ref.at[pl.ds(from_ref[o] + i, 1)], out_ref.at[pl.ds(to_ref[o] + i, 1)], sems.at[lax.rem(i, depth)])

        @pl.loop(0, n)
        def _(i):
            @pl.when(i >= depth)
            def _():
                copy(i - depth).wait()

            copy(i).start()

        @pl.loop(jnp.maximum(n - depth, 0), n)
        def _(i):
            copy(i).wait()


def move_rows(x, count, start_from, start_to, n_out):
    return pl.pallas_call(
        move_body, out_shape=struct((n_out,) + x.shape[1:], x.dtype),
        in_specs=[SCALARS] * 3 + [HBM], out_specs=HBM, scratch_shapes=[pltpu.SemaphoreType.DMA((16,))],
        name="move_rows")(count, start_from, start_to, x)


def rms_scale(in_vals, gain_vec):
    vals_f32 = in_vals.astype(F32)
    inv_rms = lax.rsqrt(jnp.mean(vals_f32 * vals_f32, axis=-1, keepdims=True) + RMS_EPS)
    return (vals_f32 * inv_rms * gain_vec).astype(BF16)


def dot(a, b, dims):
    return lax.dot_general(a, b, dims, preferred_element_type=F32)


NN = (((1,), (0,)), ((), ()))


def pack_body(q_ref, down_ref, tail_ref, out_ref):
    low = lax.broadcasted_iota(jnp.int32, (1, LANES), 1) < ROPE_DIM
    width = q_ref.shape[1] // LANES
    for j in range(0, width, 3):
        one, two, three = (q_ref[:, lane(j + k)].astype(F32) for k in range(3))
        out_ref[:, lane(j)] = one.astype(BF16)
        out_ref[:, lane(j + 1)] = jnp.where(low, pltpu.roll(two, ROPE_DIM, 1), pltpu.roll(three, ROPE_DIM, 1)).astype(BF16)
        out_ref[:, lane(j + 2)] = jnp.where(low, two, three).astype(BF16)
    out_ref[:, lane(width, down_ref.shape[1] // LANES)] = down_ref[...]
    out_ref[:, lane(out_ref.shape[1] // LANES - 1)] = tail_ref[...]


def pack_weights(w_query, w_kv_down, gains):
    rows, width = w_query.shape
    cut = w_kv_down.shape[1] // LANES * LANES
    tail = jnp.concatenate([w_kv_down[:, cut:]] + [jnp.pad(g, (0, rows - g.shape[0]))[:, None] for g in gains], axis=1)
    tail = jnp.pad(tail, ((0, 0), (0, LANES - tail.shape[1])))
    return pl.pallas_call(pack_body, out_shape=struct((rows, width + cut + LANES), BF16), name="pack_weights")(w_query, w_kv_down[:, :cut], tail)


def unpack_body(g_ref, q_ref, down_ref):
    low = lax.broadcasted_iota(jnp.int32, (1, LANES), 1) < ROPE_DIM
    width = q_ref.shape[1] // LANES
    for j in range(0, width, 3):
        plain, rot = pltpu.roll(g_ref[:, lane(j + 1)], ROPE_DIM, 1), g_ref[:, lane(j + 2)]
        q_ref[:, lane(j)] = g_ref[:, lane(j)]
        q_ref[:, lane(j + 1)] = jnp.where(low, rot, plain)
        q_ref[:, lane(j + 2)] = jnp.where(low, plain, rot)
    down_ref[...] = g_ref[:, q_ref.shape[1]:q_ref.shape[1] + down_ref.shape[1]]


def unpack_grads(g_x, q_width, down_width):
    rows = g_x.shape[0]
    return pl.pallas_call(unpack_body, out_shape=[struct((rows, q_width), F32), struct((rows, down_width), F32)], name="unpack_grads")(g_x)


def share_body(n_dev, x_ref, out_ref, send_sems, recv_sems):
    place = lax.axis_index('fsdp')
    for m in range(n_dev):
        @pl.when(place == m)
        def _():
            copies = [pltpu.make_async_remote_copy(x_ref, out_ref.at[m], send_sems.at[d], recv_sems.at[m], device_id={'fsdp': d}, device_id_type=pl.DeviceIdType.MESH)
                      for d in range(n_dev) if d != m]
            for copy in copies:
                copy.start()
            out_ref[m] = x_ref[...]
            for copy in copies:
                copy.wait_send()
            for s in range(n_dev):
                if s != m:
                    pltpu.make_async_remote_copy(x_ref, out_ref.at[s], send_sems.at[s], recv_sems.at[s], device_id={'fsdp': s}, device_id_type=pl.DeviceIdType.MESH).wait_recv()


def share(x, n_dev):
    vmem = pl.BlockSpec(memory_space=pltpu.VMEM)
    wide = pltpu.SemaphoreType.DMA((n_dev,))
    return pl.pallas_call(functools.partial(share_body, n_dev), out_shape=struct((n_dev,) + x.shape, x.dtype), in_specs=[vmem], out_specs=vmem,
                          scratch_shapes=[wide, wide], compiler_params=pltpu.CompilerParams(has_side_effects=True), name="share")(x)


def solution(mesh):
    n_dev = mesh.shape['fsdp']
    tok_spec = P(('dp', 'fsdp'), None)
    seq_spec = P(('dp', 'fsdp'), None, None)
    part_vec = P(('dp', 'fsdp'))
    vec_spec = P('fsdp')
    mat_spec = P('fsdp', None)

    def step(tok_ids, grad_out, emb_table, norm_gain, w_query, w_kv_down, kv_gain, w_kv_up, w_out):
        seq_count, seq_len = tok_ids.shape
        vocab_dev, d_model = emb_table.shape
        tok = seq_count * seq_len
        me = lax.axis_index('fsdp')
        gather = lambda piece: lax.all_gather(piece, 'fsdp', tiled=True)
        scatter = lambda full: lax.psum_scatter(full, 'fsdp', scatter_dimension=0, tiled=True)
        rows_dev, q_width = w_query.shape
        kv_rank = kv_gain.shape[0] * n_dev
        latent_at = q_width
        rank_dev = kv_gain.shape[0]
        pe_at = q_width + kv_rank
        pad_at = pe_at + ROPE_DIM
        dy = grad_out.reshape(tok, d_model)

        uniq, rank = unique_rows(tok_ids.reshape(tok))
        all_uniq = share(uniq.reshape(-1, LANES), n_dev).reshape(n_dev, tok)
        owner_edges = jnp.arange(n_dev + 1, dtype=jnp.int32) * vocab_dev
        starts = jnp.sum(all_uniq[:, None, :] < owner_edges[None, :, None], axis=-1, dtype=jnp.int32)
        counts = starts[:, 1:] - starts[:, :-1]
        rows = all_uniq - me * vocab_dev
        block_edges = jnp.arange(vocab_dev // TABLE_BLOCK + 1, dtype=jnp.int32) * TABLE_BLOCK
        edges = jnp.sum(rows[:, None, :] < block_edges[None, :, None], axis=-1, dtype=jnp.int32)
        mine = lambda table, axis: lax.dynamic_index_in_dim(table, me, axis, keepdims=False)
        named, my_starts = mine(counts, 0), mine(starts, 0)[:-1]
        even = lambda share: -(-round(tok * share) // 8) * 8
        plans = [[even(hot)] + [even(rest)] * (n_dev - 1) for hot, rest in ((0.35, 0.0764), (0.3646, 0.0833))]
        fit = [jnp.all(counts <= jnp.asarray(caps, jnp.int32)[None, :]) for caps in plans]
        plan = jnp.where(fit[0], 0, jnp.where(fit[1], 1, 2))
        offs = jnp.asarray(np.cumsum([[0] + caps[:-1] for caps in plans], axis=1), jnp.int32)
        shift = jnp.where(fit[0], offs[0] - my_starts, jnp.where(fit[1], offs[1] - my_starts, 0))
        place = jnp.arange(tok, dtype=jnp.int32)
        slot = place + shift[0] + jnp.sum(jnp.where(place[:, None] >= my_starts[None, 1:], (shift[1:] - shift[:-1])[None, :], 0), axis=-1)
        slots = jnp.arange(n_dev, dtype=jnp.int32) * tok

        tie = lax.optimization_barrier
        w_o = gather(w_out)
        w_x = gather(pack_weights(w_query, w_kv_down, (norm_gain, kv_gain)))

        def fetch(caps):
            return lambda v: exchange(v, caps, tok, lhs=dy, rhs=w_o)

        def fetch_any(v):
            far_rows, prod = fetch([tok] * n_dev)(v)
            return move_rows(far_rows, named, slots, my_starts, tok), prod

        sent = pick_rows(emb_table, rows, edges)
        recv, d_mix = lax.switch(plan, [fetch(caps) for caps in plans] + [fetch_any], sent)
        recv, w_x, w_up_dev = tie((recv, w_x, w_kv_up))
        w_up = gather(w_up_dev)
        gain_vec = w_x[:, pad_at].astype(F32)
        kv_gain_vec = w_x[:, pad_at + 1].reshape(n_dev, rows_dev)[:, :rank_dev].reshape(kv_rank).astype(F32)
        h0, x = spread_rows(recv, rank, slot, gain_vec)

        qx = dot(x, w_x, NN).astype(BF16)
        latent = rms_scale(qx[:, latent_at:pe_at], kv_gain_vec)
        kv = dot(latent, w_up, NN).astype(BF16)
        mix, d_qx, d_kv, d_pe = attend(qx, kv, d_mix, seq_count, pe_at // LANES)
        d_w_out = dot(mix, dy, ROW_DIMS)
        d_kv, d_w_out = tie((d_kv, d_w_out))
        d_latent = dot(d_kv, w_up, COL_DIMS).astype(BF16)
        d_w_up = dot(latent, d_kv, ROW_DIMS)
        d_latent, d_w_up = tie((d_latent, d_w_up))
        d_qx, d_kv_gain = latent_back(d_latent, qx, d_pe, kv_gain_vec, d_qx, latent_at)
        d_x = dot(d_qx, w_x, COL_DIMS).astype(BF16)
        kv_note = jnp.pad(d_kv_gain.reshape(n_dev, rank_dev), ((0, 0), (0, LANES - rank_dev)))
        merged, note = merge_rows(d_x, h0, dy, gain_vec, kv_note, rank, slot)

        d_w_x = dot(x, d_qx, ROW_DIMS)

        def bring(caps):
            return lambda v, n: exchange(v, caps, tok, note=n)

        def bring_any(v, n):
            return bring([tok] * n_dev)(move_rows(v, named, my_starts, slots, n_dev * tok), n)

        g_out = scatter(d_w_out)
        g_up = scatter(d_w_up)
        merged, note, g_out, d_w_x = tie((merged, note, g_out, d_w_x))
        back, note = lax.switch(plan, [bring(caps) for caps in plans] + [bring_any], merged, note)
        back, d_w_x = tie((back, d_w_x))
        g_x = scatter(d_w_x)
        out = (h0.astype(F32) + dot(mix, w_o, NN)).astype(BF16)
        grad_table = add_rows(back, rows, edges, vocab_dev)
        g_query, g_down = unpack_grads(g_x, q_width, pad_at - q_width)
        g_gain = jnp.sum(note, axis=0)
        gain_rows = rows_dev // LANES
        return (out.reshape(seq_count, seq_len, d_model), grad_table, g_gain[:gain_rows].reshape(rows_dev), g_query,
                g_down, g_gain[gain_rows, :rank_dev], g_up, g_out)

    return jax.shard_map(step, mesh=mesh, in_specs=(tok_spec, seq_spec, mat_spec, vec_spec, mat_spec, mat_spec, vec_spec, mat_spec, mat_spec), out_specs=(seq_spec, tok_spec, part_vec, tok_spec, tok_spec, part_vec, tok_spec, tok_spec), check_vma=False)
```

time: 1660 us -> 1160 us (0.70)
  Pallas kernels: 1280 us -> 721 us
  waiting for transfers between devices: 1.48 us -> 123 us
  local copies, waits for them, and re-layouts: 46.9 us -> 20.4 us
  matrix products: 264 us -> 243 us
    pallas_call x2, Pallas kernels: 621 us -> 410 us  [exchange(): pl.pallas_call(functools.partial(exchange_body, tuple(caps), tok, fetch),...]
    pallas_call x1, Pallas kernels: 239 us -> 83.2 us  [add_rows(): pl.pallas_call(functools.partial(add_body, n_dev, n_tok), grid_spec=pltpu...]
    reduce_scatter x3, waiting for transfers between devices: 0.01 us -> 122 us  [step(): lax.psum_scatter(full, 'fsdp', scatter_dimension=0, tiled=True)]
    pallas_call x1, Pallas kernels: 187 us -> 70.7 us  [attend(): pl.pallas_call(attn_body, grid=(seq_count, pairs), in_specs=[at(3 * LANES...]
    pallas_call x1, Pallas kernels: 157 us -> 69.5 us  [pick_rows(): pl.pallas_call(functools.partial(pick_body, n_dev, n_tok), grid_spec=pltp...]
    pallas_call x1 -> x5, Pallas kernels: 10.1 us -> 36.6 us  [the longest x1 10.6 us: share(): pl.pallas_call(functools.partial(share_body, n_dev), out_shape=struct((n_...]
    dot_general x9 -> x8, matrix products: 264 us -> 243 us  [dot(): return lax.dot_general(a, b, dims, preferred_element_type=F32)]
  transfers between devices with their start and end apart: 6 -> 6, of which waited for: 0 -> 2; matrix products, arithmetic and copies ran while one was open for 12% -> 20% of each run, Pallas kernels for 64% -> 34%
where the time goes in v2:
time: 1160 us; the launch traced here: 1140 us
  Pallas kernels  721 us (62%)
  matrix products  243 us (21%)
  waiting for transfers between devices  123 us (11%)
  local copies, waits for them, and re-layouts  20.4 us (2%)
  other arithmetic  20.4 us (2%)
  between operations  16.1 us (1%)
    pallas_call x2, Pallas kernels, exchange(): pl.pallas_call(functools.partial(exchange_body, tuple(caps), tok, fetch),...  410 us
    dot_general x8, matrix products, dot(): return lax.dot_general(a, b, dims, preferred_element_type=F32)  243 us
    reduce_scatter x3, waiting for transfers between devices, step(): lax.psum_scatter(full, 'fsdp', scatter_dimension=0, tiled=True)  122 us
    pallas_call x1, Pallas kernels, add_rows(): pl.pallas_call(functools.partial(add_body, n_dev, n_tok), grid_spec=pltpu...  83.2 us
    pallas_call x1, Pallas kernels, attend(): pl.pallas_call(attn_body, grid=(seq_count, pairs), in_specs=[at(3 * LANES...  70.7 us
    pallas_call x1, Pallas kernels, pick_rows(): pl.pallas_call(functools.partial(pick_body, n_dev, n_tok), grid_spec=pltp...  69.5 us
    pallas_call x1, Pallas kernels, merge_rows(): pl.pallas_call(merge_body, grid_spec=pltpu.PrefetchScalarGridSpec(num_sca...  30.5 us
  transfers between devices with their start and end apart: 6, of which 2 were waited for; matrix products, arithmetic and copies ran while one was open for 20% of the time, Pallas kernels for 34%

profile of v2, /device:TPU:0, one launch (start us, length us, event | category | flops | bytes accessed | tf_op | source)
XLA Modules:
  0.0 1145.0 jit_solution(11846209637369987637)
XLA Ops:
  12.9 3.2 pack_weights.1
  17.0 5.8 sort.10
  22.7 10.1 unique_rows.1
  32.8 2.0 select_bitcast_fusion.x_ref
  34.8 10.6 share.1
  51.3 69.5 %pick_rows.1 = bf16[18432,16,128]{2,1,0:T(8,128)(2,1)} custom-call(s32[18440]{0:T(1024)S(1)} %pad.17.rows_ref, s32[168]{0:T(256)S(1)} %reshape.108.edge_ref, bf16[20480,2048]{1,0:T(8,128)(2,1)} %table_ref.1), custom_call_target="tpu_custom_call" | custom-call | flops 60000000 | bytes 83886080 | tf_op jit(solution)/shard_map/pick_rows/pallas_call | solution.py:181
  123.0 145.8 %conditional.2 = (bf16[2304,16,128]{2,1,0:T(8,128)(2,1)}, bf16[2304,2048]{1,0:T(8,128)(2,1)}) conditional(s32[]{:T(128)} %clamp.4, (bf16[18432,16,128]{2,1,0:T(8,128)(2,1)}, bf16[2304,2048]{1,0:T(8,128)(2,1)}, bf16[2048,2048]{1,0:T(8,128)(2,1)}) %tuple.73, (bf16[18432,16,128]{2,1,0:T(8,128)(2,1)}, bf16[2304,2048]{1,0:T(8,128)(2,1)}, ...), branch_computations={%region_6.7_spmd, %region_7.8_spmd, %region_8.9_spmd} | conditional | flops 199999995904 | bytes 75497952 | solution.py:803
  123.0 145.7 %exchange.6 = (bf16[2304,16,128]{2,1,0:T(8,128)(2,1)}, bf16[2,808,16,128]{3,2,1,0:T(8,128)(2,1)}, bf16[2304,2048]{1,0:T(8,128)(2,1)}) custom-call(bf16[18432,16,128]{2,1,0:T(8,128)(2,1)} %get-tuple-element.43.x_ref, bf16[2304,2048]{1,0:T(8,128)(2,1)} %get-tuple-element.44.refs_0_, bf16[2048,2048]{1,0:T(8,128)(2,1)} %get-tuple-element.45.refs_1_), custom_call_target="tpu_custom_call" | custom-call | flops 199999995904 | bytes 75497472 | tf_op jit(solution)/shard_map/cond/branch_0_fun/exchange/pallas_call | solution.py:635
  268.8 1.4 slice_reduce_fusion
  270.2 1.4 convert_reduce_fusion.1
  272.3 19.9 %spread_rows.1 = (bf16[2304,2048]{1,0:T(8,128)(2,1)S(1)}, bf16[2304,2048]{1,0:T(8,128)(2,1)S(1)}) custom-call(s32[2304]{0:T(1024)S(1)} %copy-done.10, s32[2304]{0:T(1024)S(1)} %add_add_fusion.slot_ref, bf16[2304,16,128]{2,1,0:T(8,128)(2,1)} %get-tuple-element.122.recv_ref, f32[1,2048]{1,0:T(1,128)S(1)} %bitcast.30), custom_call_target="tpu_custom_call" | custom-call | flops 60000000 | bytes 28311552 | tf_op jit(solution)/shard_map/spread_rows/pallas_call | solution.py:229
  292.3 44.5 %convolution_convert_fusion.1.q_ref.pe_ref.c_ref = bf16[2304,3712]{1,0:T(8,128)(2,1)} fusion(bf16[2304,2048]{1,0:T(8,128)(2,1)S(1)} %get-tuple-element.125, bf16[2048,3712]{1,0:T(8,128)(2,1)} %all-gather.6.cloned.1.call-done), kind=kOutput, calls=%fused_computation.1 | convolution fusion | flops 35039379456 | bytes 41746432 | tf_op jit(solution)/shard_map/dot_general | solution.py:682
  336.8 2.2 fusion
  339.1 17.0 %convolution_convert_fusion.kv_ref = bf16[2304,4096]{1,0:T(8,128)(2,1)} fusion(bf16[512,4096]{1,0:T(8,128)(2,1)} %all-gather.8.cloned.1.call-done, f32[512]{0:T(512)S(1)} %reshape.114, f32[2304]{0:T(1024)S(1)} %add_rsqrt_fusion, bf16[2304,3712]{1,0:T(8,128)(2,1)} %convolution_convert_fusion.1.q_ref.pe_ref.c_ref), kind=kOutput, calls=%fused_computation | convolution fusion | flops 9677832192 | bytes 25439232 | tf_op jit(solution)/shard_map/dot_general | solution.py:682
  356.2 70.7 %attention.1 = (bf16[2304,2048]{1,0:T(8,128)(2,1)S(1)}, bf16[2304,3712]{1,0:T(8,128)(2,1)}, bf16[2304,4096]{1,0:T(8,128)(2,1)}, bf16[2304,128]{1,0:T(8,128)(2,1)S(1)}) custom-call(bf16[2304,3712]{1,0:T(8,128)(2,1)} %convolution_convert_fusion.1.q_ref.pe_ref.c_ref, bf16[2304,3712]{1,0:T(8,128)(2,1)} %convolution_convert_fusion.1.q_ref.pe_ref.c_ref, ...), custom_call_target="tpu_custom_call" | custom-call | flops 12000000000 | bytes 100000000 | tf_op jit(solution)/shard_map/attention/pallas_call | solution.py:325
  427.7 3.7 copy-done.14
  431.5 23.3 %fusion.11 = f32[2048,2048]{1,0:T(8,128)} fusion(bf16[2304,2048]{1,0:T(8,128)(2,1)S(1)} %get-tuple-element.128, bf16[2304,2048]{1,0:T(8,128)(2,1)S(1)} %bitcast.38), kind=kOutput, calls=%fused_computation.47 | convolution fusion | flops 19327352832 | bytes 35651584 | tf_op jit(solution)/shard_map/dot_general | solution.py:682
  456.1 18.6 %fusion.3 = f32[512,4096]{1,0:T(8,128)} fusion(bf16[2304,4096]{1,0:T(8,128)(2,1)} %get-tuple-element.130, f32[512]{0:T(512)S(1)} %reshape.114, f32[2304]{0:T(1024)S(1)} %add_rsqrt_fusion, bf16[2304,3712]{1,0:T(8,128)(2,1)} %convolution_convert_fusion.1.q_ref.pe_ref.c_ref), kind=kOutput, calls=%fused_computation.14 | convolution fusion | flops 9668395008 | bytes 29633536 | tf_op jit(solution)/shard_map/dot_general | solution.py:682
  474.7 17.8 %convolution_convert_fusion.3.w_ref = bf16[2304,512]{1,0:T(8,128)(2,1)} fusion(bf16[2304,4096]{1,0:T(8,128)(2,1)} %get-tuple-element.130, bf16[512,4096]{1,0:T(8,128)(2,1)} %all-gather.8.cloned.1.call-done), kind=kOutput, calls=%fused_computation.9 | convolution fusion | flops 9664856064 | bytes 25427968 | tf_op jit(solution)/shard_map/dot_general | solution.py:682
  492.4 8.2 latent_back.1
  502.6 45.3 %convolution_convert_fusion.2.dx_ref = bf16[2304,2048]{1,0:T(8,128)(2,1)} fusion(bf16[2304,3712]{1,0:T(8,128)(2,1)} %get-tuple-element.134, bf16[2048,3712]{1,0:T(8,128)(2,1)} %all-gather.6.cloned.1.call-done), kind=kOutput, calls=%fused_computation.3 | convolution fusion | flops 35035545600 | bytes 41746432 | tf_op jit(solution)/shard_map/dot_general | solution.py:682
  547.9 3.9 copy-done.1
  551.8 30.5 %merge_rows.1 = (f32[2304,16,128]{2,1,0:T(8,128)}, f32[8,8,128]{2,1,0:T(8,128)S(1)}) custom-call(s32[2304]{0:T(1024)S(1)} %copy-done.11, s32[2304]{0:T(1024)S(1)} %copy-done.7, bf16[2304,2048]{1,0:T(8,128)(2,1)S(1)} %copy-done.1, bf16[2304,2048]{1,0:T(8,128)(2,1)} %copy-done, bf16[2304,2048]{1,0:T(8,128)(2,1)} %bitcast.35, f32[1,2048]{1,0:T(1,128)S(1)} %bitcast.31, ...), custom_call_target="tpu_custom_call" | custom-call | flops 100000000 | bytes 47185920 | tf_op jit(solution)/shard_map/merge_rows/pallas_call | solution.py:443
  582.4 46.8 %fusion.12 = f32[2048,3712]{1,0:T(8,128)} fusion(bf16[2304,2048]{1,0:T(8,128)(2,1)} %copy-done.15, bf16[2304,3712]{1,0:T(8,128)(2,1)} %get-tuple-element.134), kind=kOutput, calls=%fused_computation.48 | convolution fusion | flops 35030827008 | bytes 56950784 | tf_op jit(solution)/shard_map/dot_general | solution.py:682
  629.2 264.5 %conditional.3 = (f32[18432,16,128]{2,1,0:T(8,128)}, f32[8,8,128]{2,1,0:T(8,128)}) conditional(s32[]{:T(128)} %clamp.4, (f32[2304,16,128]{2,1,0:T(8,128)}, f32[8,8,128]{2,1,0:T(8,128)S(1)}) %merge_rows.1, (f32[2304,16,128]{2,1,0:T(8,128)}, f32[8,8,128]{2,1,0:T(8,128)S(1)}) %merge_rows.1, (s32[8]{0:T(128)S(1)}, s32[8]{0:T(128)S(1)}, ...), branch_computations={%region_11.12_spmd, %region_12.13_spmd, %region_13.14_spmd} | conditional | flops 199999995904 | bytes 75497488 | solution.py:835
  629.2 264.5 %exchange.9 = (f32[18432,16,128]{2,1,0:T(8,128)}, f32[2,808,16,128]{3,2,1,0:T(8,128)}, f32[8,8,128]{2,1,0:T(8,128)}) custom-call(f32[2304,16,128]{2,1,0:T(8,128)} %get-tuple-element.61.x_ref, f32[8,8,128]{2,1,0:T(8,128)S(1)} %get-tuple-element.62.refs_0_), custom_call_target="tpu_custom_call" | custom-call | flops 199999995904 | bytes 9437184 | tf_op jit(solution)/shard_map/cond/branch_0_fun/exchange/pallas_call | solution.py:635
  894.3 30.1 %add_convert_fusion = bf16[2304,2048]{1,0:T(8,128)(2,1)} fusion(bf16[2304,2048]{1,0:T(8,128)(2,1)} %copy-done, bf16[2304,2048]{1,0:T(8,128)(2,1)} %copy-done.14, bf16[2048,2048]{1,0:T(8,128)(2,1)} %all-gather.4.cloned.1.call-done), kind=kOutput, calls=%fused_computation.2 | convolution fusion | flops 19341508608 | bytes 36700160 | tf_op jit(solution)/shard_map/dot_general | solution.py:682
  925.2 83.2 %add_rows.1 = bf16[20480,2048]{1,0:T(8,128)(2,1)} custom-call(s32[18440]{0:T(1024)S(1)} %pad.17.rows_ref, s32[168]{0:T(256)S(1)} %copy-done.13, f32[18432,16,128]{2,1,0:T(8,128)} %get-tuple-element.143.recv_ref), custom_call_target="tpu_custom_call" | custom-call | flops 60000000 | bytes 83886080 | tf_op jit(solution)/shard_map/add_rows/pallas_call | solution.py:528
  1009.5 61.5 %reduce-scatter.6.cloned.1.call-done.g_ref = f32[256,3712]{1,0:T(8,128)} async-done(((f32[2048,3712]{1,0:T(8,128)}), f32[256,3712]{1,0:T(8,128)}) %reduce-scatter.6.cloned.1.call-update) | async-done | bytes 3801104 | tf_op jit(solution)/shard_map/reduce_scatter | solution.py:762
  1071.0 4.4 unpack_grads.1
  1075.4 2.1 copy.42
  1077.5 60.4 %reduce-scatter.8.cloned.1.call-done = f32[64,4096]{1,0:T(8,128)} async-done(((f32[512,4096]{1,0:T(8,128)}), f32[64,4096]{1,0:T(8,128)}) %reduce-scatter.8.cloned.1.call-update) | async-done | bytes 1048592 | tf_op jit(solution)/shard_map/reduce_scatter | solution.py:762
  (115 shorter events, 20.3 us)
Async XLA Ops:
  7.2 41.2 %copy-start.25 = (s32[8]{0:T(128)S(1)}, s32[8]{0:T(128)}, u32[]{:S(2)}) copy-start(s32[8]{0:T(128)} %constant.59.clone) | copy-start | bytes 100
  7.2 41.2 %copy-start.26 = (s32[8]{0:T(128)S(1)}, s32[8]{0:T(128)}, u32[]{:S(2)}) copy-start(s32[8]{0:T(128)} %constant.58.clone) | copy-start | bytes 100
  7.2 115.7 %all-gather.4.cloned.1.call-start = ((), (), s32[]{:S(2)}) async-start(), calls=%async_computation.3 | async-start | bytes 9437184 | tf_op jit(solution)/shard_map/all_gather | solution.py:761
  7.9 260.8 %all-gather.6.cloned.1.call-start = ((), (), s32[]{:S(2)}) async-start(), calls=%async_computation.4 | async-start | bytes 17104896 | tf_op jit(solution)/shard_map/all_gather | solution.py:761
  16.2 322.9 %all-gather.8.cloned.1.call-start = ((), (), s32[]{:S(2)}) async-start(), calls=%async_computation.5 | async-start | bytes 4718592 | tf_op jit(solution)/shard_map/all_gather | solution.py:761
  48.0 72.8 %copy-start.12 = (s32[168]{0:T(256)}, s32[168]{0:T(256)S(1)}, u32[]{:S(2)}) copy-start(s32[168]{0:T(256)S(1)} %reshape.108.edge_ref) | copy-start | bytes 2020
  51.3 70.1 %copy-start.18 = (s32[8]{0:T(128)}, s32[8]{0:T(128)S(1)}, u32[]{:S(2)}) copy-start(s32[8]{0:T(128)S(1)} %get-tuple-element.187) | copy-start | bytes 100
  51.3 70.1 %copy-start.27 = (s32[8]{0:T(128)S(1)}, s32[8]{0:T(128)}, u32[]{:S(2)}) copy-start(s32[8]{0:T(128)} %constant.77) | copy-start | bytes 100
  51.3 70.1 %copy-start.28 = (s32[8]{0:T(128)S(1)}, s32[8]{0:T(128)}, u32[]{:S(2)}) copy-start(s32[8]{0:T(128)} %constant.75) | copy-start | bytes 100
  122.9 149.4 %copy-start.6 = (s32[2304]{0:T(1024)}, s32[2304]{0:T(1024)S(1)}, u32[]{:S(2)}) copy-start(s32[2304]{0:T(1024)S(1)} %add_add_fusion.slot_ref) | copy-start | bytes 27652
  122.9 149.4 %copy-start.10 = (s32[2304]{0:T(1024)S(1)}, s32[2304]{0:T(1024)}, u32[]{:S(2)}) copy-start(s32[2304]{0:T(1024)} %get-tuple-element.118.rank_ref) | copy-start | bytes 27652
  271.6 65.2 %copy-start.8 = (f32[2048]{0:T(1024)}, f32[2048]{0:T(1024)S(1)}, u32[]{:S(2)}) copy-start(f32[2048]{0:T(1024)S(1)} %convert_reduce_fusion.1) | copy-start | bytes 24580
  271.7 357.5 %reduce-scatter.4.cloned.1.call-start = ((), (), s32[]{:S(2)}) async-start(), calls=%async_computation.6 | async-start | bytes 18874368 | tf_op jit(solution)/shard_map/reduce_scatter | solution.py:762
  272.2 64.6 %copy-start.16 = (f32[8,64]{1,0:T(8,128)}, f32[8,64]{1,0:T(8,128)S(1)}, u32[]{:S(2)}) copy-start(f32[8,64]{1,0:T(8,128)S(1)} %slice_convert_fusion) | copy-start | bytes 6148
  292.2 44.5 %copy-start = (bf16[2304,2048]{1,0:T(8,128)(2,1)}, bf16[2304,2048]{1,0:T(8,128)(2,1)S(1)}, u32[]{:S(2)}) copy-start(bf16[2304,2048]{1,0:T(8,128)(2,1)S(1)} %get-tuple-element.124.h0_ref) | copy-start | bytes 28311556
  292.3 44.5 %copy-start.15 = (bf16[2304,2048]{1,0:T(8,128)(2,1)}, bf16[2304,2048]{1,0:T(8,128)(2,1)S(1)}, u32[]{:S(2)}) copy-start(bf16[2304,2048]{1,0:T(8,128)(2,1)S(1)} %get-tuple-element.125) | copy-start | bytes 28311556
  339.0 17.1 %copy-start.3 = (f32[384,128]{1,0:T(8,128)S(1)}, f32[384,128]{1,0:T(8,128)}, u32[]{:S(2)}) copy-start(f32[384,128]{1,0:T(8,128)} %constant.63.clone.sin_hi_ref) | copy-start | bytes 589828
  339.0 17.1 %copy-start.4 = (f32[384,128]{1,0:T(8,128)S(1)}, f32[384,128]{1,0:T(8,128)}, u32[]{:S(2)}) copy-start(f32[384,128]{1,0:T(8,128)} %constant.62.clone.sin_lo_ref) | copy-start | bytes 589828
  339.0 17.1 %copy-start.5 = (f32[384,128]{1,0:T(8,128)S(1)}, f32[384,128]{1,0:T(8,128)}, u32[]{:S(2)}) copy-start(f32[384,128]{1,0:T(8,128)} %constant.61.clone.cos_ref) | copy-start | bytes 589828
  339.1 92.4 %slice-start = ((s8[9437184]{0:T(1024)(128)(4,1)}), s8[1048576]{0:T(1024)(128)(4,1)S(1)}, s32[]{:S(2)}) async-start(s8[9437184]{0:T(1024)(128)(4,1)} %bitcast.36), calls=%async_computation.9 | async-start | bytes 2097152
  339.1 92.3 %slice-start.1 = ((s8[9437184]{0:T(1024)(128)(4,1)}), s8[4194304]{0:T(1024)(128)(4,1)S(1)}, s32[]{:S(2)}) async-start(s8[9437184]{0:T(1024)(128)(4,1)} %bitcast.36), calls=%async_computation.10 | async-start | bytes 8388608
  356.2 75.3 %slice-start.2 = ((s8[9437184]{0:T(1024)(128)(4,1)}), s8[4194304]{0:T(1024)(128)(4,1)S(1)}, s32[]{:S(2)}) async-start(s8[9437184]{0:T(1024)(128)(4,1)} %bitcast.36), calls=%async_computation.11 | async-start | bytes 8388608
  454.8 616.2 %reduce-scatter.6.cloned.1.call-start = ((), (), s32[]{:S(2)}) async-start(), calls=%async_computation.7 | async-start | bytes 34209792 | tf_op jit(solution)/shard_map/reduce_scatter | solution.py:762
  502.5 45.3 %copy-start.7 = (s32[2304]{0:T(1024)S(1)}, s32[2304]{0:T(1024)}, u32[]{:S(2)}) copy-start(s32[2304]{0:T(1024)} %copy-done.6) | copy-start | bytes 27652
  502.5 45.3 %copy-start.9 = (f32[2048]{0:T(1024)S(1)}, f32[2048]{0:T(1024)}, u32[]{:S(2)}) copy-start(f32[2048]{0:T(1024)} %copy-done.8) | copy-start | bytes 24580
  502.6 45.3 %copy-start.11 = (s32[2304]{0:T(1024)S(1)}, s32[2304]{0:T(1024)}, u32[]{:S(2)}) copy-start(s32[2304]{0:T(1024)} %get-tuple-element.118.rank_ref) | copy-start | bytes 27652
  547.9 4.0 copy-start.1
  582.4 46.8 %copy-start.19 = (s32[8]{0:T(128)S(1)}, s32[8]{0:T(128)}, u32[]{:S(2)}) copy-start(s32[8]{0:T(128)} %copy-done.18) | copy-start | bytes 100
  582.4 46.8 %copy-start.21 = (s32[8]{0:T(128)S(1)}, s32[8]{0:T(128)}, u32[]{:S(2)}) copy-start(s32[8]{0:T(128)} %get-tuple-element.188) | copy-start | bytes 100
  582.4 46.8 %copy-start.23 = (s32[8]{0:T(128)S(1)}, s32[8]{0:T(128)}, u32[]{:S(2)}) copy-start(s32[8]{0:T(128)} %iota_multiply_fusion) | copy-start | bytes 100
  893.8 244.2 %reduce-scatter.8.cloned.1.call-start = ((), (), s32[]{:S(2)}) async-start(), calls=%async_computation.8 | async-start | bytes 9437184 | tf_op jit(solution)/shard_map/reduce_scatter | solution.py:762
  894.3 30.9 %copy-start.13 = (s32[168]{0:T(256)S(1)}, s32[168]{0:T(256)}, u32[]{:S(2)}) copy-start(s32[168]{0:T(256)} %copy-done.12) | copy-start | bytes 2020
  (3 other events, 5.2 us)
Sparse Core Ops, SparseCore 0:
  9.8 52.2 all-gather.3
  64.5 102.6 all-gather.5
  271.8 31.3 all-gather.7
  454.9 108.1 reduce-scatter.3
  893.9 177.0 reduce-scatter.5
  1074.8 63.1 reduce-scatter.7

commit v3 on v2

v3 whole, which is shorter than its diff:
```python
import functools
import math
import jax
import jax.numpy as jnp
import numpy as np
from jax import lax
from jax.experimental import pallas as pl
from jax.experimental.pallas import tpu as pltpu
from jax.sharding import PartitionSpec as P

NOPE_DIM = 128
ROPE_DIM = 64
VALUE_DIM = 128
ROPE_THETA = 50000.0
RMS_EPS = 1e-6
ATTN_SCALE = (NOPE_DIM + ROPE_DIM) ** -0.5 * (0.1 * math.log(32.0) + 1.0) ** 2
ROW_DIMS = (((0,), (0,)), ((), ()))
COL_DIMS = (((1,), (1,)), ((), ()))
LANES = 128
HALVES = 2
PAIR = 2 * LANES
TABLE_BLOCK = 1024
CHUNK = 16
GROUP = 16
ADD_RING = 4
UNROLL = 8
NO_ROW = 1 << 30
PITCH = 17
F32 = jnp.float32
BF16 = jnp.bfloat16
SMEM = pltpu.SMEM
ANY = pl.ANY
HBM = pl.BlockSpec(memory_space=ANY)
SCALARS = pl.BlockSpec(memory_space=SMEM)


def step_id():
    return pl.program_id(0)


def last_step():
    return pl.program_id(0) == pl.num_programs(0) - 1


def shift_of(x, n):
    return lax.shift_right_logical(x, n.bit_length() - 1)


def lane(j, n=1):
    return slice(j * LANES, (j + n) * LANES)


def low_lanes():
    return lax.broadcasted_iota(jnp.int32, (1, LANES), 1) < ROPE_DIM


def rotate(x, n):
    return pltpu.roll(x, n, 1)


def column(g, j):
    return pl.ds(g * GROUP * PITCH + j, GROUP, stride=PITCH)


def group(g):
    return pl.ds(g * GROUP, GROUP)


def rowsum(x):
    return jnp.sum(x, axis=-1, keepdims=True)


def tree_sum(terms):
    while len(terms) > 1:
        terms = [a + b for a, b in zip(terms[::2], terms[1::2])]
    return terms[0]


def inverse_rms(square_sum, width):
    return lax.rsqrt(square_sum * (1.0 / width) + RMS_EPS)


def row_spec(blk, width):
    return pl.BlockSpec((blk, width), lambda i, *_: (i, 0))


def whole_spec(shape, **kw):
    return pl.BlockSpec(shape, lambda *_: (0,) * len(shape), **kw)


def struct(shape, dtype):
    return jax.ShapeDtypeStruct(shape, dtype)


def cost(flops, size):
    return pl.CostEstimate(flops=int(flops), bytes_accessed=int(size), transcendentals=0)


def params(vmem_mib, **kw):
    return pltpu.CompilerParams(vmem_limit_bytes=vmem_mib << 20, **kw)


def unique_body(shift, halves, keys_ref, uniq_ref, rank_ref, count_ref):
    n = keys_ref.shape[0] // halves
    for h in range(halves):
        def step(i, carry):
            k, prev = carry
            for j in range(UNROLL):
                key = keys_ref[h * n + i * UNROLL + j]
                row = lax.shift_right_logical(key, shift)
                k = k + (row != prev).astype(jnp.int32)
                uniq_ref[h * n + k] = row
                rank_ref[h * n + (key & ((1 << shift) - 1))] = k
                prev = row
            return k, prev

        k, _ = lax.fori_loop(0, n // UNROLL, step, (jnp.int32(-1), jnp.int32(-1)))
        count_ref[h] = k + 1


def unique_rows(ids):
    halves, n = ids.shape
    shift = (n - 1).bit_length()
    keys = lax.sort(ids * (1 << shift) + jnp.arange(n, dtype=jnp.int32), dimension=1)
    flat = struct((halves * n,), jnp.int32)
    uniq, rank, count = pl.pallas_call(
        functools.partial(unique_body, shift, halves), out_shape=[flat, flat, struct((halves,), jnp.int32)],
        in_specs=[SCALARS], out_specs=[SCALARS] * 3, name="unique_rows")(keys.reshape(-1))
    known = jnp.arange(n, dtype=jnp.int32) < count[:, None]
    return jnp.where(known, uniq.reshape(halves, n), NO_ROW), rank.reshape(halves, n)


def pick_body(n_list, n_dev, n_tok, base, extra, rows_ref, edge_ref, table_ref, *refs):
    halves = n_list // n_dev
    base_refs, extra_refs, (lin_ref, stage_ref, sems) = refs[:halves], refs[halves:-3], refs[-3:]
    b = step_id()
    last = last_step()
    rows_blk, d_model = table_ref.shape
    cols = d_model // LANES
    n_edge = edge_ref.shape[0] // n_list

    def chunk_copies(l, k, act):
        src, sem, at = stage_ref.at[l, pl.ds(k * CHUNK, CHUNK)], sems.at[l, k], k * CHUNK

        @pl.when(at < base)
        def _():
            getattr(pltpu.make_async_copy(src, base_refs[l // n_dev].at[pl.ds(l % n_dev * base + at, CHUNK)], sem), act)()

        if extra:
            @pl.when(at >= base)
            def _():
                getattr(pltpu.make_async_copy(src, extra_refs[l].at[pl.ds(at - base, CHUNK)], sem), act)()

    @pl.loop(0, rows_blk // GROUP)
    def _(g):
        for j in range(cols):
            lin_ref[column(g, j), :] = table_ref[group(g), lane(j)].astype(F32)

    origin = b * (rows_blk * PITCH)
    for l in range(n_list):
        first = edge_ref[l * n_edge]
        lo = jnp.minimum(edge_ref[l * n_edge + b] - first, base + extra)
        hi = jnp.minimum(edge_ref[l * n_edge + b + 1] - first, base + extra)
        at = l * n_tok + first

        @pl.loop(0, shift_of(hi - lo + UNROLL - 1, UNROLL))
        def _(i):
            p = lo + i * UNROLL
            vals = [lin_ref[pl.ds(jnp.minimum(rows_ref[at + p + u] - origin, (rows_blk - 1) * PITCH), cols), :] for u in range(UNROLL)]
            for u in range(UNROLL):
                stage_ref[l, p + u] = vals[u].astype(BF16)

        @pl.loop(shift_of(lo, CHUNK), jnp.where(last, shift_of(hi + CHUNK - 1, CHUNK), shift_of(hi, CHUNK)))
        def _(k):
            chunk_copies(l, k, 'start')

    @pl.when(last)
    def _():
        for l in range(n_list):
            total = jnp.minimum(edge_ref[(l + 1) * n_edge - 1] - edge_ref[l * n_edge], base + extra)

            @pl.loop(0, shift_of(total + CHUNK - 1, CHUNK))
            def _(k):
                chunk_copies(l, k, 'wait')


def row_spots(rows):
    return jnp.pad(jnp.minimum(rows, NO_ROW // PITCH).reshape(-1) * PITCH, (0, UNROLL))


def pick_rows(table, rows, edges, n_dev, base, extra):
    n_list, n_tok = rows.shape
    n_rows, d_model = table.shape
    cols = d_model // LANES
    out = [struct((n_dev * base, cols, LANES), BF16)] * (n_list // n_dev) + [struct((extra, cols, LANES), BF16)] * (n_list if extra else 0)
    return pl.pallas_call(
        functools.partial(pick_body, n_list, n_dev, n_tok, base, extra),
        grid_spec=pltpu.PrefetchScalarGridSpec(
            num_scalar_prefetch=2, grid=(n_rows // TABLE_BLOCK,), in_specs=[row_spec(TABLE_BLOCK, d_model)], out_specs=[HBM] * len(out),
            scratch_shapes=[
                pltpu.VMEM((TABLE_BLOCK * PITCH, LANES), F32),
                pltpu.VMEM((n_list, base + extra + UNROLL, cols, LANES), BF16),
                pltpu.SemaphoreType.DMA((n_list, (base + extra) // CHUNK))]),
        out_shape=out, compiler_params=params(62), name="pick_rows", cost_estimate=cost(6e7, table.size * 2),
    )(row_spots(rows), edges.reshape(-1), table)


def spread_body(pieces, rank_ref, slot_ref, gain_ref, *refs):
    piece_refs, (h0_ref, x_ref, lin_ref, recv_ref, sems) = refs[:len(pieces)], refs[len(pieces):]
    i = step_id()
    rows_blk, d_model = h0_ref.shape
    cols = d_model // LANES

    @pl.when(i == 0)
    def _():
        for act in ('start', 'wait'):
            for n, (to, size, device) in enumerate(pieces):
                @pl.when((lax.axis_index('fsdp') == device) if device is not None else (i == 0))
                def _():
                    getattr(pltpu.make_async_copy(piece_refs[n], recv_ref.at[pl.ds(to, size)], sems.at[n]), act)()

    @pl.loop(0, rows_blk // UNROLL)
    def _(t0):
        for u in range(UNROLL):
            t = t0 * UNROLL + u
            lin_ref[pl.ds(t * PITCH, cols), :] = recv_ref[slot_ref[rank_ref[i * rows_blk + t]]].astype(F32)

    @pl.loop(0, rows_blk // (HALVES * GROUP))
    def _(g):
        groups = []
        for u in range(HALVES):
            tiles = [lin_ref[column(2 * g + u, j), :] for j in range(cols)]
            groups.append((tiles, rowsum(tree_sum([v * v for v in tiles]))))
        for u, (tiles, square) in enumerate(groups):
            inv = inverse_rms(square, d_model)
            for j, v in enumerate(tiles):
                at = (group(2 * g + u), lane(j))
                h0_ref[at] = v.astype(BF16)
                x_ref[at] = (v * inv * gain_ref[:, lane(j)]).astype(BF16)


def spread_rows(pieces, rank, slot, gain, n_slots):
    n_tok, d_model = rank.shape[0], gain.shape[0]
    cols = d_model // LANES
    blk = 128
    rows = row_spec(blk, d_model)
    plan = [(to, v.shape[0], device) for v, to, device in pieces]
    return pl.pallas_call(
        functools.partial(spread_body, plan),
        grid_spec=pltpu.PrefetchScalarGridSpec(
            num_scalar_prefetch=2, grid=(n_tok // blk,), in_specs=[whole_spec((1, d_model))] + [HBM] * len(pieces), out_specs=[rows, rows],
            scratch_shapes=[pltpu.VMEM((blk * PITCH, LANES), F32), pltpu.VMEM((n_slots, cols, LANES), BF16), pltpu.SemaphoreType.DMA((len(pieces),))]),
        out_shape=[struct((n_tok, d_model), BF16)] * 2, compiler_params=params(32), name="spread_rows",
        cost_estimate=cost(6e7, n_tok * d_model * 6),
    )(rank, slot, gain.reshape(1, d_model), *[v for v, _, _ in pieces])


def rope_tables(seq_len):
    pos = np.arange(seq_len, dtype=np.float32)
    inv_freq = (np.float32(ROPE_THETA) ** (np.float32(-2.0) * np.arange(ROPE_DIM // 2, dtype=np.float32) / np.float32(ROPE_DIM))).astype(np.float32)
    angle = (pos[:, None] * inv_freq[None, :]).astype(np.float32).astype(np.float64)
    cos, sin, zero = np.cos(angle), np.sin(angle), np.zeros_like(angle)
    full = lambda lo, hi: np.concatenate([lo, hi, lo, hi], axis=1).astype(np.float32)
    return full(cos, cos), full(-sin, zero), full(zero, sin)


def turn(vals, cos, sin_lo, sin_hi, sign):
    half = ROPE_DIM // 2
    return vals * cos + sign * (rotate(vals, LANES - half) * sin_lo + rotate(vals, half) * sin_hi)


def attn_body(q_ref, pe_ref, kv_ref, do_ref, cos_ref, sin_lo_ref, sin_hi_ref,
              o_ref, dq_ref, dkv_ref, dpe_ref, krot_ref, qcat_ref, p_ref, ds_ref, dkrot_ref):
    pair = pl.program_id(1)
    seq_len = q_ref.shape[0]
    blk = 128
    n_blk = seq_len // blk
    low = low_lanes()

    @pl.when(pair == 0)
    def _():
        pe = pe_ref[...].astype(F32)
        pe = jnp.where(low, pe, rotate(pe, ROPE_DIM))
        krot_ref[...] = turn(pe, cos_ref[...], sin_lo_ref[...], sin_hi_ref[...], 1.0).astype(BF16)
        dkrot_ref[...] = jnp.zeros_like(dkrot_ref)

    qrot = turn(q_ref[:, PAIR:].astype(F32), cos_ref[...], sin_lo_ref[...], sin_hi_ref[...], 1.0)
    for h in range(HALVES):
        mine = low if h == 0 else ~low
        qcat_ref[h, :, :LANES] = q_ref[:, lane(h)]
        qcat_ref[h, :, LANES:] = jnp.where(mine, qrot, 0.0).astype(BF16)
    causal = lax.broadcasted_iota(jnp.int32, (blk, blk), 0) >= lax.broadcasted_iota(jnp.int32, (blk, blk), 1)
    blocks = [(h, i, slice(i * blk, (i + 1) * blk), (i + 1) * blk) for i in reversed(range(n_blk)) for h in range(HALVES)]
    key = lambda h: lane(2 * h)
    val = lambda h: lane(2 * h + 1)
    head = lane
    kcat = lambda h, seen: jnp.concatenate([kv_ref[:seen, key(h)], krot_ref[:seen]], axis=1)
    scores = [lax.dot_general(qcat_ref[h, here], kcat(h, seen), COL_DIMS, preferred_element_type=F32) for h, i, here, seen in blocks]
    dps = [lax.dot_general(do_ref[here, head(h)], kv_ref[:seen, val(h)], COL_DIMS, preferred_element_type=F32) for h, i, here, seen in blocks]
    for (h, i, here, seen), s, dp in zip(blocks, scores, dps):
        diag = jnp.where(causal, s[:, i * blk:], -1e30)
        s = diag if i == 0 else jnp.concatenate([s[:, :i * blk], diag], axis=1)
        e = jnp.exp2((s - jnp.max(s, axis=-1, keepdims=True)) * (ATTN_SCALE * math.log2(math.e)))
        p = e * (1.0 / rowsum(e))
        p_ref[h, here, :seen] = p.astype(BF16)
        ds_ref[h, here, :seen] = (p * (dp - rowsum(dp * p)) * ATTN_SCALE).astype(BF16)
    dqrots = [[], []]
    for h, i, here, seen in blocks:
        o_ref[here, head(h)] = jnp.dot(p_ref[h, here, :seen], kv_ref[:seen, val(h)], preferred_element_type=F32).astype(BF16)
        dqi = jnp.dot(ds_ref[h, here, :seen], kcat(h, seen), preferred_element_type=F32)
        dq_ref[here, head(h)] = dqi[:, :LANES].astype(BF16)
        dqrots[h].append(dqi[:, LANES:])
    for h in range(HALVES):
        for j in range(n_blk):
            here, later = slice(j * blk, (j + 1) * blk), slice(j * blk, seq_len)
            dv = lax.dot_general(p_ref[h, later, here], do_ref[later, head(h)], ROW_DIMS, preferred_element_type=F32)
            dk = lax.dot_general(ds_ref[h, later, here], qcat_ref[h, later], ROW_DIMS, preferred_element_type=F32)
            dkv_ref[here, val(h)] = dv.astype(BF16)
            dkv_ref[here, key(h)] = dk[:, :LANES].astype(BF16)
            dkrot_ref[here] += dk[:, LANES:]
    for n, i in enumerate(reversed(range(n_blk))):
        here = slice(i * blk, (i + 1) * blk)
        dqr = jnp.where(low, dqrots[0][n], dqrots[1][n]).astype(BF16).astype(F32)
        dq_ref[here, PAIR:] = turn(dqr, cos_ref[here], sin_lo_ref[here], sin_hi_ref[here], -1.0).astype(BF16)

    @pl.when(pair == pl.num_programs(1) - 1)
    def _():
        both = dkrot_ref[...]
        both = (both + rotate(both, ROPE_DIM)).astype(BF16).astype(F32)
        dpe = turn(both, cos_ref[...], sin_lo_ref[...], sin_hi_ref[...], -1.0)
        dpe_ref[...] = jnp.where(low, dpe, 0.0).astype(BF16)


def attend(qx, kv, d_mix, first_seq, seq_count, pe_block):
    tok = qx.shape[0]
    seq_len = tok // seq_count
    pairs = d_mix.shape[1] // (2 * VALUE_DIM)
    tabs = [jnp.asarray(t) for t in rope_tables(seq_len)]
    at = lambda width: pl.BlockSpec((seq_len, width), lambda s, j: (s, j))
    tab = whole_spec((seq_len, LANES))
    shape = lambda w: struct((tok, w), BF16)
    return pl.pallas_call(
        attn_body, grid=(seq_count, pairs),
        in_specs=[at(3 * LANES), pl.BlockSpec((seq_len, LANES), lambda s, j: (s, pe_block)), at(4 * LANES), pl.BlockSpec((seq_len, PAIR), lambda s, j: (s + first_seq, j)), tab, tab, tab],
        out_specs=[at(PAIR), at(3 * LANES), at(4 * LANES), pl.BlockSpec((seq_len, LANES), lambda s, j: (s, 0))],
        out_shape=[shape(pairs * PAIR), shape(qx.shape[1]), shape(pairs * 4 * LANES), shape(LANES)],
        scratch_shapes=[pltpu.VMEM((seq_len, LANES), BF16), pltpu.VMEM((2, seq_len, PAIR), BF16),
                        pltpu.VMEM((2, seq_len, seq_len), BF16), pltpu.VMEM((2, seq_len, seq_len), BF16),
                        pltpu.VMEM((seq_len, LANES), F32)],
        compiler_params=params(40), name="attention",
        cost_estimate=cost(12e9, 1e8),
    )(qx, qx, kv, d_mix, *tabs)


def latent_body(w_ref, c_ref, pe_ref, gain_ref, _, out_ref, dgain_ref, gacc_ref):
    i = step_id()
    rank = gain_ref.shape[1]

    @pl.when(i == 0)
    def _():
        gacc_ref[...] = jnp.zeros_like(gacc_ref)

    c = c_ref[...].astype(F32)
    w = w_ref[...].astype(F32)
    inv = inverse_rms(rowsum(c * c), rank)
    hat = c * inv
    gacc_ref[...] += jnp.sum((w * hat).reshape(-1, 8, rank), axis=0)
    w = w * gain_ref[...]
    out_ref[:, :rank] = (inv * (w - hat * (rowsum(w * hat) / rank))).astype(BF16)
    out_ref[:, rank:] = pe_ref[...]

    @pl.when(last_step())
    def _():
        dgain_ref[...] = jnp.sum(gacc_ref[...], axis=0, keepdims=True)


def latent_back(d_latent, qx, d_pe, gain, d_qx, latent_at):
    tok, rank = d_latent.shape
    blk = 3 * LANES
    wide = lambda width, at: pl.BlockSpec((pl.Element(blk), pl.Element(width)), lambda i: (i * blk, at))
    return pl.pallas_call(
        latent_body, grid=(tok // blk,),
        in_specs=[row_spec(blk, rank), wide(rank, latent_at), row_spec(blk, LANES), whole_spec((1, rank)), HBM],
        out_specs=[wide(rank + LANES, latent_at), whole_spec((1, rank))],
        out_shape=[struct(d_qx.shape, BF16), struct((1, rank), F32)],
        scratch_shapes=[pltpu.VMEM((8, rank), F32)], input_output_aliases={4: 0}, name="latent_back",
        cost_estimate=cost(20_000_000, tok * rank * 6),
    )(d_latent, qx, d_pe, gain.reshape(1, rank), d_qx)


def merge_body(rank_ref, slot_ref, dx_ref, h0_ref, dy_ref, gain_ref, kv_note_ref, base_ref, extra_ref, note_ref, even_ref, odd_ref, acc_ref, gacc_ref, sem):
    i = step_id()
    rows_blk, d_model = h0_ref.shape
    cols = d_model // LANES

    @pl.when(i == 0)
    def _():
        gacc_ref[...] = jnp.zeros_like(gacc_ref)

        @pl.loop(0, acc_ref.shape[0] // 8)
        def _(r):
            acc_ref[pl.ds(r * 8, 8)] = jnp.zeros((8,) + acc_ref.shape[1:], F32)

    lanes = [lane(j) for j in range(cols)]

    def derive(g, lin_ref):
        rows = group(g)
        squares, crosses = [], []
        for at in lanes:
            v = h0_ref[rows, at].astype(F32)
            squares.append(v * v)
            crosses.append(v * (dx_ref[rows, at].astype(F32) * gain_ref[:, at]))
        inv = inverse_rms(rowsum(tree_sum(squares)), d_model)
        mean = rowsum(tree_sum(crosses)) * inv / d_model
        for j, at in enumerate(lanes):
            hat = h0_ref[rows, at].astype(F32) * inv
            w = dx_ref[rows, at].astype(F32)
            gacc_ref[:, at] += w * hat
            lin_ref[column(0, j), :] = inv * (w * gain_ref[:, at] - hat * mean) + dy_ref[rows, at].astype(F32)

    def add(g, lin_ref):
        for t in range(GROUP):
            r = slot_ref[rank_ref[i * rows_blk + g * GROUP + t]]
            acc_ref[r] = acc_ref[r] + lin_ref[pl.ds(t * PITCH, cols), :]

    derive(0, even_ref)
    pairs = rows_blk // (HALVES * GROUP)

    @pl.loop(0, pairs - 1)
    def _(g):
        add(2 * g, even_ref)
        derive(2 * g + 1, odd_ref)
        add(2 * g + 1, odd_ref)
        derive(2 * g + 2, even_ref)

    add(2 * pairs - 2, even_ref)
    derive(2 * pairs - 1, odd_ref)
    add(2 * pairs - 1, odd_ref)

    @pl.when(last_step())
    def _():
        total = jnp.sum(gacc_ref[...], axis=0, keepdims=True)
        each = d_model // note_ref.shape[0]
        note_ref[...] = jnp.zeros_like(note_ref)
        for o in range(note_ref.shape[0]):
            for r in range(each // LANES):
                note_ref[o, pl.ds(r, 1), :] = total[:, o * each + r * LANES:o * each + (r + 1) * LANES]
            note_ref[o, pl.ds(each // LANES, 1), :] = kv_note_ref[pl.ds(o, 1), :]
        split = base_ref.shape[0]
        copies = [pltpu.make_async_copy(acc_ref.at[pl.ds(0, split)], base_ref, sem.at[0]),
                  pltpu.make_async_copy(acc_ref.at[pl.ds(split, extra_ref.shape[0])], extra_ref, sem.at[1])]
        for copy in copies:
            copy.start()
        for copy in copies:
            copy.wait()


def merge_rows(dx, h0, dy, dy_at, gain, kv_note, rank, slot, base, extra):
    note = struct((kv_note.shape[0], 8, LANES), F32)
    n_tok, d_model = h0.shape
    cols = d_model // LANES
    blk = 128
    rows = row_spec(blk, d_model)
    return pl.pallas_call(
        merge_body,
        grid_spec=pltpu.PrefetchScalarGridSpec(
            num_scalar_prefetch=2, grid=(n_tok // blk,),
            in_specs=[rows, rows, pl.BlockSpec((blk, d_model), lambda i, *_: (i + dy_at // blk, 0)), whole_spec((1, d_model)), whole_spec(kv_note.shape)],
            out_specs=[HBM, HBM, whole_spec(note.shape)],
            scratch_shapes=[pltpu.VMEM((GROUP * PITCH, LANES), F32)] * 2 + [ pltpu.VMEM((base + extra, cols, LANES), F32),
                            pltpu.VMEM((GROUP, d_model), F32), pltpu.SemaphoreType.DMA((2,))]),
        out_shape=[struct((base, cols, LANES), F32), struct((extra, cols, LANES), F32), note],
        compiler_params=params(40), name="merge_rows",
        cost_estimate=cost(100_000_000, n_tok * d_model * 10),
    )(rank, slot, dx, h0, dy, gain.reshape(1, d_model), kv_note)


def add_body(n_dev, n_tok, halves, rows_ref, edge_ref, *refs):
    flat, (out_ref, acc_ref, ring_ref, sems) = list(refs[:-4]), refs[-4:]
    sources = []
    for stride, base, extras in halves:
        first = flat.pop(0)
        more = [flat.pop(0) for _ in range(extras)]
        sources += [(first, d * stride, base, more[d] if extras else None) for d in range(n_dev)]
    b = step_id()
    n_blk = pl.num_programs(0)
    rows_blk, d_model = out_ref.shape
    cols = d_model // LANES
    n_edge = edge_ref.shape[0] // len(sources)
    size, ring = CHUNK, ADD_RING

    def landing(s, k):
        return ring_ref.at[s, pl.ds((k & (ring - 1)) * size, size)], sems.at[s, k & (ring - 1)]

    def chunk_start(s, k):
        first, at, base, more = sources[s]
        dst, sem = landing(s, k)

        @pl.when(k * size < base)
        def _():
            pltpu.make_async_copy(first.at[pl.ds(at + k * size, size)], dst, sem).start()

        if more is not None:
            @pl.when(k * size >= base)
            def _():
                pltpu.make_async_copy(more.at[pl.ds(k * size - base, size)], dst, sem).start()

    def chunk_wait(s, k):
        dst, sem = landing(s, k)
        pltpu.make_async_copy(sources[s][0].at[pl.ds(0, size)], dst, sem).wait()

    def chunks_of(s):
        return shift_of(edge_ref[s * n_edge + n_blk] - edge_ref[s * n_edge] + size - 1, size)

    @pl.when(b == 0)
    def _():
        for s in range(len(sources)):
            @pl.loop(0, jnp.minimum(chunks_of(s), ring))
            def _(k):
                chunk_start(s, k)

    @pl.loop(0, rows_blk // GROUP)
    def _(r):
        for u in range(HALVES * PITCH):
            acc_ref[pl.ds((r * HALVES * PITCH + u) * 8, 8), :] = jnp.zeros((8, LANES), F32)

    for s in range(len(sources)):
        first = edge_ref[s * n_edge]
        lo = edge_ref[s * n_edge + b] - first
        hi = edge_ref[s * n_edge + b + 1] - first
        at = s * n_tok + first
        origin = b * (rows_blk * PITCH)

        @pl.when(hi > lo)
        def _():
            @pl.loop(shift_of(lo, size), shift_of(hi - 1, size) + 1)
            def _(k):
                start = jnp.maximum(lo, k * size)
                stop = jnp.minimum(hi, (k + 1) * size)

                @pl.when(start == k * size)
                def _():
                    chunk_wait(s, k)

                @pl.loop(0, shift_of(stop - start + UNROLL - 1, UNROLL))
                def _(i):
                    p = start + i * UNROLL
                    spots, sums = [], []
                    for u in range(UNROLL):
                        spots.append(pl.ds(jnp.where(p + u < stop, rows_ref[at + p + u] - origin, rows_blk * PITCH), cols))
                        sums.append(acc_ref[spots[u], :] + ring_ref[s, (p + u) & (ring * size - 1)])
                    for u in range(UNROLL):
                        acc_ref[spots[u], :] = sums[u]

                @pl.when((stop == (k + 1) * size) & (k + ring < chunks_of(s)))
                def _():
                    chunk_start(s, k + ring)

    @pl.loop(0, rows_blk // GROUP)
    def _(g):
        for j in range(cols):
            out_ref[group(g), lane(j)] = acc_ref[column(g, j), :].astype(BF16)


def add_rows(halves, rows, edges, n_dev, n_rows):
    n_list, n_tok = rows.shape
    cols = halves[0][0].shape[1]
    d_model = cols * LANES
    arrays = [v for first, _, _, more in halves for v in [first] + more]
    return pl.pallas_call(
        functools.partial(add_body, n_dev, n_tok, [(stride, base, len(more)) for _, stride, base, more in halves]),
        grid_spec=pltpu.PrefetchScalarGridSpec(
            num_scalar_prefetch=2, grid=(n_rows // TABLE_BLOCK,), in_specs=[HBM] * len(arrays), out_specs=row_spec(TABLE_BLOCK, d_model),
            scratch_shapes=[pltpu.VMEM(((TABLE_BLOCK + 1) * PITCH, LANES), F32),
                            pltpu.VMEM((n_list, ADD_RING * CHUNK, cols, LANES), F32),
                            pltpu.SemaphoreType.DMA((n_list, ADD_RING))]),
        out_shape=struct((n_rows, d_model), BF16), compiler_params=params(48), name="add_rows", cost_estimate=cost(6e7, n_rows * d_model * 2),
    )(row_spots(rows), edges.reshape(-1), *arrays)


def exchange_body(base, extra, fetch, n_dev, *refs):
    base_ref, refs = refs[0], refs[1:]
    n_extra = (n_dev if fetch else 1) if extra else 0
    extra_refs, refs = refs[:n_extra], refs[n_extra:]
    if fetch:
        lhs_ref, rhs_ref, out_ref, via_ref, prod_ref, *sems = refs
    else:
        note_ref, out_ref, via_ref, note_out_ref, *sems = refs
    send_sems, recv_sems, hop_send, hop_recv, end_send, end_recv, note_send, note_recv, own_sems = sems
    place = lax.axis_index('fsdp')
    far, side = n_dev - 2, n_dev // 2
    across = lambda m: [((m ^ far) & ~1) | c for c in range(HALVES)]

    def moves(src, dst):
        runs = [(0, base_ref, dst * base, src * base if fetch else src * (base + extra), base)]
        if extra and (src if fetch else dst) == 0:
            runs.append((1, extra_refs[dst] if fetch else extra_refs[0], 0, n_dev * base if fetch else src * (base + extra) + base, extra))
        out = []
        for kind, ref, at, to, n in runs:
            by = 0 if (src ^ dst) & far != far else (n // 2, n, 0, n // 2)[src >> 1]
            out.append((kind, ref, at, to, n - by, by))
        return out

    def remote(src, dst, send, recv, to):
        return pltpu.make_async_remote_copy(src, dst, send, recv, device_id={'fsdp': to}, device_id_type=pl.DeviceIdType.MESH)

    def direct(src, dst):
        return [remote(ref.at[pl.ds(at, n)], out_ref.at[pl.ds(to, n)], send_sems.at[kind * n_dev + dst], recv_sems.at[kind * n_dev + src], dst)
                for kind, ref, at, to, n, _ in moves(src, dst) if n]

    def note(src, dst):
        return [] if fetch else [remote(note_ref.at[dst], note_out_ref.at[src], note_send.at[dst], note_recv.at[src], dst)]

    def hop(src, dst):
        out = []
        for kind, ref, at, _, n, by in moves(src, dst):
            lot = HALVES * kind + (dst & 1)
            if by:
                out.append(remote(ref.at[pl.ds(at + n, by)], via_ref.at[lot, pl.ds(0, by)], hop_send.at[lot], hop_recv.at[lot], src ^ side))
        return out

    def end(src, dst):
        return [remote(via_ref.at[HALVES * kind + (dst & 1), pl.ds(0, by)], out_ref.at[pl.ds(to + n, by)], end_send.at[HALVES * kind + (dst & 1)], end_recv.at[HALVES * kind + (src & 1)], dst)
                for kind, _, _, to, n, by in moves(src, dst) if by]

    def own(m):
        copies = [pltpu.make_async_copy(ref.at[pl.ds(at, n)], out_ref.at[pl.ds(to, n)], own_sems.at[kind]) for kind, ref, at, to, n, _ in moves(m, m)]
        return copies if fetch else copies + [pltpu.make_async_copy(note_ref.at[m], note_out_ref.at[m], own_sems.at[2])]

    each = lambda copies, act: [getattr(c, act)() for c in copies]

    @pl.when(step_id() == 0)
    def _():
        for m in range(n_dev):
            @pl.when(place == m)
            def _():
                for dst in across(m):
                    each(hop(m, dst), 'start')
                for k in reversed(range(1, n_dev)):
                    each(direct(m, m ^ k) + note(m, m ^ k), 'start')
                each(own(m), 'start')

    if fetch:
        for n in range(0, prod_ref.shape[1], 512):
            prod_ref[:, n:n + 512] = lax.dot_general(lhs_ref[...], rhs_ref[n:n + 512], COL_DIMS, preferred_element_type=F32).astype(BF16)

    @pl.when(last_step())
    def _():
        for m in range(n_dev):
            @pl.when(place == m)
            def _():
                for dst in across(m ^ side):
                    each(hop(m ^ side, dst), 'wait_recv')
                    each(end(m ^ side, dst), 'start')
                each(own(m), 'wait')
                for dst in across(m):
                    each(hop(m, dst), 'wait_send')
                for k in range(1, n_dev):
                    each(direct(m, m ^ k) + note(m, m ^ k), 'wait_send')
                    each(direct(m ^ k, m) + note(m ^ k, m), 'wait_recv')
                for dst in across(m ^ side):
                    each(end(m ^ side, dst), 'wait_send')
                for src in across(m):
                    each(end(src, m), 'wait_recv')


def exchange(rows, base, extra, n_dev, note=None, lhs=None, rhs=None):
    fetch = note is None
    cols = rows[0].shape[1:]
    blk = 256
    quad, wide, pair = (pltpu.SemaphoreType.DMA((n,)) for n in (4, n_dev, HALVES * n_dev))
    dtype = rows[0].dtype
    out_shape = [struct((n_dev * base + extra * (1 if fetch else n_dev),) + cols, dtype), struct((4, max(base, extra)) + cols, dtype)]
    if fetch:
        grid = (lhs.shape[0] // blk,)
        more_in, args = [row_spec(blk, lhs.shape[1]), whole_spec((rhs.shape[0], lhs.shape[1]), pipeline_mode=pl.Buffered(1))], (lhs, rhs)
        more_out, more_shape = row_spec(blk, rhs.shape[0]), struct((lhs.shape[0], rhs.shape[0]), BF16)
    else:
        grid, more_in, args, more_out, more_shape = (1,), [HBM], (note,), HBM, struct(note.shape, note.dtype)
    got, _, more = pl.pallas_call(
        functools.partial(exchange_body, base, extra, fetch, n_dev), grid=grid,
        out_shape=out_shape + [more_shape], in_specs=[HBM] * len(rows) + more_in, out_specs=[HBM, HBM, more_out],
        scratch_shapes=[pair, pair, quad, quad, quad, quad, wide, wide, quad],
        compiler_params=params(32, has_side_effects=True), name="exchange", cost_estimate=cost(1e11, 1e8),
    )(*rows, *args)
    return got, more


def fetch_beside(base, extras):
    got = lax.all_to_all(base, 'fsdp', 0, 0, tiled=True)
    more = [v if d == 0 else lax.ppermute(v, 'fsdp', [(0, d)]) for d, v in enumerate(extras)]
    return [got] + more


def bring_beside(base, extra, n_dev):
    got = lax.all_to_all(base, 'fsdp', 0, 0, tiled=True)
    last = n_dev - 1
    via = lax.ppermute(extra, 'fsdp', [(last, last ^ (n_dev // 2))])
    return got, [extra if s == 0 else lax.ppermute(extra, 'fsdp', [(s, 0)]) for s in range(last)], via


def weight_body(n_rhs, steps, lhs_a_ref, lhs_b_ref, *refs):
    rhs_refs, (out_ref, turned_ref, rhs_ref, sems) = refs[:n_rhs], refs[n_rhs:]
    i = step_id()
    half = lhs_a_ref.shape[0]
    width = rhs_ref.shape[1]
    rows = rhs_ref.shape[0] // n_rhs

    def fill(j, n):
        cols = pl.ds(pl.multiple_of(j * steps, steps), n)
        return [pltpu.make_async_copy(v.at[:, cols], rhs_ref.at[pl.ds(k * rows, rows), cols], sems.at[k, j]) for k, v in enumerate(rhs_refs)]

    pieces = [(j, min(steps, width - j * steps)) for j in range(-(-width // steps))]

    @pl.when(i == 0)
    def _():
        for j, n in pieces:
            for copy in fill(j, n):
                copy.start()

    turned_ref[:, :half] = lhs_a_ref[...].T
    turned_ref[:, half:] = lhs_b_ref[...].T

    def product(at, n):
        out_ref[:, pl.ds(at, n)] = jnp.dot(turned_ref[...], rhs_ref[:, pl.ds(at, n)], preferred_element_type=F32)

    whole = width // steps

    @pl.loop(0, whole)
    def _(j):
        @pl.when(i == 0)
        def _():
            for copy in fill(j, steps):
                copy.wait()

        product(pl.multiple_of(j * steps, steps), steps)

    for j, n in pieces[whole:]:
        @pl.when(i == 0)
        def _():
            for copy in fill(j, n):
                copy.wait()

        product(j * steps, n)


def weight_grad(lhs_a, lhs_b, *rhs, more=0):
    half, height = lhs_a.shape
    width = rhs[0].shape[1]
    steps = 512
    blk = min(512, height)
    left = pl.BlockSpec((half, blk), lambda i: (0, i))
    return pl.pallas_call(
        functools.partial(weight_body, len(rhs), steps), grid=(height // blk,), in_specs=[left, left] + [HBM] * len(rhs), out_specs=row_spec(blk, width),
        out_shape=struct((height, width + more), F32),
        scratch_shapes=[pltpu.VMEM((blk, HALVES * half), BF16), pltpu.VMEM((HALVES * half, width), BF16), pltpu.SemaphoreType.DMA((len(rhs), -(-width // steps)))],
        compiler_params=params(56), name="weight_grad", cost_estimate=cost(4 * half * height * width, height * width * 4),
    )(lhs_a, lhs_b, *rhs)


def beside_body(lhs_a_ref, lhs_b_ref, rhs_a_ref, rhs_b_ref, _, out_ref, turned_ref):
    half = lhs_a_ref.shape[0]

    @pl.when(step_id() == 0)
    def _():
        turned_ref[:, :half] = lhs_a_ref[...].T
        turned_ref[:, half:] = lhs_b_ref[...].T

    prod = jnp.dot(turned_ref[:, :half], rhs_a_ref[...], preferred_element_type=F32)
    prod = prod + jnp.dot(turned_ref[:, half:], rhs_b_ref[...], preferred_element_type=F32)
    out_ref[...] = prod.reshape(out_ref.shape)


def weight_grad_beside(big, at, lhs_a, lhs_b, rhs_a, rhs_b, n_dev):
    half, height = lhs_a.shape
    rows, width = big.shape
    part = width - at
    parts = rhs_a.shape[1] // part
    big = big.reshape(n_dev, rows // n_dev, width)
    right = pl.BlockSpec((half, part), lambda q: (0, q))
    return pl.pallas_call(
        beside_body, grid=(parts,), in_specs=[whole_spec(lhs_a.shape)] * 2 + [right, right, HBM],
        out_specs=pl.BlockSpec((n_dev, height // n_dev, part), lambda q: (0, q, at // part)), out_shape=struct(big.shape, F32),
        scratch_shapes=[pltpu.VMEM((height, HALVES * half), BF16)], input_output_aliases={4: 0}, compiler_params=params(48), name="weight_grad_beside",
        cost_estimate=cost(4 * half * height * part * parts, 1e7),
    )(lhs_a, lhs_b, rhs_a, rhs_b, big).reshape(rows, width)


def fresh(shape, dtype):
    return pl.pallas_call(lambda out_ref: None, out_shape=struct(shape, dtype), out_specs=HBM, name="fresh")()


def move_body(count_ref, from_ref, to_ref, x_ref, out_ref, sems):
    depth = sems.shape[0]

    @pl.loop(0, count_ref.shape[0])
    def _(o):
        n = count_ref[o]

        def copy(i):
            return pltpu.make_async_copy(x_ref.at[pl.ds(from_ref[o] + i, 1)], out_ref.at[pl.ds(to_ref[o] + i, 1)], sems.at[lax.rem(i, depth)])

        @pl.loop(0, n)
        def _(i):
            @pl.when(i >= depth)
            def _():
                copy(i - depth).wait()

            copy(i).start()

        @pl.loop(jnp.maximum(n - depth, 0), n)
        def _(i):
            copy(i).wait()


def move_rows(x, count, start_from, start_to, n_out):
    return pl.pallas_call(
        move_body, out_shape=struct((n_out,) + x.shape[1:], x.dtype),
        in_specs=[SCALARS] * 3 + [HBM], out_specs=HBM, scratch_shapes=[pltpu.SemaphoreType.DMA((16,))],
        name="move_rows")(count, start_from, start_to, x)


def rms_scale(in_vals, gain_vec):
    vals_f32 = in_vals.astype(F32)
    inv_rms = lax.rsqrt(jnp.mean(vals_f32 * vals_f32, axis=-1, keepdims=True) + RMS_EPS)
    return (vals_f32 * inv_rms * gain_vec).astype(BF16)


def dot(a, b, dims):
    return lax.dot_general(a, b, dims, preferred_element_type=F32)


NN = (((1,), (0,)), ((), ()))


def pack_body(o_ref, q_ref, down_ref, tail_ref, out_ref):
    low = low_lanes()
    start, width = o_ref.shape[1] // LANES, q_ref.shape[1] // LANES
    out_ref[:, lane(0, start)] = o_ref[...]
    for j in range(0, width, 3):
        one, two, three = (q_ref[:, lane(j + k)].astype(F32) for k in range(3))
        out_ref[:, lane(start + j)] = one.astype(BF16)
        out_ref[:, lane(start + j + 1)] = jnp.where(low, rotate(two, ROPE_DIM), rotate(three, ROPE_DIM)).astype(BF16)
        out_ref[:, lane(start + j + 2)] = jnp.where(low, two, three).astype(BF16)
    out_ref[:, lane(start + width, down_ref.shape[1] // LANES)] = down_ref[...]
    out_ref[:, lane(out_ref.shape[1] // LANES - 1)] = tail_ref[...]


def pack_weights(w_out, w_query, w_kv_down, gains):
    rows, width = w_query.shape
    cut = w_kv_down.shape[1] // LANES * LANES
    tail = jnp.concatenate([w_kv_down[:, cut:]] + [jnp.pad(g, (0, rows - g.shape[0]))[:, None] for g in gains], axis=1)
    tail = jnp.pad(tail, ((0, 0), (0, LANES - tail.shape[1])))
    return pl.pallas_call(pack_body, out_shape=struct((rows, w_out.shape[1] + width + cut + LANES), BF16),
                          name="pack_weights")(w_out, w_query, w_kv_down[:, :cut], tail)


def unpack_body(g_ref, q_ref, down_ref):
    low = low_lanes()
    width = q_ref.shape[1] // LANES
    for j in range(0, width, 3):
        plain, rot = rotate(g_ref[:, lane(j + 1)], ROPE_DIM), g_ref[:, lane(j + 2)]
        q_ref[:, lane(j)] = g_ref[:, lane(j)]
        q_ref[:, lane(j + 1)] = jnp.where(low, rot, plain)
        q_ref[:, lane(j + 2)] = jnp.where(low, plain, rot)
    down_ref[...] = g_ref[:, q_ref.shape[1]:q_ref.shape[1] + down_ref.shape[1]]


def unpack_grads(g_x, q_width, down_width):
    rows = g_x.shape[0]
    return pl.pallas_call(unpack_body, out_shape=[struct((rows, q_width), F32), struct((rows, down_width), F32)], name="unpack_grads")(g_x)


def share_body(n_dev, x_ref, out_ref, send_sems, recv_sems):
    place = lax.axis_index('fsdp')
    for m in range(n_dev):
        @pl.when(place == m)
        def _():
            copies = [pltpu.make_async_remote_copy(x_ref, out_ref.at[m], send_sems.at[d], recv_sems.at[m], device_id={'fsdp': d}, device_id_type=pl.DeviceIdType.MESH)
                      for d in range(n_dev) if d != m]
            for copy in copies:
                copy.start()
            out_ref[m] = x_ref[...]
            for copy in copies:
                copy.wait_send()
            for s in range(n_dev):
                if s != m:
                    pltpu.make_async_remote_copy(x_ref, out_ref.at[s], send_sems.at[s], recv_sems.at[s], device_id={'fsdp': s}, device_id_type=pl.DeviceIdType.MESH).wait_recv()


def share(x, n_dev):
    vmem = pl.BlockSpec(memory_space=pltpu.VMEM)
    wide = pltpu.SemaphoreType.DMA((n_dev,))
    return pl.pallas_call(functools.partial(share_body, n_dev), out_shape=struct((n_dev,) + x.shape, x.dtype), in_specs=[vmem], out_specs=vmem,
                          scratch_shapes=[wide, wide], compiler_params=pltpu.CompilerParams(has_side_effects=True), name="share")(x)


def solution(mesh):
    n_dev = mesh.shape['fsdp']
    tok_spec = P(('dp', 'fsdp'), None)
    seq_spec = P(('dp', 'fsdp'), None, None)
    part_vec = P(('dp', 'fsdp'))
    vec_spec = P('fsdp')
    mat_spec = P('fsdp', None)

    def step(tok_ids, grad_out, emb_table, norm_gain, w_query, w_kv_down, kv_gain, w_kv_up, w_out):
        seq_count, seq_len = tok_ids.shape
        vocab_dev, d_model = emb_table.shape
        tok = seq_count * seq_len
        half = tok // HALVES
        per_half = seq_count // HALVES
        me = lax.axis_index('fsdp')
        gather = lambda piece: lax.all_gather(piece, 'fsdp', tiled=True)
        scatter = lambda full: lax.psum_scatter(full, 'fsdp', scatter_dimension=0, tiled=True)
        tie = lax.optimization_barrier
        rows_dev, q_width = w_query.shape
        rank_dev, = kv_gain.shape
        kv_rank = rank_dev * n_dev
        pe_at = q_width + kv_rank
        pad_at = pe_at + ROPE_DIM
        dy = grad_out.reshape(tok, d_model)
        w_ox = gather(pack_weights(w_out, w_query, w_kv_down, (norm_gain, kv_gain)))

        base, extra = [-(-round(half * share) // CHUNK) * CHUNK for share in (0.09, 0.31)]
        n_slots = n_dev * base + extra
        uniq, rank = unique_rows(tok_ids.reshape(HALVES, half))
        all_uniq = share(uniq.reshape(-1, LANES), n_dev).reshape(n_dev, HALVES, half)
        below = lambda lists, edges: jnp.sum(lists[..., None, :] < edges[:, None], axis=-1, dtype=jnp.int32)
        starts = below(all_uniq, jnp.arange(n_dev + 1, dtype=jnp.int32) * vocab_dev)
        counts = starts[..., 1:] - starts[..., :-1]
        fits = jnp.all(counts <= jnp.asarray([base + extra] + [base] * (n_dev - 1), jnp.int32))
        lists = jnp.swapaxes(all_uniq, 0, 1).reshape(HALVES * n_dev, half) - me * vocab_dev
        edges = below(lists, jnp.arange(vocab_dev // TABLE_BLOCK + 1, dtype=jnp.int32) * TABLE_BLOCK)
        my_starts, named = (lax.dynamic_index_in_dim(v, me, keepdims=False) for v in (starts[..., :-1], counts))
        place = jnp.arange(half, dtype=jnp.int32)
        begun = place[:, None] >= my_starts[:, None, 1:]
        slot = place + jnp.sum(jnp.where(begun, base - named[:, None, :-1], 0), axis=-1)
        slot = jnp.where((place >= base) & ~begun[..., 0], place + (n_dev - 1) * base, slot)
        slot = jnp.where(fits, slot, place)
        slots = jnp.arange(n_dev, dtype=jnp.int32) * half
        (rank_a, rank_b), (slot_a, slot_b) = rank, slot

        base_a, base_b, *extras = pick_rows(emb_table, lists, edges, n_dev, base, extra)
        extras_a, extras_b = extras[:n_dev], extras[n_dev:]

        def fetch_any(h):
            mine = slice(h * n_dev, (h + 1) * n_dev)
            far, = pick_rows(emb_table, lists[mine], edges[mine], n_dev, half, 0)
            far, prod = exchange([far], half, 0, n_dev, lhs=dy, rhs=w_ox)
            return move_rows(far, named[h], slots, my_starts[h], n_slots), prod

        recv, d_mix = lax.cond(fits, lambda: exchange([base_a] + extras_a, base, extra, n_dev, lhs=dy, rhs=w_ox), lambda: fetch_any(0))
        recv, w_ox, w_kv_up, base_b, extras_b = tie((recv, w_ox, w_kv_up, base_b, extras_b))
        w_o, w_x = w_ox[:, :d_model], w_ox[:, d_model:]
        w_up = gather(w_kv_up)
        pieces = fetch_beside(base_b, extras_b)
        gain_vec = w_x[:, pad_at].astype(F32)
        kv_gain_vec = w_x[:, pad_at + 1].reshape(n_dev, rows_dev)[:, :rank_dev].reshape(kv_rank).astype(F32)

        def compute(h, x):
            qx = dot(x, w_x, NN).astype(BF16)
            latent = rms_scale(qx[:, q_width:pe_at], kv_gain_vec)
            kv = dot(latent, w_up, NN).astype(BF16)
            return (qx, latent) + tuple(attend(qx, kv, d_mix, h * per_half, per_half, pe_at // LANES))

        def descend(qx, d_qx, d_kv, d_pe, kv_note):
            d_latent = dot(d_kv, w_up, COL_DIMS).astype(BF16)
            d_qx, d_kv_gain = latent_back(d_latent, qx, d_pe, kv_gain_vec, d_qx, q_width)
            return d_qx, kv_note + jnp.pad(d_kv_gain.reshape(n_dev, rank_dev), ((0, 0), (0, LANES - rank_dev)))

        h0_a, x_a = spread_rows([(recv, 0, None)], rank_a, slot_a, gain_vec, n_slots)
        qx_a, latent_a, mix_a, d_qx_a, d_kv_a, d_pe_a = compute(0, x_a)
        no_note = jnp.zeros((n_dev, LANES), F32)
        d_qx_a, kv_note = descend(qx_a, d_qx_a, d_kv_a, d_pe_a, no_note)
        d_x = dot(d_qx_a, w_x, COL_DIMS).astype(BF16)
        *merged_a, note_a = merge_rows(d_x, h0_a, dy, 0, gain_vec, no_note, rank_a, slot_a, n_dev * base, extra)
        back_a = bring_beside(*merged_a, n_dev)

        pieces, note_a = tie((pieces, note_a))
        h0_b, x_b = lax.cond(
            fits, lambda v: spread_rows([(v[0], 0, None)] + [(p, n_dev * base, d) for d, p in enumerate(v[1:])], rank_b, slot_b, gain_vec, n_slots),
            lambda v: spread_rows([(fetch_any(1)[0], 0, None)], rank_b, slot_b, gain_vec, n_slots), pieces)
        qx_b, latent_b, mix_b, d_qx_b, d_kv_b, d_pe_b = compute(1, x_b)
        got_a, extra_a, via = back_a
        via, d_kv_b = tie((via, d_kv_b))
        extra_a = extra_a + [lax.ppermute(via, 'fsdp', [(n_dev // 2 - 1, 0)])]
        d_w_o = weight_grad(mix_a, mix_b, dy, more=w_up.size // d_model)
        d_w_o = weight_grad_beside(d_w_o, d_model, latent_a, latent_b, d_kv_a, d_kv_b, n_dev)
        d_kv_b, d_w_o = tie((d_kv_b, d_w_o))
        d_qx_b, kv_note = descend(qx_b, d_qx_b, d_kv_b, d_pe_b, kv_note)
        d_x = dot(d_qx_b, w_x, COL_DIMS).astype(BF16)
        d_w_x = weight_grad(x_a, x_b, d_qx_a, d_qx_b)
        *merged_b, note_b = merge_rows(d_x, h0_b, dy, half, gain_vec, kv_note, rank_b, slot_b, n_dev * base, extra)

        g_o = scatter(d_w_o)
        merged_b, note, d_w_x = tie((merged_b, note_a + note_b, d_w_x))

        def bring_any(h, merged, note):
            far = move_rows(jnp.concatenate(merged, axis=0), named[h], my_starts[h], slots, n_dev * half)
            return exchange([far], half, 0, n_dev, note=note)

        room = base + extra
        back_b, note = lax.cond(fits, lambda v, n: exchange(v, base, extra, n_dev, note=n),
                                lambda v, n: (fresh((n_dev * room, d_model // LANES, LANES), F32), bring_any(1, v, n)[1]), merged_b, note)
        back_b, d_w_x, h0_b, mix_b = tie((back_b, d_w_x, h0_b, mix_b))
        g_x = scatter(d_w_x)
        out = jnp.concatenate([(h0.astype(F32) + dot(mix, w_o, NN)).astype(BF16) for h0, mix in ((h0_a, mix_a), (h0_b, mix_b))], axis=0)
        grad_table = lax.cond(
            fits, lambda: add_rows([(got_a, base, base, extra_a), (back_b, room, room, [])], lists, edges, n_dev, vocab_dev),
            lambda: add_rows([(bring_any(h, v, note)[0], half, half, []) for h, v in enumerate((merged_a, merged_b))], lists, edges, n_dev, vocab_dev))
        g_up = jnp.swapaxes(g_o[:, d_model:].reshape(-1, rank_dev, g_o.shape[1] - d_model), 0, 1).reshape(w_kv_up.shape)
        g_query, g_down = unpack_grads(g_x, q_width, pad_at - q_width)
        g_gain = jnp.sum(note, axis=0)
        gain_rows = rows_dev // LANES
        return (out.reshape(seq_count, seq_len, d_model), grad_table, g_gain[:gain_rows].reshape(rows_dev), g_query,
                g_down, g_gain[gain_rows, :rank_dev], g_up, g_o[:, :d_model])

    return jax.shard_map(step, mesh=mesh, in_specs=(tok_spec, seq_spec, mat_spec, vec_spec, mat_spec, mat_spec, vec_spec, mat_spec, mat_spec), out_specs=(seq_spec, tok_spec, part_vec, tok_spec, tok_spec, part_vec, tok_spec, tok_spec), check_vma=False)
```

time: 1160 us -> 1320 us (1.14)
  waiting for transfers between devices: 123 us -> 311 us
  matrix products: 243 us -> 174 us
  starting transfers between devices: 0.71 us -> 42.9 us
  local copies, waits for them, and re-layouts: 20.4 us -> 34.8 us
    ppermute x0 -> x15, waiting for transfers between devices: none -> 288 us  [the longest x6 232 us: bring_beside(): lax.ppermute(extra, 'fsdp', [(s, 0)])]
    reduce_scatter x3 -> x2, waiting for transfers between devices: 122 us -> 0.03 us  [step(): lax.psum_scatter(full, 'fsdp', scatter_dimension=0, tiled=True)]
    dot_general x8 -> x10, matrix products: 243 us -> 174 us  [dot(): return lax.dot_general(a, b, dims, preferred_element_type=F32)]
    ppermute x0 -> x15, starting transfers between devices: none -> 35.5 us  [the longest x7 24.2 us: fetch_beside(): lax.ppermute(v, 'fsdp', [(0, d)])]
    all_gather x3 -> x2, waiting for transfers between devices: 0.06 us -> 23 us  [step(): gather = lambda piece: lax.all_gather(piece, 'fsdp', tiled=True)]
    pallas_call x7 -> x11, Pallas kernels: 596 us -> 581 us  [the longest x2 274 us: exchange(): pl.pallas_call(functools.partial(exchange_body, base, extra, fetch, n_dev...]
    pallas_call x1 -> x2, Pallas kernels: 70.7 us -> 74.1 us  [attend(): pl.pallas_call(attn_body, grid=(seq_count, pairs), in_specs=[at(3 * LANES...]
    pallas_call x1 -> x2, Pallas kernels: 30.5 us -> 30.8 us  [merge_rows(): pl.pallas_call(merge_body, grid_spec=pltpu.PrefetchScalarGridSpec(num_sca...]
  transfers between devices with their start and end apart: 6 -> 21, of which waited for: 2 -> 4; matrix products, arithmetic and copies ran while one was open for 20% -> 15% of each run, Pallas kernels for 34% -> 46%
where the time goes in v3:
time: 1320 us; the launch traced here: 1310 us
  Pallas kernels  710 us (54%)
  waiting for transfers between devices  311 us (24%)
  matrix products  174 us (13%)
  starting transfers between devices  42.9 us (3%)
  local copies, waits for them, and re-layouts  34.8 us (3%)
  between operations  17.7 us (1%)
  other arithmetic  16 us (1%)
    pallas_call x2, Pallas kernels, exchange(): pl.pallas_call(functools.partial(exchange_body, base, extra, fetch, n_dev...  274 us
    ppermute x6, waiting for transfers between devices, bring_beside(): lax.ppermute(extra, 'fsdp', [(s, 0)])  232 us
    dot_general x10, matrix products, dot(): return lax.dot_general(a, b, dims, preferred_element_type=F32)  174 us
    pallas_call x1, Pallas kernels, add_rows(): pl.pallas_call(functools.partial(add_body, n_dev, n_tok, [(stride, base,...  108 us
    pallas_call x2, Pallas kernels, weight_grad(): pl.pallas_call(functools.partial(weight_body, len(rhs), steps), grid=(hei...  81.6 us
    pallas_call x2, Pallas kernels, attend(): pl.pallas_call(attn_body, grid=(seq_count, pairs), in_specs=[at(3 * LANES...  74.1 us
    pallas_call x1, Pallas kernels, pick_rows(): pl.pallas_call(functools.partial(pick_body, n_list, n_dev, n_tok, base, e...  63.4 us
    ppermute x1, waiting for transfers between devices, step(): extra_a = extra_a + [lax.ppermute(via, 'fsdp', [(n_dev // 2 - 1, 0)])]  56 us
  transfers between devices with their start and end apart: 21, of which 4 were waited for; matrix products, arithmetic and copies ran while one was open for 15% of the time, Pallas kernels for 46%

profile of v3, /device:TPU:0, one launch (start us, length us, event | category | flops | bytes accessed | tf_op | source)
XLA Modules:
  0.0 1309.1 jit_solution(3072309852360567883)
XLA Ops:
  19.8 10.8 unique_rows.1
  32.8 10.6 share.1
  48.5 63.4 %pick_rows.5 = (bf16[896,16,128]{2,1,0:T(8,128)(2,1)}, bf16[896,16,128]{2,1,0:T(8,128)(2,1)}, bf16[368,16,128]{2,1,0:T(8,128)(2,1)S(1)}, bf16[368,16,128]{2,1,0:...) custom-call(s32[18440]{0:T(1024)} %pad.34.rows_ref, ...), custom_call_target="tpu_custom_call" | custom-call | flops 60000000 | bytes 83886080 | tf_op jit(solution)/shard_map/pick_rows/pallas_call | solution.py:196
  111.9 23.0 %all-gather.3.cloned.1.call-done = bf16[2048,5760]{1,0:T(8,128)(2,1)} async-done(((bf16[256,5760]{1,0:T(8,128)(2,1)}), bf16[2048,5760]{1,0:T(8,128)(2,1)}) %all-gather.3.cloned.1.call-update) | async-done | bytes 23592976 | tf_op jit(solution)/shard_map/all_gather | solution.py:913
  134.9 86.3 %conditional.4 = (bf16[1264,16,128]{2,1,0:T(8,128)(2,1)}, bf16[2304,2048]{1,0:T(8,128)(2,1)}) conditional(s32[]{:T(128)} %convert_element_type.105, (s32[2,8]{1,0:T(2,128)S(1)}, s32[2,8]{1,0:T(2,128)S(1)}, s32[16,1152]{1,0:T(8,128)S(1)}, s32[16,21]{0,1:T(8,128)S(1)}, bf16[20480,2048]{1,0:T(8,128)(2,1)}, /*index=5*/bf16[2304,2048]{1,0:T(8,128)(2,1)}, ...), branch_computations={%region_5.6_spmd, %region_6.7_spmd} | conditional | flops 100060012544 | bytes 184112816 | solution.py:952
  134.9 86.2 %exchange.8 = (bf16[1264,16,128]{2,1,0:T(8,128)(2,1)}, bf16[4,368,16,128]{3,2,1,0:T(8,128)(2,1)}, bf16[2304,2048]{1,0:T(8,128)(2,1)}) custom-call(bf16[896,16,128]{2,1,0:T(8,128)(2,1)} %get-tuple-element.160.refs_0_, bf16[368,16,128]{2,1,0:T(8,128)(2,1)S(1)} %get-tuple-element.161.refs_1_, bf16[368,16,128]{2,1,0:T(8,128)(2,1)} %get-tuple-element.162.refs_2_, ...), custom_call_target="tpu_custom_call" | custom-call | flops 99999997952 | bytes 100000000 | tf_op jit(solution)/shard_map/cond/branch_1_fun/exchange/pallas_call | solution.py:680
  242.9 11.2 spread_rows.5
  256.2 23.2 %convolution_convert_fusion.3.q_ref.pe_ref.c_ref = bf16[1152,3712]{1,0:T(8,128)(2,1)S(1)} fusion(bf16[1152,2048]{1,0:T(8,128)(2,1)S(1)} %get-tuple-element.350.lhs_a_ref, bf16[2048,5760]{1,0:T(8,128)(2,1)} %all-gather.3.cloned.1.call-done), kind=kOutput, calls=%fused_computation.20 | convolution fusion | flops 17519689728 | bytes 28475392 | tf_op jit(solution)/shard_map/dot_general | solution.py:830
  283.3 10.2 convolution_convert_fusion.1.kv_ref
  293.6 37.0 %attention.2 = (bf16[1152,2048]{1,0:T(8,128)(2,1)S(1)}, bf16[1152,3712]{1,0:T(8,128)(2,1)S(1)}, bf16[1152,4096]{1,0:T(8,128)(2,1)}, bf16[1152,128]{1,0:T(8,128)(2,1)S(1)}) custom-call(bf16[1152,3712]{1,0:T(8,128)(2,1)} %copy-done.17, bf16[1152,3712]{1,0:T(8,128)(2,1)} %copy-done.17, bf16[1152,4096]{1,0:T(8,128)(2,1)} %convolution_convert_fusion.1.kv_ref, ...), custom_call_target="tpu_custom_call" | custom-call | flops 12000000000 | bytes 100000000 | tf_op jit(solution)/shard_map/attention/pallas_call | solution.py:342
  330.6 12.3 convolution_convert_fusion.5.w_ref
  358.0 23.9 %fusion.6.dx_ref = bf16[1152,2048]{1,0:T(8,128)(2,1)S(1)} fusion(bf16[1152,3712]{1,0:T(8,128)(2,1)} %get-tuple-element.357.refs_0_, bf16[2048,5760]{1,0:T(8,128)(2,1)} %all-gather.3.cloned.1.call-done), kind=kOutput, calls=%fused_computation.30 | convolution fusion | flops 17517772800 | bytes 28475392 | tf_op jit(solution)/shard_map/dot_general | solution.py:830
  382.1 14.8 %merge_rows.2 = (f32[896,16,128]{2,1,0:T(8,128)}, f32[368,16,128]{2,1,0:T(8,128)}, f32[8,8,128]{2,1,0:T(8,128)S(1)}) custom-call(s32[1152]{0:T(1024)S(1)} %get-tuple-element.552.rank_ref, s32[1152]{0:T(1024)S(1)} %get-tuple-element.532.slot_ref, bf16[1152,2048]{1,0:T(8,128)(2,1)S(1)} %fusion.6.dx_ref, bf16[1152,2048]{1,0:T(8,128)(2,1)S(1)} %bitcast.68, ...), custom_call_target="tpu_custom_call" | custom-call | flops 100000000 | bytes 23592960 | tf_op jit(solution)/shard_map/merge_rows/pallas_call | solution.py:464
  399.3 11.7 conditional.5
  399.3 11.7 spread_rows.4
  411.0 23.2 %convolution_convert_fusion.2.q_ref.pe_ref.c_ref = bf16[1152,3712]{1,0:T(8,128)(2,1)S(1)} fusion(bf16[1152,2048]{1,0:T(8,128)(2,1)} %get-tuple-element.378.lhs_b_ref, bf16[2048,5760]{1,0:T(8,128)(2,1)} %all-gather.3.cloned.1.call-done), kind=kOutput, calls=%fused_computation.19 | convolution fusion | flops 17519689728 | bytes 28475392 | tf_op jit(solution)/shard_map/dot_general | solution.py:830
  445.2 37.1 %attention.3 = (bf16[1152,2048]{1,0:T(8,128)(2,1)S(1)}, bf16[1152,3712]{1,0:T(8,128)(2,1)S(1)}, bf16[1152,4096]{1,0:T(8,128)(2,1)}, bf16[1152,128]{1,0:T(8,128)(2,1)S(1)}) custom-call(bf16[1152,3712]{1,0:T(8,128)(2,1)} %copy-done.16, bf16[1152,3712]{1,0:T(8,128)(2,1)} %copy-done.16, bf16[1152,4096]{1,0:T(8,128)(2,1)} %convolution_convert_fusion.kv_ref, ...), custom_call_target="tpu_custom_call" | custom-call | flops 12000000000 | bytes 100000000 | tf_op jit(solution)/shard_map/attention/pallas_call | solution.py:342
  488.7 30.0 %weight_grad.2 = f32[2048,3072]{1,0:T(8,128)} custom-call(bf16[1152,2048]{1,0:T(8,128)(2,1)} %copy-done.14, bf16[1152,2048]{1,0:T(8,128)(2,1)} %copy-done.15, bf16[2304,2048]{1,0:T(8,128)(2,1)} %bitcast.74), custom_call_target="tpu_custom_call" | custom-call | flops 19327352832 | bytes 16777216 | tf_op jit(solution)/shard_map/weight_grad/pallas_call | solution.py:753
  518.7 16.7 %weight_grad_beside.1 = f32[8,256,3072]{2,1,0:T(8,128)} custom-call(bf16[1152,512]{1,0:T(8,128)(2,1)S(1)} %copy-done.5, bf16[1152,512]{1,0:T(8,128)(2,1)S(1)} %fusion.19.lhs_b_ref, bf16[1152,4096]{1,0:T(8,128)(2,1)} %get-tuple-element.354.rhs_a_ref, bf16[1152,4096]{1,0:T(8,128)(2,1)} %get-tuple-element.382.rhs_b_ref, ...), custom_call_target="tpu_custom_call", output_to_operand_aliasing={{}: (4, {})} | custom-call | flops 9663676416 | bytes 10000000 | tf_op jit(solution)/shard_map/weight_grad_beside/pallas_call | solution.py:781
  536.8 12.4 convolution_convert_fusion.4.w_ref
  555.1 27.1 %fusion.9.dx_ref = bf16[1152,2048]{1,0:T(8,128)(2,1)S(1)} fusion(bf16[1152,3712]{1,0:T(8,128)(2,1)} %get-tuple-element.385.refs_1_, bf16[2048,5760]{1,0:T(8,128)(2,1)} %all-gather.3.cloned.1.call-done), kind=kOutput, calls=%fused_computation.31 | convolution fusion | flops 17517772800 | bytes 28475392 | tf_op jit(solution)/shard_map/dot_general | solution.py:830
  582.3 16.0 %merge_rows.3 = (f32[896,16,128]{2,1,0:T(8,128)}, f32[368,16,128]{2,1,0:T(8,128)}, f32[8,8,128]{2,1,0:T(8,128)S(1)}) custom-call(s32[1152]{0:T(1024)S(1)} %get-tuple-element.553.rank_ref, s32[1152]{0:T(1024)S(1)} %get-tuple-element.533.slot_ref, bf16[1152,2048]{1,0:T(8,128)(2,1)S(1)} %fusion.9.dx_ref, bf16[1152,2048]{1,0:T(8,128)(2,1)} %get-tuple-element.398.h0_ref, ...), custom_call_target="tpu_custom_call" | custom-call | flops 100000000 | bytes 23592960 | tf_op jit(solution)/shard_map/merge_rows/pallas_call | solution.py:464
  598.4 51.6 %weight_grad.3 = f32[2048,3712]{1,0:T(8,128)} custom-call(bf16[1152,2048]{1,0:T(8,128)(2,1)} %copy-done.8, bf16[1152,2048]{1,0:T(8,128)(2,1)} %get-tuple-element.378.lhs_b_ref, bf16[1152,3712]{1,0:T(8,128)(2,1)} %get-tuple-element.357.refs_0_, bf16[1152,3712]{1,0:T(8,128)(2,1)} %get-tuple-element.385.refs_1_), custom_call_target="tpu_custom_call" | custom-call | flops 35030827008 | bytes 30408704 | tf_op jit(solution)/shard_map/weight_grad/pallas_call | solution.py:753
  650.0 188.1 %conditional.6 = (f32[3840,16,128]{2,1,0:T(8,128)}, f32[8,8,128]{2,1,0:T(8,128)S(1)}) conditional(s32[]{:T(128)} %convert_element_type.105, (s32[2,8]{1,0:T(2,128)S(1)}, s32[2,8]{1,0:T(2,128)S(1)}, f32[896,16,128]{2,1,0:T(8,128)}, f32[368,16,128]{2,1,0:T(8,128)S(1)}, s32[8]{0:T(128)S(1)}, /*index=5*/f32[8,8,128]{2,1,0:T(8,128)S(1)}) %tuple.125, ...), branch_computations={%region_11.12_spmd, %region_12.13_spmd} | conditional | flops 100002586624 | bytes 120709520 | solution.py:1003
  650.2 187.9 %exchange.11 = (f32[3840,16,128]{2,1,0:T(8,128)}, f32[4,368,16,128]{3,2,1,0:T(8,128)}, f32[8,8,128]{2,1,0:T(8,128)S(1)}) custom-call(f32[896,16,128]{2,1,0:T(8,128)} %get-tuple-element.204.refs_0_, f32[368,16,128]{2,1,0:T(8,128)S(1)} %get-tuple-element.205.refs_1_, f32[8,8,128]{2,1,0:T(8,128)S(1)} %get-tuple-element.206.refs_2_), custom_call_target="tpu_custom_call" | custom-call | flops 99999997952 | bytes 100000000 | tf_op jit(solution)/shard_map/cond/branch_1_fun/exchange/pallas_call | solution.py:680
  848.6 18.8 %add_convert_fusion.1 = bf16[1152,2048]{1,0:T(8,128)(2,1)} fusion(bf16[1152,2048]{1,0:T(8,128)(2,1)} %copy-done.3, bf16[1152,2048]{1,0:T(8,128)(2,1)} %copy-done.14, bf16[2048,5760]{1,0:T(8,128)(2,1)} %all-gather.3.cloned.1.call-done), kind=kOutput, calls=%fused_computation.29 | convolution fusion | flops 9670754304 | bytes 22544384 | tf_op jit(solution)/shard_map/dot_general | solution.py:830
  868.5 170.2 %collective-permute-done.13 = f32[368,16,128]{2,1,0:T(8,128)} collective-permute-done((f32[368,16,128]{2,1,0:T(8,128)}, f32[368,16,128]{2,1,0:T(8,128)}, u32[]{:S(2)}, u32[]{:S(2)}) %collective-permute-start.13) | collective-permute-done | bytes 3014688 | tf_op jit(solution)/shard_map/ppermute | solution.py:699
  1039.9 61.8 %collective-permute-done.12 = f32[368,16,128]{2,1,0:T(8,128)} collective-permute-done((f32[368,16,128]{2,1,0:T(8,128)}, f32[368,16,128]{2,1,0:T(8,128)}, u32[]{:S(2)}, u32[]{:S(2)}) %collective-permute-start.12) | collective-permute-done | bytes 3014688 | tf_op jit(solution)/shard_map/ppermute | solution.py:699
  1103.0 15.3 %add_convert_fusion = bf16[1152,2048]{1,0:T(8,128)(2,1)S(1)} fusion(bf16[1152,2048]{1,0:T(8,128)(2,1)} %get-tuple-element.398.h0_ref, bf16[1152,2048]{1,0:T(8,128)(2,1)} %copy-done.15, bf16[2048,5760]{1,0:T(8,128)(2,1)} %all-gather.3.cloned.1.call-done), kind=kOutput, calls=%fused_computation.28 | convolution fusion | flops 9670754304 | bytes 22544384 | tf_op jit(solution)/shard_map/dot_general | solution.py:830
  1122.6 56.0 %collective-permute-done.14 = f32[368,16,128]{2,1,0:T(8,128)} collective-permute-done((f32[368,16,128]{2,1,0:T(8,128)}, f32[368,16,128]{2,1,0:T(8,128)}, u32[]{:S(2)}, u32[]{:S(2)}) %collective-permute-start.14) | collective-permute-done | bytes 3014688 | tf_op jit(solution)/shard_map/ppermute | solution.py:986
  1178.6 112.0 %conditional.7 = (bf16[20480,2048]{1,0:T(8,128)(2,1)}) conditional(s32[]{:T(128)} %convert_element_type.105, (s32[16,1152]{1,0:T(8,128)S(1)}, s32[16,21]{0,1:T(8,128)S(1)}, s32[2,8]{1,0:T(2,128)S(1)}, s32[2,8]{1,0:T(2,128)S(1)}, f32[896,16,128]{2,1,0:T(8,128)}, /*index=5*/f32[368,16,128]{2,1,0:T(8,128)}, s32[8]{0:T(128)S(1)}, ...), branch_computations={%region_13.14_spmd, %region_14.15_spmd} | conditional | flops 200065220608 | bytes 325752864 | solution.py:1008
  1183.0 107.6 %add_rows.3 = bf16[20480,2048]{1,0:T(8,128)(2,1)} custom-call(s32[18440]{0:T(1024)S(1)} %pad.26.rows_ref, s32[336]{0:T(512)S(1)} %reshape.169.edge_ref, f32[896,16,128]{2,1,0:T(8,128)} %get-tuple-element.224.refs_0_, f32[368,16,128]{2,1,0:T(8,128)} %get-tuple-element.225.refs_1_, f32[368,16,128]{2,1,0:T(8,128)} %get-tuple-element.226.refs_2_, ...), custom_call_target="tpu_custom_call" | custom-call | flops 60000000 | bytes 83886080 | tf_op jit(solution)/shard_map/cond/branch_1_fun/add_rows/pallas_call | solution.py:570
  (247 shorter events, 118.5 us)
Async XLA Ops:
  9.4 125.5 %all-gather.3.cloned.1.call-start = ((), (), s32[]{:S(2)}) async-start(), calls=%async_computation.4 | async-start | bytes 26542080 | tf_op jit(solution)/shard_map/all_gather | solution.py:913
  18.3 265.0 %all-gather.5.cloned.1.call-start = ((), (), s32[]{:S(2)}) async-start(), calls=%async_computation.5 | async-start | bytes 4718592 | tf_op jit(solution)/shard_map/all_gather | solution.py:913
  18.4 116.5 %copy-start.40 = (s32[8]{0:T(128)}, s32[8]{0:T(128)S(1)}, u32[]{:S(2)}) copy-start(s32[8]{0:T(128)S(1)} %iota_multiply_fusion) | copy-start | bytes 100
  47.0 87.9 %copy-start.20 = (s32[2,8,1152]{2,1,0:T(8,128)}, s32[2,8,1152]{2,1,0:T(8,128)S(1)}, u32[]{:S(2)}) copy-start(s32[2,8,1152]{2,1,0:T(8,128)S(1)} %copy.88) | copy-start | bytes 221188
  47.5 87.4 %copy-start.26 = (s32[16,21]{0,1:T(8,128)}, s32[16,21]{0,1:T(8,128)S(1)}, u32[]{:S(2)}) copy-start(s32[16,21]{0,1:T(8,128)S(1)} %convert_reduce_fusion) | copy-start | bytes 4036
  48.5 172.8 %copy-start.34 = (s32[2,8]{1,0:T(2,128)}, s32[2,8]{1,0:T(2,128)S(1)}, u32[]{:S(2)}) copy-start(s32[2,8]{1,0:T(2,128)S(1)} %get-tuple-element.555) | copy-start | bytes 196
  48.5 172.9 %copy-start.30 = (s32[2,8]{1,0:T(2,128)}, s32[2,8]{1,0:T(2,128)S(1)}, u32[]{:S(2)}) copy-start(s32[2,8]{1,0:T(2,128)S(1)} %get-tuple-element.554) | copy-start | bytes 196
  134.9 87.6 %copy-start.29 = (s32[2304]{0:T(1024)S(1)}, s32[2304]{0:T(1024)}, u32[]{:S(2)}) copy-start(s32[2304]{0:T(1024)} %get-tuple-element.325) | copy-start | bytes 27652
  224.6 172.3 %all-to-all-start = ((bf16[896,16,128]{2,1,0:T(8,128)(2,1)}), bf16[896,16,128]{2,1,0:T(8,128)(2,1)}, u32[]{:S(2)}, u32[]{:S(2)}) async-start(bf16[896,16,128]{2,1,0:T(8,128)(2,1)} %get-tuple-element.359), calls=%async_computation | async-start | bytes 7340032 | tf_op jit(solution)/shard_map/all_to_all | solution.py:690
  227.9 1062.7 %reduce-scatter.5.cloned.1.call-start = ((), (), s32[]{:S(2)}) async-start(), calls=%async_computation.7 | async-start | bytes 28311552 | tf_op jit(solution)/shard_map/reduce_scatter | solution.py:914
  228.0 119.2 %collective-permute-start.1 = (bf16[368,16,128]{2,1,0:T(8,128)(2,1)}, bf16[368,16,128]{2,1,0:T(8,128)(2,1)S(1)}, u32[]{:S(2)}, u32[]{:S(2)}) collective-permute-start(bf16[368,16,128]{2,1,0:T(8,128)(2,1)} %get-tuple-element.361), channel_id=1, source_target_pairs={{0,1}} | collective-permute-start | bytes 4521992 | tf_op jit(solution)/shard_map/ppermute | solution.py:691
  230.3 125.2 %collective-permute-start.2 = (bf16[368,16,128]{2,1,0:T(8,128)(2,1)}, bf16[368,16,128]{2,1,0:T(8,128)(2,1)}, u32[]{:S(2)}, u32[]{:S(2)}) collective-permute-start(bf16[368,16,128]{2,1,0:T(8,128)(2,1)} %get-tuple-element.362), channel_id=1, source_target_pairs={{0,2}} | collective-permute-start | bytes 4521992 | tf_op jit(solution)/shard_map/ppermute | solution.py:691
  234.1 162.7 %collective-permute-start.3 = (bf16[368,16,128]{2,1,0:T(8,128)(2,1)}, bf16[368,16,128]{2,1,0:T(8,128)(2,1)}, u32[]{:S(2)}, u32[]{:S(2)}) collective-permute-start(bf16[368,16,128]{2,1,0:T(8,128)(2,1)} %get-tuple-element.363), channel_id=1, source_target_pairs={{0,3}} | collective-permute-start | bytes 4521992 | tf_op jit(solution)/shard_map/ppermute | solution.py:691
  236.5 160.3 %collective-permute-start.4 = (bf16[368,16,128]{2,1,0:T(8,128)(2,1)}, bf16[368,16,128]{2,1,0:T(8,128)(2,1)}, u32[]{:S(2)}, u32[]{:S(2)}) collective-permute-start(bf16[368,16,128]{2,1,0:T(8,128)(2,1)} %get-tuple-element.364), channel_id=1, source_target_pairs={{0,4}} | collective-permute-start | bytes 4521992 | tf_op jit(solution)/shard_map/ppermute | solution.py:691
  239.0 157.9 %collective-permute-start.5 = (bf16[368,16,128]{2,1,0:T(8,128)(2,1)}, bf16[368,16,128]{2,1,0:T(8,128)(2,1)}, u32[]{:S(2)}, u32[]{:S(2)}) collective-permute-start(bf16[368,16,128]{2,1,0:T(8,128)(2,1)} %get-tuple-element.365), channel_id=1, source_target_pairs={{0,5}} | collective-permute-start | bytes 4521992 | tf_op jit(solution)/shard_map/ppermute | solution.py:691
  347.2 49.6 %collective-permute-start.6 = (bf16[368,16,128]{2,1,0:T(8,128)(2,1)}, bf16[368,16,128]{2,1,0:T(8,128)(2,1)}, u32[]{:S(2)}, u32[]{:S(2)}) collective-permute-start(bf16[368,16,128]{2,1,0:T(8,128)(2,1)} %get-tuple-element.366), channel_id=1, source_target_pairs={{0,6}} | collective-permute-start | bytes 4521992 | tf_op jit(solution)/shard_map/ppermute | solution.py:691
  355.5 41.3 %collective-permute-start.7 = (bf16[368,16,128]{2,1,0:T(8,128)(2,1)}, bf16[368,16,128]{2,1,0:T(8,128)(2,1)}, u32[]{:S(2)}, u32[]{:S(2)}) collective-permute-start(bf16[368,16,128]{2,1,0:T(8,128)(2,1)} %get-tuple-element.367), channel_id=1, source_target_pairs={{0,7}} | collective-permute-start | bytes 4521992 | tf_op jit(solution)/shard_map/ppermute | solution.py:691
  396.9 121.8 %collective-permute-start = (f32[368,16,128]{2,1,0:T(8,128)}, f32[368,16,128]{2,1,0:T(8,128)}, u32[]{:S(2)}, u32[]{:S(2)}) collective-permute-start(f32[368,16,128]{2,1,0:T(8,128)} %get-tuple-element.358), channel_id=1, source_target_pairs={{7,3}} | collective-permute-start | bytes 9043976 | tf_op jit(solution)/shard_map/ppermute | solution.py:698
  535.4 759.3 %reduce-scatter.3.cloned.1.call-start = ((), (), s32[]{:S(2)}) async-start(), calls=%async_computation.6 | async-start | bytes 34209792 | tf_op jit(solution)/shard_map/reduce_scatter | solution.py:914
  838.2 340.4 %all-to-all-start.1 = ((f32[896,16,128]{2,1,0:T(8,128)}), f32[896,16,128]{2,1,0:T(8,128)}, u32[]{:S(2)}, u32[]{:S(2)}) async-start(f32[896,16,128]{2,1,0:T(8,128)} %get-tuple-element.400), calls=%async_computation.1 | async-start | bytes 14680064 | tf_op jit(solution)/shard_map/all_to_all | solution.py:696
  842.1 196.6 %collective-permute-start.13 = (f32[368,16,128]{2,1,0:T(8,128)}, f32[368,16,128]{2,1,0:T(8,128)}, u32[]{:S(2)}, u32[]{:S(2)}) collective-permute-start(f32[368,16,128]{2,1,0:T(8,128)} %get-tuple-element.358), channel_id=1, source_target_pairs={{6,0}} | collective-permute-start | bytes 9043976 | tf_op jit(solution)/shard_map/ppermute | solution.py:699
  843.4 258.3 %collective-permute-start.12 = (f32[368,16,128]{2,1,0:T(8,128)}, f32[368,16,128]{2,1,0:T(8,128)}, u32[]{:S(2)}, u32[]{:S(2)}) collective-permute-start(f32[368,16,128]{2,1,0:T(8,128)} %get-tuple-element.358), channel_id=1, source_target_pairs={{5,0}} | collective-permute-start | bytes 9043976 | tf_op jit(solution)/shard_map/ppermute | solution.py:699
  844.7 277.9 %collective-permute-start.11 = (f32[368,16,128]{2,1,0:T(8,128)}, f32[368,16,128]{2,1,0:T(8,128)}, u32[]{:S(2)}, u32[]{:S(2)}) collective-permute-start(f32[368,16,128]{2,1,0:T(8,128)} %get-tuple-element.358), channel_id=1, source_target_pairs={{4,0}} | collective-permute-start | bytes 9043976 | tf_op jit(solution)/shard_map/ppermute | solution.py:699
  846.0 276.6 %collective-permute-start.10 = (f32[368,16,128]{2,1,0:T(8,128)}, f32[368,16,128]{2,1,0:T(8,128)}, u32[]{:S(2)}, u32[]{:S(2)}) collective-permute-start(f32[368,16,128]{2,1,0:T(8,128)} %get-tuple-element.358), channel_id=1, source_target_pairs={{3,0}} | collective-permute-start | bytes 9043976 | tf_op jit(solution)/shard_map/ppermute | solution.py:699
  847.3 275.3 %collective-permute-start.9 = (f32[368,16,128]{2,1,0:T(8,128)}, f32[368,16,128]{2,1,0:T(8,128)}, u32[]{:S(2)}, u32[]{:S(2)}) collective-permute-start(f32[368,16,128]{2,1,0:T(8,128)} %get-tuple-element.358), channel_id=1, source_target_pairs={{2,0}} | collective-permute-start | bytes 9043976 | tf_op jit(solution)/shard_map/ppermute | solution.py:699
  867.9 250.4 %slice-start.8 = ((s8[4718592]{0:T(1024)(128)(4,1)}), s8[4194304]{0:T(1024)(128)(4,1)S(1)}, s32[]{:S(2)}) async-start(s8[4718592]{0:T(1024)(128)(4,1)} %bitcast.82), calls=%async_computation.18 | async-start | bytes 8388608
  868.5 249.8 %slice-start.9 = ((s8[4718592]{0:T(1024)(128)(4,1)}), s8[524288]{0:T(1024)(128)(4,1)S(1)}, s32[]{:S(2)}) async-start(s8[4718592]{0:T(1024)(128)(4,1)} %bitcast.82), calls=%async_computation.19 | async-start | bytes 1048576
  1038.7 83.9 %collective-permute-start.8 = (f32[368,16,128]{2,1,0:T(8,128)}, f32[368,16,128]{2,1,0:T(8,128)}, u32[]{:S(2)}, u32[]{:S(2)}) collective-permute-start(f32[368,16,128]{2,1,0:T(8,128)} %get-tuple-element.358), channel_id=1, source_target_pairs={{1,0}} | collective-permute-start | bytes 9043976 | tf_op jit(solution)/shard_map/ppermute | solution.py:699
  1101.7 76.9 %collective-permute-start.14 = (f32[368,16,128]{2,1,0:T(8,128)}, f32[368,16,128]{2,1,0:T(8,128)}, u32[]{:S(2)}, u32[]{:S(2)}) collective-permute-start(f32[368,16,128]{2,1,0:T(8,128)} %collective-permute-done), channel_id=1, source_target_pairs={{3,0}} | collective-permute-start | bytes 9043976 | tf_op jit(solution)/shard_map/ppermute | solution.py:986
  1118.3 60.3 %copy-start.22 = (s32[2,8,1152]{2,1,0:T(8,128)S(1)}, s32[2,8,1152]{2,1,0:T(8,128)}, u32[]{:S(2)}) copy-start(s32[2,8,1152]{2,1,0:T(8,128)} %copy-done.20) | copy-start | bytes 221188
  1118.3 60.3 %copy-start.28 = (s32[16,21]{0,1:T(8,128)S(1)}, s32[16,21]{0,1:T(8,128)}, u32[]{:S(2)}) copy-start(s32[16,21]{0,1:T(8,128)} %copy-done.26) | copy-start | bytes 4036
  1118.3 60.3 %copy-start.33 = (s32[2,8]{1,0:T(2,128)S(1)}, s32[2,8]{1,0:T(2,128)}, u32[]{:S(2)}) copy-start(s32[2,8]{1,0:T(2,128)} %copy-done.30) | copy-start | bytes 196
  (47 other events, 1038.2 us)
Sparse Core Ops, SparseCore 0:
  11.8 5.4 sort.11.cloned.1.call-done
  (1 shorter events, 0.0 us)
Sparse Core Ops, SparseCore 1:
  18.4 116.4 all-gather.2
  221.3 57.7 all-gather.4
  535.5 226.4 reduce-scatter.4
  838.3 329.6 reduce-scatter.2
